TPU v7x, 16 devices: a whole 2x2x2 slice. The times are simulated.
16 devices in a mesh: model: 2 (over z), data: 8 (over y, x, core).
Axes of the slice: x: 2, y: 2, z: 2, core: 2. Of those that a mesh axis runs over, the one named last changes fastest.
Arguments:
- x_in: bfloat16 [96, 512, 512], P('data')
- cot_out: bfloat16 [96, 512, 512], P('data')
- step_emb: bfloat16 [4, 512], replicated
- w_q: bfloat16 [512, 512], P(None, 'model')
- w_k: bfloat16 [512, 512], P(None, 'model')
- w_v: bfloat16 [512, 512], P(None, 'model')
- w_o: bfloat16 [512, 512], P('model')
- w_1: bfloat16 [512, 2048], P(None, 'model')
- w_2: bfloat16 [2048, 512], P('model')
Outputs:
- output 1: float32 [512, 512], P(None, 'model')
- output 2: float32 [512, 512], P(None, 'model')
- output 3: float32 [512, 512], P(None, 'model')
- output 4: float32 [512, 512], P('model')
- output 5: float32 [512, 2048], P(None, 'model')
- output 6: float32 [2048, 512], P('model')
- output 7: bfloat16 [96, 512, 512], P('data')
All inputs are finite; a program needn't handle non-finite values.
Results may differ from a plain program's by a relative error of at most 0.0174562.
Values are sent between devices in bfloat16 or wider.
A program may use at most 1 GiB of HBM per device.

v0:
```python
import jax
import jax.numpy as jnp
from jax import lax
from jax.sharding import PartitionSpec as P

HEAD_DIM = 64
EPS_NORM = 1e-6


def rms_norm(values):
    return values * lax.rsqrt(jnp.mean(values * values, axis=-1, keepdims=True) + EPS_NORM)


def split_heads(qkv):
    batch_size, seq_len, triple_width = qkv.shape
    stacked = qkv.reshape(batch_size, seq_len, 3, triple_width // (3 * HEAD_DIM), HEAD_DIM)
    return stacked[:, :, 0], stacked[:, :, 1], stacked[:, :, 2]


def attn_probs(q_head, k_head):
    scores = jnp.einsum('bqhe,bkhe->bhqk', q_head, k_head, preferred_element_type=jnp.float32)
    return jax.nn.softmax(scores * (HEAD_DIM ** -0.5), axis=-1)


def layer_forward(x_cur, step_vec, w_qkv, w_out, w_up, w_down, reduce_model):
    batch_size, seq_len = x_cur.shape[0], x_cur.shape[1]
    x_f = x_cur.astype(jnp.float32) + step_vec.astype(jnp.float32)
    u_in = rms_norm(x_f).astype(jnp.bfloat16)
    qkv = jnp.einsum('bsd,de->bse', u_in, w_qkv, preferred_element_type=jnp.float32).astype(jnp.bfloat16)
    q_head, k_head, v_head = split_heads(qkv)
    prob_mat = attn_probs(q_head, k_head).astype(jnp.bfloat16)
    context = jnp.einsum('bhqk,bkhe->bqhe', prob_mat, v_head, preferred_element_type=jnp.float32)
    context = context.astype(jnp.bfloat16).reshape(batch_size, seq_len, w_out.shape[0])
    attn_out = reduce_model(jnp.einsum('bse,ed->bsd', context, w_out, preferred_element_type=jnp.float32))
    h_mid = (x_f + attn_out).astype(jnp.bfloat16)
    m_in = rms_norm(h_mid.astype(jnp.float32)).astype(jnp.bfloat16)
    z_up = jnp.einsum('bsd,df->bsf', m_in, w_up, preferred_element_type=jnp.float32).astype(jnp.bfloat16)
    g_act = jax.nn.gelu(z_up.astype(jnp.float32)).astype(jnp.bfloat16)
    mlp_out = reduce_model(jnp.einsum('bsf,fd->bsd', g_act, w_down, preferred_element_type=jnp.float32))
    x_next = (h_mid.astype(jnp.float32) + mlp_out).astype(jnp.bfloat16)
    return x_next, (x_cur, u_in, qkv, context, h_mid, m_in, z_up, g_act)


def layer_backward(d_next, step_vec, saved_acts, w_qkv, w_out, w_up, w_down, reduce_model):
    x_cur, u_in, qkv, context, h_mid, m_in, z_up, g_act = saved_acts
    batch_size, seq_len = x_cur.shape[0], x_cur.shape[1]
    grad_down = jnp.einsum('bsf,bsd->fd', g_act, d_next, preferred_element_type=jnp.float32)
    d_act = jnp.einsum('bsd,fd->bsf', d_next, w_down, preferred_element_type=jnp.float32).astype(jnp.bfloat16)
    gelu_pull = jax.vjp(jax.nn.gelu, z_up.astype(jnp.float32))[1]
    d_up = gelu_pull(d_act.astype(jnp.float32))[0].astype(jnp.bfloat16)
    grad_up = jnp.einsum('bsd,bsf->df', m_in, d_up, preferred_element_type=jnp.float32)
    d_norm2 = reduce_model(jnp.einsum('bsf,df->bsd', d_up, w_up, preferred_element_type=jnp.float32)).astype(jnp.bfloat16)
    norm_pull = jax.vjp(rms_norm, h_mid.astype(jnp.float32))[1]
    d_mid = (d_next.astype(jnp.float32) + norm_pull(d_norm2.astype(jnp.float32))[0]).astype(jnp.bfloat16)
    grad_wo = jnp.einsum('bse,bsd->ed', context, d_mid, preferred_element_type=jnp.float32)
    head_shape = (batch_size, seq_len, w_out.shape[0] // HEAD_DIM, HEAD_DIM)
    d_context = jnp.einsum('bsd,ed->bse', d_mid, w_out, preferred_element_type=jnp.float32).astype(jnp.bfloat16).reshape(head_shape)
    q_head, k_head, v_head = split_heads(qkv)
    prob_f = attn_probs(q_head, k_head)
    d_prob = jnp.einsum('bqhe,bkhe->bhqk', d_context, v_head, preferred_element_type=jnp.float32).astype(jnp.bfloat16).astype(jnp.float32)
    d_value = jnp.einsum('bhqk,bqhe->bkhe', prob_f.astype(jnp.bfloat16), d_context, preferred_element_type=jnp.float32).astype(jnp.bfloat16)
    d_scores = (prob_f * (d_prob - jnp.sum(prob_f * d_prob, axis=-1, keepdims=True)) * (HEAD_DIM ** -0.5)).astype(jnp.bfloat16)
    d_query = jnp.einsum('bhqk,bkhe->bqhe', d_scores, k_head, preferred_element_type=jnp.float32).astype(jnp.bfloat16)
    d_key = jnp.einsum('bhqk,bqhe->bkhe', d_scores, q_head, preferred_element_type=jnp.float32).astype(jnp.bfloat16)
    d_qkv = jnp.stack([d_query, d_key, d_value], axis=2).reshape(batch_size, seq_len, w_qkv.shape[1])
    grad_qkv = jnp.einsum('bsd,bse->de', u_in, d_qkv, preferred_element_type=jnp.float32)
    d_norm1 = reduce_model(jnp.einsum('bse,de->bsd', d_qkv, w_qkv, preferred_element_type=jnp.float32)).astype(jnp.bfloat16)
    x_f = x_cur.astype(jnp.float32) + step_vec.astype(jnp.float32)
    norm_pull_x = jax.vjp(rms_norm, x_f)[1]
    d_prev = (d_mid.astype(jnp.float32) + norm_pull_x(d_norm1.astype(jnp.float32))[0]).astype(jnp.bfloat16)
    return d_prev, (grad_qkv, grad_wo, grad_up, grad_down)


def solution(mesh):
    spec_col = P(None, 'model')
    spec_row = P('model', None)
    spec_act = P('data', None, None)
    spec_rep = P(None, None)

    def sum_model(values):
        return lax.psum(values, 'model')

    def device_step(x_in, cot_out, step_emb, w_q, w_k, w_v, w_o, w_1, w_2):
        w_qkv = jnp.concatenate([w_q, w_k, w_v], axis=1)
        layer_count = step_emb.shape[0]
        x_cur = x_in
        saved_list = []
        for layer_idx in range(layer_count):
            x_cur, saved_acts = layer_forward(x_cur, step_emb[layer_idx], w_qkv, w_o, w_1, w_2, sum_model)
            saved_list.append(saved_acts)
        d_cur = cot_out
        totals = None
        for layer_idx in reversed(range(layer_count)):
            d_cur, layer_grads = layer_backward(d_cur, step_emb[layer_idx], saved_list[layer_idx], w_qkv, w_o, w_1, w_2, sum_model)
            layer_grads = lax.psum(layer_grads, 'data')
            if totals is None:
                totals = layer_grads
            else:
                totals = jax.tree.map(jnp.add, totals, layer_grads)
        grad_qkv, grad_wo, grad_up, grad_down = totals
        col_width = w_q.shape[1]
        return (grad_qkv[:, :col_width], grad_qkv[:, col_width:2 * col_width], grad_qkv[:, 2 * col_width:],
                grad_wo, grad_up, grad_down, d_cur)

    return jax.shard_map(device_step, mesh=mesh,
                         in_specs=(spec_act, spec_act, spec_rep, spec_col, spec_col, spec_col, spec_row, spec_col, spec_row),
                         out_specs=(spec_col, spec_col, spec_col, spec_row, spec_col, spec_row, spec_act),
                         check_vma=False)
```

profile of v0, /device:TPU:0, one launch (start us, length us, event | category | flops | bytes accessed | tf_op | source)
XLA Modules:
  0.0 6033.3 jit_solution(2569806353258303002)
XLA Ops:
  36.6 21.2 fusion.161
  57.9 50.3 fusion.275
  108.2 17.8 fusion.165
  134.1 287.0 %all-reduce.18.cloned.1.call-done = f32[12,512,512]{2,1,0:T(8,128)} async-done(((f32[12,512,512]{2,1,0:T(8,128)}), f32[12,512,512]{2,1,0:T(8,128)}) %all-reduce.18.cloned.1.call-update) | async-done | bytes 12582928 | tf_op jit(solution)/shard_map/psum | solution.py:81
  439.2 15.3 fusion.200
  454.6 284.2 %all-reduce.20.cloned.1.call-done = f32[12,512,512]{2,1,0:T(8,128)} async-done(((f32[12,512,512]{2,1,0:T(8,128)}), f32[12,512,512]{2,1,0:T(8,128)}) %all-reduce.20.cloned.1.call-update) | async-done | bytes 12582928 | tf_op jit(solution)/shard_map/psum | solution.py:81
  769.7 21.2 fusion.162
  791.0 50.4 fusion.276
  841.4 17.8 fusion.170
  867.2 284.1 %all-reduce.22.cloned.1.call-done = f32[12,512,512]{2,1,0:T(8,128)} async-done(((f32[12,512,512]{2,1,0:T(8,128)}), f32[12,512,512]{2,1,0:T(8,128)}) %all-reduce.22.cloned.1.call-update) | async-done | bytes 12582928 | tf_op jit(solution)/shard_map/psum | solution.py:81
  1169.4 15.3 fusion.198
  1184.8 284.1 %all-reduce.24.cloned.1.call-done = f32[12,512,512]{2,1,0:T(8,128)} async-done(((f32[12,512,512]{2,1,0:T(8,128)}), f32[12,512,512]{2,1,0:T(8,128)}) %all-reduce.24.cloned.1.call-update) | async-done | bytes 12582928 | tf_op jit(solution)/shard_map/psum | solution.py:81
  1487.0 12.7 copy.72
  1499.8 21.2 fusion.163
  1521.0 50.3 fusion.277
  1571.3 17.8 fusion.175
  1597.2 284.1 %all-reduce.26.cloned.1.call-done = f32[12,512,512]{2,1,0:T(8,128)} async-done(((f32[12,512,512]{2,1,0:T(8,128)}), f32[12,512,512]{2,1,0:T(8,128)}) %all-reduce.26.cloned.1.call-update) | async-done | bytes 12582928 | tf_op jit(solution)/shard_map/psum | solution.py:81
  1899.6 15.3 fusion.196
  1915.0 284.1 %all-reduce.28.cloned.1.call-done = f32[12,512,512]{2,1,0:T(8,128)} async-done(((f32[12,512,512]{2,1,0:T(8,128)}), f32[12,512,512]{2,1,0:T(8,128)}) %all-reduce.28.cloned.1.call-update) | async-done | bytes 12582928 | tf_op jit(solution)/shard_map/psum | solution.py:81
  2229.9 21.2 fusion.164
  2251.1 50.4 fusion.278
  2301.5 17.7 fusion.180
  2327.4 284.1 %all-reduce.30.cloned.1.call-done = f32[12,512,512]{2,1,0:T(8,128)} async-done(((f32[12,512,512]{2,1,0:T(8,128)}), f32[12,512,512]{2,1,0:T(8,128)}) %all-reduce.30.cloned.1.call-update) | async-done | bytes 12582928 | tf_op jit(solution)/shard_map/psum | solution.py:81
  2629.2 25.2 fusion.42
  2654.4 14.4 fusion.208
  2668.8 288.2 %all-reduce.33 = bf16[12,512,512]{2,1,0:T(8,128)(2,1)} all-reduce(f32[12,512,512]{2,1,0:T(8,128)} %fusion.208), channel_id=1, replica_groups=mesh['model'=2,'data'=8] {'model'}, use_global_device_ids=true, to_apply=%region_23.0 | all-reduce | flops 3145728 | bytes 18874368 | tf_op jit(solution)/shard_map/psum | solution.py:81
  2977.2 19.9 convert_bitcast_fusion.9
  2997.2 13.7 convolution_convert_fusion.3
  3010.8 50.0 convert_bitcast_fusion.11
  3060.8 50.5 convert_bitcast_fusion.10
  3140.3 286.4 %all-reduce.34 = bf16[12,512,512]{2,1,0:T(8,128)(2,1)} all-reduce(f32[12,512,512]{2,1,0:T(8,128)} %fusion.270), channel_id=1, replica_groups=mesh['model'=2,'data'=8] {'model'}, use_global_device_ids=true, to_apply=%region_27.0 | all-reduce | flops 3145728 | bytes 18874368 | tf_op jit(solution)/shard_map/psum | solution.py:81
  3441.2 16.6 fusion.258
  3457.8 25.8 fusion.45
  3483.7 12.9 fusion.145
  3506.2 285.3 %all-reduce.35 = bf16[12,512,512]{2,1,0:T(8,128)(2,1)} all-reduce(f32[12,512,512]{2,1,0:T(8,128)} %fusion.206), channel_id=1, replica_groups=mesh['model'=2,'data'=8] {'model'}, use_global_device_ids=true, to_apply=%region_29.0 | all-reduce | flops 3145728 | bytes 18874368 | tf_op jit(solution)/shard_map/psum | solution.py:81
  3812.3 19.9 convert_bitcast_fusion.6
  3832.3 13.6 convolution_convert_fusion.2
  3845.9 50.2 convert_bitcast_fusion.8
  3896.0 50.8 convert_bitcast_fusion.7
  3964.0 12.8 fusion.159
  3985.2 284.1 %all-reduce.36 = bf16[12,512,512]{2,1,0:T(8,128)(2,1)} all-reduce(f32[12,512,512]{2,1,0:T(8,128)} %fusion.269), channel_id=1, replica_groups=mesh['model'=2,'data'=8] {'model'}, use_global_device_ids=true, to_apply=%region_33.0 | all-reduce | flops 3145728 | bytes 18874368 | tf_op jit(solution)/shard_map/psum | solution.py:81
  4283.4 16.7 fusion.261
  4300.2 25.9 fusion.48
  4326.1 12.9 fusion.148
  4348.5 283.4 %all-reduce.37 = bf16[12,512,512]{2,1,0:T(8,128)(2,1)} all-reduce(f32[12,512,512]{2,1,0:T(8,128)} %fusion.204), channel_id=1, replica_groups=mesh['model'=2,'data'=8] {'model'}, use_global_device_ids=true, to_apply=%region_35.0 | all-reduce | flops 3145728 | bytes 18874368 | tf_op jit(solution)/shard_map/psum | solution.py:81
  4652.7 20.0 convert_bitcast_fusion.3
  4672.7 13.6 convolution_convert_fusion.1
  4686.3 50.0 convert_bitcast_fusion.5
  4736.3 50.7 convert_bitcast_fusion.4
  4804.1 12.8 fusion.158
  4825.2 282.7 %all-reduce.38 = bf16[12,512,512]{2,1,0:T(8,128)(2,1)} all-reduce(f32[12,512,512]{2,1,0:T(8,128)} %fusion.268), channel_id=1, replica_groups=mesh['model'=2,'data'=8] {'model'}, use_global_device_ids=true, to_apply=%region_39.0 | all-reduce | flops 3145728 | bytes 18874368 | tf_op jit(solution)/shard_map/psum | solution.py:81
  5122.0 16.7 fusion.264
  5138.7 25.6 fusion.51
  5164.4 12.9 fusion.151
  5186.8 282.0 %all-reduce.39 = bf16[12,512,512]{2,1,0:T(8,128)(2,1)} all-reduce(f32[12,512,512]{2,1,0:T(8,128)} %fusion.202), channel_id=1, replica_groups=mesh['model'=2,'data'=8] {'model'}, use_global_device_ids=true, to_apply=%region_41.0 | all-reduce | flops 3145728 | bytes 18874368 | tf_op jit(solution)/shard_map/psum | solution.py:81
  5489.5 20.0 convert_bitcast_fusion
  5509.5 13.7 convolution_convert_fusion
  5523.2 50.1 convert_bitcast_fusion.2
  5573.2 50.5 convert_bitcast_fusion.1
  5641.0 12.8 fusion.157
  5673.5 16.9 bitcast_add_fusion
  5690.5 12.9 bitcast_add_fusion.3
  5703.4 14.2 bitcast_add_fusion.6
  5717.6 281.2 %all-reduce.40 = bf16[12,512,512]{2,1,0:T(8,128)(2,1)} all-reduce(f32[12,512,512]{2,1,0:T(8,128)} %fusion.267), channel_id=1, replica_groups=mesh['model'=2,'data'=8] {'model'}, use_global_device_ids=true, to_apply=%region_57.0 | all-reduce | flops 3145728 | bytes 18874368 | tf_op jit(solution)/shard_map/psum | solution.py:81
  (394 shorter events, 511.5 us)
Async XLA Ops:
  7.2 422.3 %copy-start = (bf16[512,1024]{1,0:T(8,128)(2,1)S(1)}, bf16[512,1024]{1,0:T(8,128)(2,1)}, u32[]{:S(2)}) copy-start(bf16[512,1024]{1,0:T(8,128)(2,1)} %param.16) | copy-start | bytes 3145732
  7.2 413.8 %all-reduce.18.cloned.1.call-start = ((), (), s32[]{:S(2)}) async-start(), calls=%async_computation | async-start | bytes 25165824 | tf_op jit(solution)/shard_map/psum | solution.py:81
  8.7 412.4 %copy-start.85 = (f32[1,512]{1,0:T(1,128)}, f32[1,512]{1,0:T(1,128)S(1)}, u32[]{:S(2)}) copy-start(f32[1,512]{1,0:T(1,128)S(1)} %get-tuple-element.30) | copy-start | bytes 6148
  108.2 17.8 copy-start.79
  108.2 19.4 copy-start.37
  134.0 604.7 %all-reduce.20.cloned.1.call-start = ((), (), s32[]{:S(2)}) async-start(), calls=%async_computation.1 | async-start | bytes 25165824 | tf_op jit(solution)/shard_map/psum | solution.py:81
  454.5 284.2 %copy-start.90 = (f32[1,512]{1,0:T(1,128)S(1)}, f32[1,512]{1,0:T(1,128)}, u32[]{:S(2)}) copy-start(f32[1,512]{1,0:T(1,128)} %get-tuple-element.29) | copy-start | bytes 6148
  454.6 696.8 %all-reduce.22.cloned.1.call-start = ((), (), s32[]{:S(2)}) async-start(), calls=%async_computation.2 | async-start | bytes 25165824 | tf_op jit(solution)/shard_map/psum | solution.py:81
  841.3 17.8 copy-start.81
  841.4 19.4 copy-start.38
  867.2 601.7 %all-reduce.24.cloned.1.call-start = ((), (), s32[]{:S(2)}) async-start(), calls=%async_computation.3 | async-start | bytes 25165824 | tf_op jit(solution)/shard_map/psum | solution.py:81
  1184.7 284.2 %copy-start.92 = (f32[1,512]{1,0:T(1,128)S(1)}, f32[1,512]{1,0:T(1,128)}, u32[]{:S(2)}) copy-start(f32[1,512]{1,0:T(1,128)} %get-tuple-element.31) | copy-start | bytes 6148
  1184.8 696.6 %all-reduce.26.cloned.1.call-start = ((), (), s32[]{:S(2)}) async-start(), calls=%async_computation.4 | async-start | bytes 25165824 | tf_op jit(solution)/shard_map/psum | solution.py:81
  1571.3 17.8 copy-start.83
  1571.3 19.5 copy-start.39
  1597.2 601.9 %all-reduce.28.cloned.1.call-start = ((), (), s32[]{:S(2)}) async-start(), calls=%async_computation.5 | async-start | bytes 25165824 | tf_op jit(solution)/shard_map/psum | solution.py:81
  1914.9 284.2 %copy-start.87 = (f32[1,512]{1,0:T(1,128)S(1)}, f32[1,512]{1,0:T(1,128)}, u32[]{:S(2)}) copy-start(f32[1,512]{1,0:T(1,128)} %get-tuple-element.28) | copy-start | bytes 6148
  1914.9 696.5 %all-reduce.30.cloned.1.call-start = ((), (), s32[]{:S(2)}) async-start(), calls=%async_computation.6 | async-start | bytes 25165824 | tf_op jit(solution)/shard_map/psum | solution.py:81
  2301.5 19.4 copy-start.40
  2327.3 3688.4 %all-reduce.32.cloned.1.call-start = ((), (), s32[]{:S(2)}) async-start(), calls=%async_computation.7 | async-start | bytes 12582912 | tf_op jit(solution)/shard_map/psum | solution.py:95
  2611.5 17.7 slice-start.10
  2619.4 344.0 %copy-start.73 = (f32[12,512]{1,0:T(8,128)}, f32[12,512]{1,0:T(8,128)S(1)}, u32[]{:S(2)}) copy-start(f32[12,512]{1,0:T(8,128)S(1)} %fusion.233) | copy-start | bytes 73732
  3140.3 286.5 %copy-start.88 = (f32[1,512]{1,0:T(1,128)S(1)}, f32[1,512]{1,0:T(1,128)}, u32[]{:S(2)}) copy-start(f32[1,512]{1,0:T(1,128)} %get-tuple-element.28) | copy-start | bytes 6148
  3140.3 293.3 %copy-start.61 = (f32[12,512]{1,0:T(8,128)S(1)}, f32[12,512]{1,0:T(8,128)}, u32[]{:S(2)}) copy-start(f32[12,512]{1,0:T(8,128)} %copy-done.60) | copy-start | bytes 73732
  3140.3 293.4 %copy-start.69 = (f32[12,512]{1,0:T(8,128)S(1)}, f32[12,512]{1,0:T(8,128)}, u32[]{:S(2)}) copy-start(f32[12,512]{1,0:T(8,128)} %copy-done.68) | copy-start | bytes 73732
  3441.1 16.7 copy-start.25
  3441.1 16.7 copy-start.98
  3441.1 42.5 slice-start.4
  3457.8 25.9 slice-start.5
  3457.8 25.9 copy-start.78
  3483.7 12.9 copy-start.125
  3506.2 291.8 %copy-start.59 = (f32[12,512]{1,0:T(8,128)S(1)}, f32[12,512]{1,0:T(8,128)}, u32[]{:S(2)}) copy-start(f32[12,512]{1,0:T(8,128)} %copy-done.58) | copy-start | bytes 73732
  3964.0 12.9 copy-start.35
  3964.0 12.9 copy-start.105
  3964.0 12.9 copy-start.112
  3964.0 12.9 copy-start.119
  3985.2 290.9 %copy-start.57 = (f32[12,512]{1,0:T(8,128)S(1)}, f32[12,512]{1,0:T(8,128)}, u32[]{:S(2)}) copy-start(f32[12,512]{1,0:T(8,128)} %copy-done.56) | copy-start | bytes 73732
  4283.4 16.7 copy-start.21
  4283.4 16.7 copy-start.99
  4283.4 42.7 slice-start.2
  4300.2 26.0 slice-start.3
  4300.2 26.0 copy-start.72
  4326.1 12.9 copy-start.126
  4348.5 289.9 %copy-start.55 = (f32[12,512]{1,0:T(8,128)S(1)}, f32[12,512]{1,0:T(8,128)}, u32[]{:S(2)}) copy-start(f32[12,512]{1,0:T(8,128)} %copy-done.54) | copy-start | bytes 73732
  4804.1 12.9 copy-start.106
  4825.2 289.6 %copy-start.53 = (f32[12,512]{1,0:T(8,128)S(1)}, f32[12,512]{1,0:T(8,128)}, u32[]{:S(2)}) copy-start(f32[12,512]{1,0:T(8,128)} %copy-done.52) | copy-start | bytes 73732
  5122.0 16.7 copy-start.23
  5122.0 16.7 copy-start.100
  5122.0 42.3 slice-start
  5138.7 25.6 slice-start.1
  5138.7 25.6 copy-start.65
  5164.3 12.9 copy-start.127
  5186.8 288.5 %copy-start.51 = (f32[12,512]{1,0:T(8,128)S(1)}, f32[12,512]{1,0:T(8,128)}, u32[]{:S(2)}) copy-start(f32[12,512]{1,0:T(8,128)} %copy-done.50) | copy-start | bytes 73732
  5632.1 34.0 slice-start.8
  5641.0 25.1 slice-start.9
  5668.0 22.4 slice-start.6
  5673.5 16.9 slice-start.7
  5673.5 16.9 copy-start.74
  5673.5 16.9 copy-start.122
  5673.5 16.9 copy-start.123
  5673.5 16.9 copy-start.124
  5690.5 12.9 copy-start.70
  5690.5 12.9 copy-start.89
  5717.6 288.1 %copy-start.49 = (f32[12,512]{1,0:T(8,128)S(1)}, f32[12,512]{1,0:T(8,128)}, u32[]{:S(2)}) copy-start(f32[12,512]{1,0:T(8,128)} %copy-done.48) | copy-start | bytes 73732
  (88 other events, 590.9 us)
Sparse Core Ops, SparseCore 0:
  134.1 286.8 all-reduce.17
  454.7 284.0 all-reduce.19
  867.3 284.0 all-reduce.21
  1184.9 283.9 all-reduce.23
  1597.3 284.0 all-reduce.25
  1915.1 283.9 all-reduce.27
  2327.4 284.0 all-reduce.29
  5717.7 99.1 all-reduce.31
where the time goes:
time: 6050 us; the launch traced here: 6030 us
  blocking collectives  2270 us (38%)
  waiting for transfers between devices  1990 us (33%)
  matrix products  1210 us (20%)
  other arithmetic  406 us (7%)
  local copies, waits for them, and re-layouts  133 us (2%)
    psum x8, blocking collectives, sum_model(): return lax.psum(values, 'model')  2270 us
    psum x7, waiting for transfers between devices, sum_model(): return lax.psum(values, 'model')  1990 us
    dot_general x4, matrix products, layer_backward(): jnp.einsum('bhqk,bqhe->bkhe', d_scores, q_head, preferred_element_type=jn...  203 us
    sub x4, other arithmetic, attn_probs(): return jax.nn.softmax(scores * HEAD_DIM ** (-0.5), axis=-1)  201 us
    dot_general x4, matrix products, layer_backward(): jnp.einsum('bhqk,bkhe->bqhe', d_scores, k_head, preferred_element_type=jn...  200 us
  transfers between devices with their start and end apart: 8, of which 7 were waited for; matrix products, arithmetic and copies ran while one was open for 0% of the time, Pallas kernels for 0%

commit v1 on v0

v1 whole, which is shorter than its diff:
```python
import functools
import jax
import jax.numpy as jnp
from jax import lax
from jax.experimental import pallas as pl
from jax.experimental.pallas import tpu as pltpu
from jax.sharding import PartitionSpec as P

F32, BF16 = jnp.float32, jnp.bfloat16
T, D, FF, H, E, L = 512, 512, 2048, 8, 64, 4
EPS = 1e-6
LOG2E = 1.4426950408889634
SCALE = E ** -0.5
GK0 = 0.7978845608028654
GK1 = 0.044715


def dot_nn(a, b):
    return lax.dot_general(a, b, (((1,), (0,)), ((), ())), preferred_element_type=F32)


def dot_nt(a, b):
    return lax.dot_general(a, b, (((1,), (1,)), ((), ())), preferred_element_type=F32)


def lanes4(e):
    return jnp.concatenate([e] * (T // 128), axis=1)


def rms_scale(v):
    return lax.rsqrt(jnp.mean(v * v, axis=0, keepdims=True) + EPS)


def rms_pull(v, r, dy):
    a = jnp.mean(dy * v, axis=0, keepdims=True)
    return r * dy - v * (r * r * r * a)


def gelu_fwd(z):
    inner = GK0 * (z + GK1 * (z * z * z))
    return 0.5 * z * (1.0 + jnp.tanh(inner))


def gelu_both(z):
    z2 = z * z
    t = jnp.tanh(z * (GK0 + (GK0 * GK1) * z2))
    hp = 0.5 + 0.5 * t
    g = z * hp
    dg = hp + (0.5 * z) * (1.0 - t * t) * (GK0 + (3.0 * GK0 * GK1) * z2)
    return g, dg


def qrow(hd):
    return 768 * (hd // 4) + 64 * (hd % 4)


def pad_head(rows, hh):
    zero = jnp.zeros_like(rows)
    return jnp.concatenate([rows, zero] if hh == 0 else [zero, rows], axis=0)


def kernel(nseq, x_ref, cot_ref, emb_ref, wqkv_h, wo_h, w1_h, w2_h,
           dx_ref, gqkv_h, go_h, g1_h, g2_h,
           wqkv, wo, w1, w2, wqkvt, wot, w1t, w2t, gqkv, go, g1, g2,
           xs, qkv, ctx, hs, zs, lse, u, m, act, dz, dn, dmid, dctx, dqkv, sem):
    step = pl.program_id(0)
    halves = range(2)
    pairs_in = ([(wqkv_h.at[k], wqkv.at[:, pl.ds(768 * k, 768)]) for k in halves] + [(wo_h, wo)]
                + [(w1_h.at[k], w1.at[:, pl.ds(1024 * k, 1024)]) for k in halves] + [(w2_h, w2)])
    pairs_out = ([(gqkv.at[:, pl.ds(768 * k, 768)], gqkv_h.at[k]) for k in halves] + [(go, go_h)]
                 + [(g1.at[:, pl.ds(1024 * k, 1024)], g1_h.at[k]) for k in halves] + [(g2, g2_h)])

    @pl.when(step == 0)
    def _():
        cps = [pltpu.make_async_copy(s, d, sem.at[i]) for i, (s, d) in enumerate(pairs_in)]
        for c in cps:
            c.start()
        for c in cps:
            c.wait()
        for j in range(3):
            wqkvt[pl.ds(512 * j, 512), :] = wqkv[:, pl.ds(512 * j, 512)].T
        wot[...] = wo[...].T
        for j in range(4):
            w1t[pl.ds(512 * j, 512), :] = w1[:, pl.ds(512 * j, 512)].T
            w2t[:, pl.ds(512 * j, 512)] = w2[pl.ds(512 * j, 512), :].T
        gqkv[...] = jnp.zeros_like(gqkv)
        go[...] = jnp.zeros_like(go)
        g1[...] = jnp.zeros_like(g1)
        g2[...] = jnp.zeros_like(g2)

    xs[0] = x_ref[0].T

    def fwd(l, carry):
        s = xs[l].astype(F32) + lanes4(emb_ref[l])
        u[...] = (s * rms_scale(s)).astype(BF16)
        for j in range(3):
            qkv[l, pl.ds(512 * j, 512), :] = dot_nn(wqkvt[pl.ds(512 * j, 512), :], u[...]).astype(BF16)
        for p in range(4):
            kp = qkv[l, pl.ds(qrow(2 * p) + 256, 128), :].T
            for hh in range(2):
                hd = 2 * p + hh
                qp = pad_head(qkv[l, pl.ds(qrow(hd), 64), :], hh)
                vt = qkv[l, pl.ds(qrow(hd) + 512, 64), :]
                for c in range(2):
                    cs = slice(256 * c, 256 * c + 256)
                    st = dot_nn(kp, qp[:, cs])
                    mx = jnp.max(st, axis=0, keepdims=True)
                    e = jnp.exp2((st - mx) * (SCALE * LOG2E))
                    sm = jnp.sum(e, axis=0, keepdims=True)
                    pr = (e * (1.0 / sm)).astype(BF16)
                    lse[l, pl.ds(hd, 1), pl.ds(256 * c, 256)] = mx * (SCALE * LOG2E) + jnp.log2(sm)
                    ctx[l, pl.ds(64 * hd, 64), pl.ds(256 * c, 256)] = dot_nn(vt, pr).astype(BF16)
        s = xs[l].astype(F32) + lanes4(emb_ref[l])
        hb = (s + dot_nn(wot[...], ctx[l])).astype(BF16)
        hs[l] = hb
        hf = hb.astype(F32)
        m[...] = (hf * rms_scale(hf)).astype(BF16)
        for j in range(4):
            z = dot_nn(w1t[pl.ds(512 * j, 512), :], m[...]).astype(BF16)
            zs[l, pl.ds(512 * j, 512), :] = z

        @pl.when(l < L - 1)
        def _():
            for j in range(4):
                act[pl.ds(512 * j, 512), :] = gelu_fwd(zs[l, pl.ds(512 * j, 512), :].astype(F32)).astype(BF16)
            xs[l + 1] = (hs[l].astype(F32) + dot_nn(w2t[...], act[...])).astype(BF16)
        return carry

    lax.fori_loop(0, L, fwd, 0)

    dn[...] = cot_ref[0].T

    def bwd(i, carry):
        l = L - 1 - i
        hf = hs[l].astype(F32)
        r = rms_scale(hf)
        m[...] = (hf * r).astype(BF16)
        for j in range(4):
            js = pl.ds(512 * j, 512)
            dg = dot_nn(w2[js, :], dn[...]).astype(BF16).astype(F32)
            g, gp = gelu_both(zs[l, js, :].astype(F32))
            act[js, :] = g.astype(BF16)
            dz[js, :] = (dg * gp).astype(BF16)
            g2[js, :] += dot_nt(act[js, :], dn[...])
            g1[:, js] += dot_nt(m[...], dz[js, :])
        dm = dot_nn(w1[...], dz[...]).astype(BF16).astype(F32)
        hf = hs[l].astype(F32)
        dmid[...] = (dn[...].astype(F32) + rms_pull(hf, rms_scale(hf), dm)).astype(BF16)
        go[...] += dot_nt(ctx[l], dmid[...])
        dctx[...] = dot_nn(wo[...], dmid[...]).astype(BF16)
        for p in range(4):
            kp = qkv[l, pl.ds(qrow(2 * p) + 256, 128), :].T
            vp = qkv[l, pl.ds(qrow(2 * p) + 512, 128), :].T
            for hh in range(2):
                hd = 2 * p + hh
                hsl = pl.ds(64 * hd, 64)
                qt = qkv[l, pl.ds(qrow(hd), 64), :]
                kt = qkv[l, pl.ds(qrow(hd) + 256, 64), :]
                dc = dctx[hsl, :]
                qp = pad_head(qt, hh)
                dcp = pad_head(dc, hh)
                delta = jnp.sum(dc.astype(F32) * ctx[l, hsl, :].astype(F32), axis=0, keepdims=True)
                dv = jnp.zeros((E, T), F32)
                dk = jnp.zeros((E, T), F32)
                for c in range(2):
                    cs = slice(256 * c, 256 * c + 256)
                    st = dot_nn(kp, qp[:, cs])
                    pr = jnp.exp2(st * (SCALE * LOG2E) - lse[l, pl.ds(hd, 1), pl.ds(256 * c, 256)])
                    dp = dot_nn(vp, dcp[:, cs]).astype(BF16).astype(F32)
                    ds = (pr * (dp - delta[:, cs])).astype(BF16)
                    dqkv[pl.ds(qrow(hd), 64), pl.ds(256 * c, 256)] = (dot_nn(kt, ds) * SCALE).astype(BF16)
                    dv += dot_nt(dc[:, cs], pr.astype(BF16))
                    dk += dot_nt(qt[:, cs], ds)
                dqkv[pl.ds(qrow(hd) + 256, 64), :] = (dk * SCALE).astype(BF16)
                dqkv[pl.ds(qrow(hd) + 512, 64), :] = dv.astype(BF16)
        s = xs[l].astype(F32) + lanes4(emb_ref[l])
        u[...] = (s * rms_scale(s)).astype(BF16)
        for j in range(3):
            js = pl.ds(512 * j, 512)
            gqkv[:, js] += dot_nt(u[...], dqkv[js, :])
        du = dot_nn(wqkv[...], dqkv[...]).astype(BF16).astype(F32)
        s = xs[l].astype(F32) + lanes4(emb_ref[l])
        dn[...] = (dmid[...].astype(F32) + rms_pull(s, rms_scale(s), du)).astype(BF16)
        return carry

    lax.fori_loop(0, L, bwd, 0)
    dx_ref[0] = dn[...].T

    @pl.when(step == nseq - 1)
    def _():
        cps = [pltpu.make_async_copy(s, d, sem.at[i]) for i, (s, d) in enumerate(pairs_out)]
        for c in cps:
            c.start()
        for c in cps:
            c.wait()


def run_kernel(x, cot, emb, wqkv, wo, w1, w2):
    nseq = x.shape[0]
    embb = jnp.broadcast_to(emb.astype(F32)[:, :, None], (L, D, 128))
    blk = pl.BlockSpec((1, T, D), lambda i: (i, 0, 0))
    anyspec = pl.BlockSpec(memory_space=pl.ANY)
    V = pltpu.VMEM
    return pl.pallas_call(
        functools.partial(kernel, nseq),
        grid=(nseq,),
        in_specs=[blk, blk, pl.BlockSpec(memory_space=pltpu.VMEM)] + [anyspec] * 4,
        out_specs=[blk] + [anyspec] * 4,
        out_shape=[jax.ShapeDtypeStruct((nseq, T, D), BF16), jax.ShapeDtypeStruct((2, D, 768), F32),
                   jax.ShapeDtypeStruct((D, D), F32), jax.ShapeDtypeStruct((2, D, 1024), F32), jax.ShapeDtypeStruct((FF, D), F32)],
        scratch_shapes=[V((D, 1536), BF16), V((D, D), BF16), V((D, FF), BF16), V((FF, D), BF16),
                        V((1536, D), BF16), V((D, D), BF16), V((FF, D), BF16), V((D, FF), BF16),
                        V((D, 1536), F32), V((D, D), F32), V((D, FF), F32), V((FF, D), F32),
                        V((L, D, T), BF16), V((L, 1536, T), BF16), V((L, D, T), BF16), V((L, D, T), BF16),
                        V((L, FF, T), BF16), V((L, H, T), F32), V((D, T), BF16), V((D, T), BF16), V((FF, T), BF16),
                        V((FF, T), BF16), V((D, T), BF16), V((D, T), BF16), V((D, T), BF16), V((1536, T), BF16),
                        pltpu.SemaphoreType.DMA((6,))],
        compiler_params=pltpu.CompilerParams(dimension_semantics=("arbitrary",), vmem_limit_bytes=67_000_000),
    )(x, cot, embb, wqkv, wo, w1, w2)


def solution(mesh):
    spec_col, spec_row, spec_act, spec_rep = P(None, 'model'), P('model', None), P('data', None, None), P(None, None)
    both = ('model', 'data')

    def part(w, d, parts):
        rows = w.shape[0] // parts
        return lax.dynamic_slice_in_dim(w, d * rows, rows, 0)

    def device_step(x_in, cot_out, step_emb, w_q, w_k, w_v, w_o, w_1, w_2):
        mi, di = lax.axis_index('model'), lax.axis_index('data')
        nd = mesh.shape['data']
        half = x_in.shape[0] // 2
        x = lax.dynamic_slice_in_dim(x_in, mi * half, half, 0)
        cot = lax.dynamic_slice_in_dim(cot_out, mi * half, half, 0)
        w_qkv = jnp.concatenate([part(w, di, nd) for w in (w_q, w_k, w_v)], axis=1)
        gat = lambda w: lax.all_gather(w, both, axis=0, tiled=True)
        wqkv = gat(w_qkv).reshape(2, D, 768)
        wo = gat(part(w_o, di, nd))
        w1 = gat(part(w_1, di, nd)).reshape(2, D, 1024)
        w2 = gat(part(w_2, di, nd))
        dx, gqkv, go, g1, g2 = run_kernel(x, cot, step_emb, wqkv, wo, w1, w2)
        red = lambda g: lax.all_gather(lax.psum_scatter(g, both, scatter_dimension=0, tiled=True), 'data', axis=0, tiled=True)
        gqkv = red(gqkv.reshape(2 * D, 768))
        go = red(go)
        g1 = red(g1.reshape(2 * D, 1024))
        g2 = red(g2)
        dx = lax.all_gather(dx, 'model', axis=0, tiled=True)
        return gqkv[:, :256], gqkv[:, 256:512], gqkv[:, 512:], go, g1, g2, dx

    return jax.shard_map(device_step, mesh=mesh,
                         in_specs=(spec_act, spec_act, spec_rep, spec_col, spec_col, spec_col, spec_row, spec_col, spec_row),
                         out_specs=(spec_col, spec_col, spec_col, spec_row, spec_col, spec_row, spec_act),
                         check_vma=False)
```

time: 6050 us -> 1190 us (0.20)
  blocking collectives: 2270 us -> 24.5 us
  waiting for transfers between devices: 1990 us -> 454 us
  matrix products: 1210 us -> 0 us
  Pallas kernels: 0 us -> 672 us
  other arithmetic: 406 us -> 0.65 us
  local copies, waits for them, and re-layouts: 133 us -> 23.5 us
    psum x8 -> x0, blocking collectives: 2270 us -> none  [sum_model(): return lax.psum(values, 'model')]
    psum x8 -> x0, waiting for transfers between devices: 1990 us -> none  [the longest x7 1990 us: sum_model(): return lax.psum(values, 'model')]
    dot_general x71 -> x0, matrix products: 1210 us -> none  [the longest x4 203 us: layer_backward(): jnp.einsum('bhqk,bqhe->bkhe', d_scores, q_head, preferred_element_type=jn...]
    pallas_call x0 -> x1, Pallas kernels: none -> 672 us  [run_kernel(): pl.pallas_call(functools.partial(kernel, nseq), grid=(nseq,), in_specs=[b...]
    reduce_scatter x0 -> x4, waiting for transfers between devices: none -> 241 us  [device_step(): lax.psum_scatter(g, both, scatter_dimension=0, tiled=True)]
    all_gather x0 -> x7, waiting for transfers between devices: none -> 210 us  [the longest x3 71.9 us: device_step(): lax.all_gather(lax.psum_scatter(g, both, scatter_dimension=0, tiled=True)...]
    sub x4 -> x0, other arithmetic: 201 us -> none  [attn_probs(): return jax.nn.softmax(scores * HEAD_DIM ** (-0.5), axis=-1)]
    reduce_sum x16 -> x0, other arithmetic: 113 us -> none  [the longest x8 59.4 us: rms_norm(): jnp.mean(values * values, axis=-1, keepdims=True) + EPS_NORM]
  transfers between devices with their start and end apart: 8 -> 11, of which waited for: 7 -> 11; matrix products, arithmetic and copies ran while one was open for 0% -> 1% of each run, Pallas kernels for 0% -> 0%
where the time goes in v1:
time: 1190 us
  Pallas kernels  672 us (56%)
  waiting for transfers between devices  454 us (38%)
  blocking collectives  24.5 us (2%)
  local copies, waits for them, and re-layouts  23.5 us (2%)
  between operations  13.9 us (1%)
    pallas_call x1, Pallas kernels, run_kernel(): pl.pallas_call(functools.partial(kernel, nseq), grid=(nseq,), in_specs=[b...  672 us
    reduce_scatter x4, waiting for transfers between devices, device_step(): lax.psum_scatter(g, both, scatter_dimension=0, tiled=True)  241 us
    all_gather x3, waiting for transfers between devices, device_step(): lax.all_gather(lax.psum_scatter(g, both, scatter_dimension=0, tiled=True)...  71.9 us
    all_gather x1, waiting for transfers between devices, device_step(): dx = lax.all_gather(dx, 'model', axis=0, tiled=True)  69.9 us
    all_gather x3, waiting for transfers between devices, device_step(): gat = lambda w: lax.all_gather(w, both, axis=0, tiled=True)  67.9 us
  transfers between devices with their start and end apart: 11, of which 11 were waited for; matrix products, arithmetic and copies ran while one was open for 1% of the time, Pallas kernels for 0%

profile of v1, /device:TPU:0, one launch (start us, length us, event | category | flops | bytes accessed | tf_op | source)
XLA Modules:
  0.0 1188.9 jit_solution(2027405816133221220)
XLA Ops:
  7.2 0.0 all-gather.8.cloned.1.call-start
  7.2 0.8 constant_dynamic-slice_fusion.5
  8.0 0.8 constant_dynamic-slice_fusion.3
  8.8 0.6 pad_maximum_fusion
  9.4 0.0 all-gather.8.cloned.1.call-update
  9.4 0.0 all-gather.10.cloned.1.call-start
  9.5 1.6 constant_dynamic-slice_fusion.1
  11.1 0.0 all-gather.10.cloned.1.call-update
  11.1 0.0 all-gather.12.cloned.1.call-start
  11.1 1.6 constant_dynamic-slice_fusion
  12.7 0.0 all-gather.12.cloned.1.call-update
  12.7 0.0 reduce-scatter.5.cloned.1.call-start
  12.8 0.8 constant_dynamic-slice_fusion.2
  13.6 15.3 %all_gather.28.wo_h = bf16[512,512]{1,0:T(8,128)(2,1)} all-gather(bf16[32,512]{1,0:T(8,128)(2,1)S(1)} %constant_dynamic-slice_fusion.2), channel_id=1, replica_groups=mesh['model'=2,'data'=8] {'model','data'}, dimensions={0}, use_global_device_ids=true | all-gather | bytes 557056 | tf_op jit(solution)/shard_map/all_gather | solution.py:237
  28.9 0.0 copy-start.1
  28.9 5.9 constant_dynamic-slice_fusion.6
  34.8 5.6 all-gather.8.cloned.1.call-done
  40.4 31.1 %all-gather.10.cloned.1.call-done = bf16[1024,1024]{1,0:T(8,128)(2,1)} async-done(((bf16[64,1024]{1,0:T(8,128)(2,1)}), bf16[1024,1024]{1,0:T(8,128)(2,1)}) %all-gather.10.cloned.1.call-update) | async-done | bytes 2097168 | tf_op jit(solution)/shard_map/all_gather | solution.py:237
  71.6 31.1 %all-gather.12.cloned.1.call-done.w2_h = bf16[2048,512]{1,0:T(8,128)(2,1)} async-done(((bf16[128,512]{1,0:T(8,128)(2,1)}), bf16[2048,512]{1,0:T(8,128)(2,1)}) %all-gather.12.cloned.1.call-update) | async-done | bytes 2097168 | tf_op jit(solution)/shard_map/all_gather | solution.py:237
  102.7 0.0 copy-done.1
  102.7 1.3 broadcast_in_dim.2.emb_ref
  104.0 672.3 %shard_map.144 = (bf16[6,512,512]{2,1,0:T(8,128)(2,1)}, f32[2,512,768]{2,1,0:T(8,128)}, f32[512,512]{1,0:T(8,128)}, f32[2,512,1024]{2,1,0:T(8,128)}, f32[2048,512]{1,0:T(8,128)}) custom-call(bf16[6,512,512]{2,1,0:T(8,128)(2,1)} %get-tuple-element.21.x_ref, bf16[6,512,512]{2,1,0:T(8,128)(2,1)} %get-tuple-element.20.cot_ref, ...), custom_call_target="tpu_custom_call" | custom-call | tf_op jit(solution)/shard_map/pallas_call | solution.py:204
  776.3 0.0 reduce-scatter.5.cloned.1.call-update
  776.3 0.0 reduce-scatter.9.cloned.1.call-start
  776.4 0.5 reduce-scatter.9.cloned.1.call-update
  776.9 0.0 reduce-scatter.11.cloned.1.call-start
  776.9 0.5 reduce-scatter.11.cloned.1.call-update
  777.5 0.0 reduce-scatter.7.cloned.1.call-start
  777.5 0.7 reduce-scatter.7.cloned.1.call-update
  778.2 0.0 all-gather.20.cloned.1.call-start
  778.3 0.7 all-gather.20.cloned.1.call-update
  779.0 0.0 all-gather.14.cloned.1.call-start
  779.0 51.9 %reduce-scatter.5.cloned.1.call-done = f32[64,768]{1,0:T(8,128)} async-done(((f32[1024,768]{1,0:T(8,128)}), f32[64,768]{1,0:T(8,128)}) %reduce-scatter.5.cloned.1.call-update) | async-done | bytes 196624 | tf_op jit(solution)/shard_map/reduce_scatter | solution.py:243
  830.9 0.0 all-gather.14.cloned.1.call-update
  831.0 0.0 all-gather.16.cloned.1.call-start
  831.0 66.2 %reduce-scatter.9.cloned.1.call-done = f32[64,1024]{1,0:T(8,128)} async-done(((f32[1024,1024]{1,0:T(8,128)}), f32[64,1024]{1,0:T(8,128)}) %reduce-scatter.9.cloned.1.call-update) | async-done | bytes 262160 | tf_op jit(solution)/shard_map/reduce_scatter | solution.py:243
  897.2 0.0 all-gather.16.cloned.1.call-update
  897.3 0.0 all-gather.18.cloned.1.call-start
  897.3 65.6 %reduce-scatter.11.cloned.1.call-done = f32[128,512]{1,0:T(8,128)} async-done(((f32[2048,512]{1,0:T(8,128)}), f32[128,512]{1,0:T(8,128)}) %reduce-scatter.11.cloned.1.call-update) | async-done | bytes 262160 | tf_op jit(solution)/shard_map/reduce_scatter | solution.py:243
  962.9 0.0 all-gather.18.cloned.1.call-update
  962.9 57.7 %reduce-scatter.7.cloned.1.call-done = f32[32,512]{1,0:T(8,128)} async-done(((f32[512,512]{1,0:T(8,128)}), f32[32,512]{1,0:T(8,128)}) %reduce-scatter.7.cloned.1.call-update) | async-done | bytes 65552 | tf_op jit(solution)/shard_map/reduce_scatter | solution.py:243
  1020.6 9.2 all_gather.32
  1029.8 69.9 %all-gather.20.cloned.1.call-done = bf16[12,512,512]{2,1,0:T(8,128)(2,1)} async-done(((bf16[6,512,512]{2,1,0:T(8,128)(2,1)}), bf16[12,512,512]{2,1,0:T(8,128)(2,1)}) %all-gather.20.cloned.1.call-update) | async-done | bytes 6291472 | tf_op jit(solution)/shard_map/all_gather | solution.py:248
  1099.7 23.4 %all-gather.14.cloned.1.call-done = f32[512,768]{1,0:T(8,128)} async-done(((f32[64,768]{1,0:T(8,128)}), f32[512,768]{1,0:T(8,128)}) %all-gather.14.cloned.1.call-update) | async-done | bytes 1572880 | tf_op jit(solution)/shard_map/all_gather | solution.py:243
  1123.1 0.0 slice-start
  1123.1 2.7 fusion
  1125.8 22.8 %all-gather.16.cloned.1.call-done = f32[512,1024]{1,0:T(8,128)} async-done(((f32[64,1024]{1,0:T(8,128)}), f32[512,1024]{1,0:T(8,128)}) %all-gather.16.cloned.1.call-update) | async-done | bytes 2097168 | tf_op jit(solution)/shard_map/all_gather | solution.py:243
  1148.6 25.6 %all-gather.18.cloned.1.call-done = f32[1024,512]{1,0:T(8,128)} async-done(((f32[128,512]{1,0:T(8,128)}), f32[1024,512]{1,0:T(8,128)}) %all-gather.18.cloned.1.call-update) | async-done | bytes 2097168 | tf_op jit(solution)/shard_map/all_gather | solution.py:243
  1174.3 0.0 copy-start
  1174.3 0.8 copy.20
  1175.1 0.0 slice-start.1
  1175.1 3.3 copy.21
  1178.4 0.0 copy-done
  1178.4 1.3 copy.22
  1179.7 0.0 slice-done
  1179.7 0.0 slice-done.1
  1179.7 2.7 copy.23
  (1 shorter events, 0.0 us)
Async XLA Ops:
  7.2 33.3 %all-gather.8.cloned.1.call-start = ((), (), s32[]{:S(2)}) async-start(), calls=%async_computation.4 | async-start | bytes 1671168 | tf_op jit(solution)/shard_map/all_gather | solution.py:237
  9.4 62.1 %all-gather.10.cloned.1.call-start = ((), (), s32[]{:S(2)}) async-start(), calls=%async_computation.5 | async-start | bytes 2228224 | tf_op jit(solution)/shard_map/all_gather | solution.py:237
  11.1 91.6 %all-gather.12.cloned.1.call-start = ((), (), s32[]{:S(2)}) async-start(), calls=%async_computation.6 | async-start | bytes 2228224 | tf_op jit(solution)/shard_map/all_gather | solution.py:237
  12.7 818.2 %reduce-scatter.5.cloned.1.call-start = ((), (), s32[]{:S(2)}) async-start(), calls=%async_computation.7 | async-start | bytes 3342336 | tf_op jit(solution)/shard_map/reduce_scatter | solution.py:243
  28.9 73.8 %copy-start.1 = (bf16[4,512]{1,0:T(4,128)(2,1)S(1)}, bf16[4,512]{1,0:T(4,128)(2,1)}, u32[]{:S(2)}) copy-start(bf16[4,512]{1,0:T(4,128)(2,1)} %param.11) | copy-start | bytes 12292
  776.3 120.9 %reduce-scatter.9.cloned.1.call-start = ((), (), s32[]{:S(2)}) async-start(), calls=%async_computation.10 | async-start | bytes 4456448 | tf_op jit(solution)/shard_map/reduce_scatter | solution.py:243
  776.9 186.0 %reduce-scatter.11.cloned.1.call-start = ((), (), s32[]{:S(2)}) async-start(), calls=%async_computation.12 | async-start | bytes 4456448 | tf_op jit(solution)/shard_map/reduce_scatter | solution.py:243
  777.5 243.1 %reduce-scatter.7.cloned.1.call-start = ((), (), s32[]{:S(2)}) async-start(), calls=%async_computation.9 | async-start | bytes 1114112 | tf_op jit(solution)/shard_map/reduce_scatter | solution.py:243
  778.2 321.5 %all-gather.20.cloned.1.call-start = ((), (), s32[]{:S(2)}) async-start(), calls=%async_computation.14 | async-start | bytes 9437184 | tf_op jit(solution)/shard_map/all_gather | solution.py:248
  779.0 344.2 %all-gather.14.cloned.1.call-start = ((), (), s32[]{:S(2)}) async-start(), calls=%async_computation.8 | async-start | bytes 1769472 | tf_op jit(solution)/shard_map/all_gather | solution.py:243
  831.0 317.7 %all-gather.16.cloned.1.call-start = ((), (), s32[]{:S(2)}) async-start(), calls=%async_computation.11 | async-start | bytes 2359296 | tf_op jit(solution)/shard_map/all_gather | solution.py:243
  897.3 277.0 %all-gather.18.cloned.1.call-start = ((), (), s32[]{:S(2)}) async-start(), calls=%async_computation.13 | async-start | bytes 2359296 | tf_op jit(solution)/shard_map/all_gather | solution.py:243
  1123.1 56.6 %slice-start = ((s8[6291456]{0:T(1024)(128)(4,1)}), s8[2097152]{0:T(1024)(128)(4,1)S(1)}, s32[]{:S(2)}) async-start(s8[6291456]{0:T(1024)(128)(4,1)} %bitcast.4), calls=%async_computation.15 | async-start | bytes 4194304
  1174.3 4.1 copy-start
  1175.1 4.6 slice-start.1
Sparse Core Ops, SparseCore 0:
  10.8 29.6 all-gather.7
  43.2 28.2 all-gather.9
  74.4 28.2 all-gather.11
  776.4 54.4 reduce-scatter.4
  833.6 63.5 reduce-scatter.8
  899.4 63.4 reduce-scatter.10
  965.7 54.8 reduce-scatter.6
  1022.1 77.5 all-gather.19
  1101.5 21.5 all-gather.13
  1124.8 23.7 all-gather.15
  1150.5 23.7 all-gather.17

commit v2 on v1

v2 whole, which is shorter than its diff:
```python
import functools

import jax
import jax.numpy as jnp
from jax import lax
from jax.experimental import pallas as pl
from jax.experimental.pallas import tpu as pltpu
from jax.sharding import PartitionSpec as P

F32, BF16 = jnp.float32, jnp.bfloat16
T, D, FF, H, E, L = 512, 512, 2048, 8, 64, 4
EPS = 1e-6
CEXP = E ** -0.5 * 1.4426950408889634
SCALE = E ** -0.5
GK0 = 0.7978845608028654
GK1 = 0.044715
R = 16
LN = 128


def dot_nn(a, b):
    return lax.dot_general(a, b, (((1,), (0,)), ((), ())), preferred_element_type=F32)


def dot_nt(a, b):
    return lax.dot_general(a, b, (((1,), (1,)), ((), ())), preferred_element_type=F32)


def rows(r, n=R):
    return pl.ds(r, n)


def wide(e):
    return jnp.concatenate([e] * (T // LN), axis=1)


def fold8(v):
    return v[:8] + v[8:]


def col_sum(tile_fn):
    accs = [None, None]
    for i, r in enumerate(range(0, D, R)):
        v = fold8(tile_fn(r))
        accs[i % 2] = v if accs[i % 2] is None else accs[i % 2] + v
    return jnp.sum(accs[0] + accs[1], axis=0, keepdims=True)


def rms_of(tile_fn):
    def sq(r):
        v = tile_fn(r)
        return v * v
    return lax.rsqrt(col_sum(sq) * (1.0 / D) + EPS)


def weave(*streams):
    total = max(len(s) for s in streams)
    done = [0] * len(streams)
    for t in range(total):
        for k, s in enumerate(streams):
            upto = -(-len(s) * (t + 1) // total)
            while done[k] < upto:
                s[done[k]]()
                done[k] += 1


def gelu_fwd(z):
    t = jnp.tanh(z * (GK0 + (GK0 * GK1) * (z * z)))
    return (0.5 * z) * (1.0 + t)


def gelu_both(z):
    z2 = z * z
    t = jnp.tanh(z * (GK0 + (GK0 * GK1) * z2))
    up = 1.0 + t
    hz = 0.5 * z
    w = z * (GK0 + (3.0 * GK0 * GK1) * z2)
    return hz * up, (0.5 * up) * (1.0 + w * (1.0 - t))


def qrow(hd):
    return 768 * (hd // 4) + 64 * (hd % 4)


def pad_head(block, hh):
    zero = jnp.zeros_like(block)
    return jnp.concatenate([block, zero] if hh == 0 else [zero, block], axis=0)


def max_cols(ref, cols):
    accs = [None] * 4
    for i, r in enumerate(range(0, T, 8)):
        v = ref[rows(r, 8), cols]
        accs[i % 4] = v if accs[i % 4] is None else jnp.maximum(accs[i % 4], v)
    m = jnp.maximum(jnp.maximum(accs[0], accs[1]), jnp.maximum(accs[2], accs[3]))
    return jnp.max(m, axis=0, keepdims=True)

GL, GROWS = 256, 6144

def kernel(nseq, x_ref, cot_ref, emb_ref, wqkv_h, wo_h, w1_h, w2_h,
           dx_ref, grad_h,
           wqkv, wo, w1, w2, wqkvt, wot, w1t, w2t, gqkv, go, g1, g2,
           xs, qkv, ctx, ctxl, hs, zs, lse, u, m, act, dz, dn, dmid, dctx, dqkv, tmp, sbuf, sem):
    step = pl.program_id(0)
    halves = range(2)
    pairs_in = ([(wqkv_h.at[k], wqkv.at[:, pl.ds(768 * k, 768)]) for k in halves] + [(wo_h, wo)]
                + [(w1_h.at[k], w1.at[:, pl.ds(1024 * k, 1024)]) for k in halves] + [(w2_h, w2)])
    @pl.when(step == 0)
    def _():
        cps = [pltpu.make_async_copy(s, d, sem.at[i]) for i, (s, d) in enumerate(pairs_in)]
        for c in cps:
            c.start()
        for c in cps:
            c.wait()
        for j in range(3):
            wqkvt[pl.ds(512 * j, 512), :] = wqkv[:, pl.ds(512 * j, 512)].T
        wot[...] = wo[...].T
        for j in range(4):
            w1t[pl.ds(512 * j, 512), :] = w1[:, pl.ds(512 * j, 512)].T
            w2t[:, pl.ds(512 * j, 512)] = w2[pl.ds(512 * j, 512), :].T
        gqkv[...] = jnp.zeros_like(gqkv)
        go[...] = jnp.zeros_like(go)
        g1[...] = jnp.zeros_like(g1)
        g2[...] = jnp.zeros_like(g2)

    xs[0] = x_ref[0].T
    half = [pl.ds(0, 256), pl.ds(256, 256)]

    def s_tile(l):
        return lambda r: xs[l, rows(r), :].astype(F32) + wide(emb_ref[l, rows(r), :].astype(F32))

    def norm_into(dst, tile_fn):
        box = {}

        def stat():
            box['r'] = rms_of(tile_fn)

        def put(r):
            dst[rows(r), :] = (tile_fn(r) * box['r']).astype(BF16)

        return [stat] + [functools.partial(put, r) for r in range(0, D, R)]

    def pull_into(dst, base, tile_fn, dy):
        box = {}

        def stat():
            box['r'] = rms_of(tile_fn)

        def stat2():
            a = col_sum(lambda r: dy[rows(r), :].astype(F32) * tile_fn(r)) * (1.0 / D)
            rr = box['r']
            box['a'] = rr * rr * rr * a

        def put(r):
            g = dy[rows(r), :].astype(F32)
            dst[rows(r), :] = (base[rows(r), :].astype(F32) + (box['r'] * g - tile_fn(r) * box['a'])).astype(BF16)

        return [stat, stat2] + [functools.partial(put, r) for r in range(0, D, R)]

    def run(stream):
        for f in stream:
            f()

    def h_tile(l):
        return lambda r: hs[l, rows(r), :].astype(F32)

    def fwd(l, carry):
        run(norm_into(u, s_tile(l)))
        for j in range(3):
            qkv[l, pl.ds(512 * j, 512), :] = dot_nn(wqkvt[pl.ds(512 * j, 512), :], u[...]).astype(BF16)

        kps = {}
        inv = {}

        def stage_a(hd):
            p, hh = divmod(hd, 2)

            def first():
                if hh == 0:
                    kps[p] = qkv[l, pl.ds(qrow(hd) + 256, 128), :].T

            def part(c):
                qp = pad_head(qkv[l, pl.ds(qrow(hd), 64), half[c]], hh)
                sbuf[hd % 2, :, half[c]] = dot_nn(kps[p], qp)

            return [first, lambda: part(0), lambda: part(1)]

        def stage_b(hd):
            sref, eref = sbuf.at[hd % 2], act.at[pl.ds(512 * (hd % 2), 512), :]

            def group(g):
                cols = half[g]
                mx = max_cols(sref, cols) * CEXP
                accs = [None, None]
                for i, r in enumerate(range(0, T, 8)):
                    e = jnp.exp2(sref[rows(r, 8), cols] * CEXP - mx)
                    accs[i % 2] = e if accs[i % 2] is None else accs[i % 2] + e
                    eref[rows(r, 8), cols] = e.astype(BF16)
                sm = jnp.sum(accs[0] + accs[1], axis=0, keepdims=True)
                lse[l, pl.ds(hd, 1), cols] = mx + jnp.log2(sm)
                inv[hd, g] = 1.0 / sm

            return [functools.partial(group, g) for g in range(2)]

        def stage_c(hd):
            def part(c):
                cn = dot_nn(qkv[l, pl.ds(qrow(hd) + 512, 64), :], act[pl.ds(512 * (hd % 2), 512), half[c]])
                cn = cn * inv[hd, c]
                hi = cn.astype(BF16)
                ctx[l, pl.ds(64 * hd, 64), half[c]] = hi
                ctxl[l, pl.ds(64 * hd, 64), half[c]] = (cn - hi.astype(F32)).astype(BF16)

            return [lambda: part(0), lambda: part(1)]

        run(stage_a(0))
        for hd in range(H + 1):
            mx = (stage_a(hd + 1) if hd + 1 < H else []) + (stage_c(hd - 1) if hd >= 1 else [])
            va = stage_b(hd) if hd < H else []
            weave(mx, va)

        st = s_tile(l)
        for c in range(2):
            o = dot_nn(wot[...], ctx[l, :, half[c]])
            for r in range(0, D, R):
                sx = xs[l, rows(r), half[c]].astype(F32) + jnp.concatenate([emb_ref[l, rows(r), :].astype(F32)] * 2, axis=1)
                hs[l, rows(r), half[c]] = (sx + o[r:r + R]).astype(BF16)
        run(norm_into(m, h_tile(l)))

        def z_dot(j):
            def f(c):
                js = pl.ds(512 * j, 512)
                zs[l, js, half[c]] = dot_nn(w1t[js, :], m[:, half[c]]).astype(BF16)
            return [lambda: f(0), lambda: f(1)]

        def gelu_stream(j):
            def f(r):
                act[rows(r), :] = gelu_fwd(zs[l, rows(r), :].astype(F32)).astype(BF16)
            return [functools.partial(f, r) for r in range(512 * j, 512 * j + 512, R)]

        @pl.when(l < L - 1)
        def _():
            run(z_dot(0))
            for j in range(4):
                weave(z_dot(j + 1) if j < 3 else [], gelu_stream(j))
            for c in range(2):
                o = dot_nn(w2t[...], act[:, half[c]])
                for r in range(0, D, R):
                    xs[l + 1, rows(r), half[c]] = (hs[l, rows(r), half[c]].astype(F32) + o[r:r + R]).astype(BF16)

        @pl.when(l == L - 1)
        def _():
            for j in range(4):
                run(z_dot(j))
        return carry

    lax.fori_loop(0, L, fwd, 0)

    dn[...] = cot_ref[0].T

    def bwd(i, carry):
        l = L - 1 - i

        def dg_dot(j):
            def f(c):
                js = pl.ds(512 * j, 512)
                dz[js, half[c]] = dot_nn(w2[js, :], dn[:, half[c]]).astype(BF16)
            return [lambda: f(0), lambda: f(1)]

        def gelu_stream(j):
            def f(r):
                g, gp = gelu_both(zs[l, rows(r), :].astype(F32))
                act[rows(r), :] = g.astype(BF16)
                dz[rows(r), :] = (dz[rows(r), :].astype(F32) * gp).astype(BF16)
            return [functools.partial(f, r) for r in range(512 * j, 512 * j + 512, R)]

        def wgrad(j):
            js = pl.ds(512 * j, 512)

            def a(c):
                g2[js, half[c]] += dot_nt(act[js, :], dn[half[c], :])

            def b(c):
                jc = pl.ds(512 * j + 256 * c, 256)
                g1[:, jc] += dot_nt(m[...], dz[jc, :])
            return [lambda: a(0), lambda: a(1), lambda: b(0), lambda: b(1)]

        weave(dg_dot(0), norm_into(m, h_tile(l)))
        weave(dg_dot(1) + dg_dot(2), gelu_stream(0))
        weave(wgrad(0) + dg_dot(3), gelu_stream(1))
        weave(wgrad(1), gelu_stream(2))
        weave(wgrad(2), gelu_stream(3))
        for c in range(2):
            tmp[:, half[c]] = dot_nn(w1[...], dz[:, half[c]]).astype(BF16)
        weave(wgrad(3), pull_into(dmid, dn, h_tile(l), tmp))
        for c in range(2):
            dctx[:, half[c]] = dot_nn(wo[...], dmid[:, half[c]]).astype(BF16)

        kps, vps, delta = {}, {}, {}

        def stage_a(hd):
            p, hh = divmod(hd, 2)
            hsl = pl.ds(64 * hd, 64)

            def first():
                if hh == 0:
                    kps[p] = qkv[l, pl.ds(qrow(hd) + 256, 128), :].T
                    vps[p] = qkv[l, pl.ds(qrow(hd) + 512, 128), :].T
                c = ctx[l, hsl, :].astype(F32) + ctxl[l, hsl, :].astype(F32)
                delta[hd] = jnp.sum(dctx[hsl, :].astype(F32) * c, axis=0, keepdims=True)

            def s_part(c):
                qp = pad_head(qkv[l, pl.ds(qrow(hd), 64), half[c]], hh)
                sbuf[hd % 2, :, half[c]] = dot_nn(kps[p], qp)

            def p_part(c):
                dcp = pad_head(dctx[hsl, half[c]], hh)
                dz[pl.ds(512 * (hd % 2), 512), half[c]] = dot_nn(vps[p], dcp).astype(BF16)

            return [first, lambda: s_part(0), lambda: s_part(1), lambda: p_part(0), lambda: p_part(1)]

        def stage_b(hd):
            sl = 512 * (hd % 2)

            def group(g, r0):
                cols = half[g]
                ls = lse[l, pl.ds(hd, 1), cols]
                de = delta[hd][:, 256 * g:256 * g + 256]
                for r in range(r0, r0 + 128, 8):
                    pr = jnp.exp2(sbuf[hd % 2, rows(r, 8), cols] * CEXP - ls)
                    act[rows(sl + r, 8), cols] = pr.astype(BF16)
                    dp = dz[rows(sl + r, 8), cols].astype(F32)
                    act[rows(1024 + sl + r, 8), cols] = (pr * (dp - de)).astype(BF16)

            return [functools.partial(group, g, r0) for g in range(2) for r0 in range(0, T, 128)]

        def stage_c(hd):
            sl = 512 * (hd % 2)
            pb = act.at[pl.ds(sl, 512), :]
            db = act.at[pl.ds(1024 + sl, 512), :]
            hsl = pl.ds(64 * hd, 64)

            def f_v():
                dqkv[pl.ds(qrow(hd) + 512, 64), :] = dot_nt(dctx[hsl, :], pb[...]).astype(BF16)

            def f_k():
                dqkv[pl.ds(qrow(hd) + 256, 64), :] = (dot_nt(qkv[l, pl.ds(qrow(hd), 64), :], db[...]) * SCALE).astype(BF16)

            def f_q():
                dqkv[pl.ds(qrow(hd), 64), :] = (dot_nn(qkv[l, pl.ds(qrow(hd) + 256, 64), :], db[...]) * SCALE).astype(BF16)

            return [f_v, f_k, f_q]

        def wo_grad():
            go[...] += dot_nt(ctx[l], dmid[...])

        run(stage_a(0))
        for hd in range(H + 1):
            mx = (stage_a(hd + 1) if hd + 1 < H else []) + (stage_c(hd - 1) if hd >= 1 else [wo_grad])
            va = stage_b(hd) if hd < H else []
            weave(mx, va)

        for c in range(2):
            tmp[:, half[c]] = dot_nn(wqkv[...], dqkv[:, half[c]]).astype(BF16)

        def qkv_grad(j):
            js = pl.ds(256 * j, 256)
            gqkv[:, js] += dot_nt(u[...], dqkv[js, :])

        run(norm_into(u, s_tile(l)))
        weave([functools.partial(qkv_grad, j) for j in range(6)], pull_into(dn, dmid, s_tile(l), tmp))
        return carry

    lax.fori_loop(0, L, bwd, 0)
    dx_ref[0] = dn[...].T

    @pl.when(step == nseq - 1)
    def _():
        cps = []
        for m_ in range(2):
            g = grad_h.at[m_]
            for k in range(3):
                cps.append((gqkv.at[:, pl.ds(768 * m_ + 256 * k, 256)], g.at[pl.ds(512 * k, 512), :]))
            for k in range(4):
                cps.append((g1.at[:, pl.ds(1024 * m_ + 256 * k, 256)], g.at[pl.ds(1536 + 512 * k, 512), :]))
            for k in range(2):
                cps.append((g2.at[pl.ds(1024 * m_, 1024), pl.ds(256 * k, 256)], g.at[pl.ds(3584 + 1024 * k, 1024), :]))
            for k in range(2):
                cps.append((go.at[pl.ds(256 * m_, 256), pl.ds(256 * k, 256)], g.at[pl.ds(5632 + 256 * k, 256), :]))
        cps = [pltpu.make_async_copy(s, d, sem.at[i]) for i, (s, d) in enumerate(cps)]
        for c in cps:
            c.start()
        for c in cps:
            c.wait()


def run_kernel(x, cot, emb, wqkv, wo, w1, w2):
    nseq = x.shape[0] // 2
    embb = jnp.broadcast_to(emb[:, :, None], (L, D, LN))
    blk = pl.BlockSpec((1, T, D), lambda i: (lax.axis_index('model') * nseq + i, 0, 0))
    anyspec = pl.BlockSpec(memory_space=pl.ANY)
    V = pltpu.VMEM
    return pl.pallas_call(
        functools.partial(kernel, nseq),
        grid=(nseq,),
        in_specs=[blk, blk, pl.BlockSpec(memory_space=pltpu.VMEM)] + [anyspec] * 4,
        out_specs=[blk, anyspec],
        out_shape=[jax.ShapeDtypeStruct((2 * nseq, T, D), BF16), jax.ShapeDtypeStruct((2, GROWS, GL), F32)],
        scratch_shapes=[V((D, 1536), BF16), V((D, D), BF16), V((D, FF), BF16), V((FF, D), BF16),
                        V((1536, D), BF16), V((D, D), BF16), V((FF, D), BF16), V((D, FF), BF16),
                        V((D, 1536), F32), V((D, D), F32), V((D, FF), F32), V((FF, D), F32),
                        V((L, D, T), BF16), V((L, 1536, T), BF16), V((L, D, T), BF16), V((L, D, T), BF16), V((L, D, T), BF16),
                        V((L, FF, T), BF16), V((L, H, T), F32), V((D, T), BF16), V((D, T), BF16), V((FF, T), BF16),
                        V((FF, T), BF16), V((D, T), BF16), V((D, T), BF16), V((D, T), BF16), V((1536, T), BF16), V((D, T), BF16),
                        V((2, T, T), F32), pltpu.SemaphoreType.DMA((22,))],
        compiler_params=pltpu.CompilerParams(dimension_semantics=("arbitrary",), vmem_limit_bytes=67_000_000),
    )(x, cot, embb, wqkv, wo, w1, w2)


MESH_ID = pl.DeviceIdType.MESH
NCOL = 2
BR, GL = 384, 256
GROWS = NCOL * 8 * BR
ORDERS = ('xyz', 'yxz')
NW = 6


def neighbours():
    mi = lax.axis_index('model')
    di = lax.axis_index('data')
    core, x, y = di % 2, (di // 2) % 2, di // 4
    dev = {'x': {'model': mi, 'data': di + 2 - 4 * x}, 'y': {'model': mi, 'data': di + 4 - 8 * y},
           'z': {'model': 1 - mi, 'data': di}, 'c': {'model': mi, 'data': di + 1 - 2 * core}}
    return {'x': x, 'y': y, 'z': mi}, core, dev


def greet(dev, names):
    barrier = pltpu.get_barrier_semaphore()
    for d in names:
        pl.semaphore_signal(barrier, inc=1, device_id=dev[d], device_id_type=MESH_ID)
    pl.semaphore_wait(barrier, len(names))


def gather_kernel(*refs):
    w_in, (wqkv, wo, w1, w2), (stage, lsem, ssem, zsend, zrecv, csend, crecv) = refs[:NW], refs[NW:NW + 4], refs[NW + 4:]
    me, core, dev = neighbours()
    mi = me['z']
    greet(dev, 'zc')

    def place(k, m, r0, n):
        if k < 3:
            return wqkv.at[m, pl.ds(r0, n), pl.ds(256 * k, 256)]
        if k == 3:
            return wo.at[pl.ds(256 * m + r0, n), :]
        if k == 4:
            return w1.at[m, pl.ds(r0, n), :]
        return w2.at[pl.ds(1024 * m + r0, n), :]

    n_rows = (512, 512, 512, 256, 512, 1024)
    zc, cc, loc, put = [], [], [], []
    for k in range(NW):
        n = n_rows[k] // 2
        zc.append(pltpu.make_async_remote_copy(w_in[k].at[pl.ds(n * core, n), :], place(k, mi, n * core, n), zsend.at[k], zrecv.at[k],
                                               device_id=dev['z'], device_id_type=MESH_ID))
        zc[k].start()
    for k in range(NW):
        loc.append(pltpu.make_async_copy(w_in[k], stage.at[k, pl.ds(0, n_rows[k]), pl.ds(0, w_in[k].shape[1])], lsem.at[k]))
        loc[k].start()
    for k in range(NW):
        loc[k].wait()
        put.append(pltpu.make_async_copy(stage.at[k, pl.ds(0, n_rows[k]), pl.ds(0, w_in[k].shape[1])], place(k, mi, 0, n_rows[k]), ssem.at[k]))
        put[k].start()
    for k in range(NW):
        n = n_rows[k] // 2
        zc[k].wait_recv()
        got = place(k, 1 - mi, n * core, n)
        cc.append(pltpu.make_async_remote_copy(got, got, csend.at[k], crecv.at[k], device_id=dev['c'], device_id_type=MESH_ID))
        cc[k].start()
    for k in range(NW):
        put[k].wait()
        zc[k].wait_send()
        cc[k].wait()


def run_gather(ws):
    anyspec = pl.BlockSpec(memory_space=pl.ANY)
    S = pltpu.SemaphoreType.DMA
    return pl.pallas_call(
        gather_kernel,
        in_specs=[anyspec] * NW,
        out_specs=[anyspec] * 4,
        out_shape=[jax.ShapeDtypeStruct((2, D, 768), BF16), jax.ShapeDtypeStruct((D, D), BF16),
                   jax.ShapeDtypeStruct((2, D, 1024), BF16), jax.ShapeDtypeStruct((FF, D), BF16)],
        scratch_shapes=[pltpu.VMEM((NW, 1024, 1024), BF16)] + [S((NW,))] * 6,
        compiler_params=pltpu.CompilerParams(vmem_limit_bytes=60_000_000, collective_id=0, has_side_effects=True),
    )(*ws)


def reduce_kernel(g_h, dx_in, out, dx, acc, rd, r1, r2, r3, locsem, ds, dr, ps, pr, gs, gr, cs, cr, xs_, xr_):
    me, core, dev = neighbours()
    x, y, mi = me['x'], me['y'], me['z']
    nseq = dx.shape[0] // 2

    def rdma(src, dst, s, r, d):
        return pltpu.make_async_remote_copy(src, dst, s, r, device_id=dev[d], device_id_type=MESH_ID)

    greet(dev, 'xyzc')

    xc = []
    for s in range(nseq):
        here = dx.at[mi * nseq + s]
        xc.append(rdma(here, here, xs_.at[s], xr_.at[s], 'z'))

    def blk(color, pos):
        return (pos['z'] * NCOL + color) * 4 + pos['y'] * 2 + pos['x']

    def all_pos(fixed):
        out_ = [dict(fixed)]
        for ax in 'zyx':
            if ax not in fixed:
                out_ = [dict(p, **{ax: v}) for p in out_ for v in (0, 1)]
        return out_

    def add(dst, src):
        def body(i, c):
            r = pl.multiple_of(i * 32, 32)
            acc[dst, pl.ds(r, 32), :] += src[pl.ds(r, 32), :]
            return c
        lax.fori_loop(0, BR // 32, body, 0)

    first, rest = [], []
    for color in range(NCOL):
        a = ORDERS[color][0]
        first += [blk(color, p) for p in all_pos({a: 1 - me[a]})]
        rest += [blk(color, p) for p in all_pos({a: me[a]})]
    seq = first + rest
    nb = len(seq)
    dcp, lcp = [], []
    for i, b in enumerate(seq):
        dcp.append(rdma(g_h.at[b * 2 + (1 - core)], rd.at[b], ds.at[i], dr.at[i], 'c'))
        lcp.append(pltpu.make_async_copy(g_h.at[b * 2 + core], acc.at[b], locsem.at[i]))
    for i in range(nb):
        dcp[i].start()
        lcp[i].start()
    for s in range(4):
        xc[s].start()

    def fold_core(i):
        dcp[i].wait_recv()
        lcp[i].wait()
        add(seq[i], rd.at[seq[i]])

    p1, p2, p3 = [], [], []
    for j in range(4):
        for color in range(NCOL):
            a = ORDERS[color][0]
            i = 4 * color + j
            fold_core(i)
            cp = rdma(acc.at[blk(color, all_pos({a: 1 - me[a]})[j])], r1.at[i], ps.at[i], pr.at[i], a)
            cp.start()
            p1.append(cp)
    p1 = [p1[(i % 4) * NCOL + i // 4] for i in range(4 * NCOL)]
    for i in range(4 * NCOL, nb):
        fold_core(i)
    for color in range(NCOL):
        a, b = ORDERS[color][0], ORDERS[color][1]
        for j, p in enumerate(all_pos({a: me[a]})):
            p1[4 * color + j].wait_recv()
            add(blk(color, p), r1.at[4 * color + j])
        for j, p in enumerate(all_pos({a: me[a], b: 1 - me[b]})):
            i = 2 * color + j
            cp = rdma(acc.at[blk(color, p)], r2.at[i], ps.at[4 * NCOL + i], pr.at[4 * NCOL + i], b)
            cp.start()
            p2.append(cp)
    for color in range(NCOL):
        a, b, c = ORDERS[color]
        for j, p in enumerate(all_pos({a: me[a], b: me[b]})):
            p2[2 * color + j].wait_recv()
            add(blk(color, p), r2.at[2 * color + j])
        cp = rdma(acc.at[blk(color, dict(me, **{c: 1 - me[c]}))], r3.at[color], ps.at[6 * NCOL + color], pr.at[6 * NCOL + color], c)
        cp.start()
        p3.append(cp)
    for s in range(4, nseq):
        xc[s].start()

    cps, g1_, g2_ = [], [], []

    def out_at(color, yy, xx):
        return out.at[(color * 4 + yy * 2 + xx) * 2 + core]

    def to_sibling(color, yy, xx, i):
        o = out_at(color, yy, xx)
        cp = rdma(o, o, cs.at[i], cr.at[i], 'c')
        cp.start()
        cps.append(cp)

    for color in range(NCOL):
        p3[color].wait_recv()
        b = blk(color, me)
        o_blk = (color * 4 + y * 2 + x) * 2 + core

        def body(i, c, b=b, o_blk=o_blk, color=color):
            r = pl.multiple_of(i * 32, 32)
            out[o_blk, pl.ds(r, 32), :] = acc[b, pl.ds(r, 32), :] + r3[color, pl.ds(r, 32), :]
            return c
        lax.fori_loop(0, BR // 32, body, 0)
        o = out_at(color, y, x)
        cp = rdma(o, o, gs.at[color], gr.at[color], ORDERS[color][0])
        cp.start()
        g1_.append(cp)
        c2 = rdma(o, o, gs.at[NCOL + 2 * color], gr.at[NCOL + 2 * color], ORDERS[color][1])
        c2.start()
        g2_.append(c2)
        to_sibling(color, y, x, color)
    for color in range(NCOL):
        g1_[color].wait_recv()
        a, b = ORDERS[color][0], ORDERS[color][1]
        yy, xx = (y, 1 - x) if a == 'x' else (1 - y, x)
        o = out_at(color, yy, xx)
        c2 = rdma(o, o, gs.at[NCOL + 2 * color + 1], gr.at[NCOL + 2 * color + 1], b)
        c2.start()
        g2_.append(c2)
        to_sibling(color, yy, xx, NCOL + color)
    for k in range(2 * NCOL):
        color = k % NCOL
        b = ORDERS[color][1]
        g2_[k].wait_recv()
        if k < NCOL:
            ty, tx = (y, 1 - x) if b == 'x' else (1 - y, x)
        else:
            ty, tx = 1 - y, 1 - x
        to_sibling(color, ty, tx, 2 * NCOL + k)
    for cp in cps:
        cp.wait()
    for cp in dcp + p1 + p2 + p3 + g1_ + g2_:
        cp.wait_send()
    for s in range(nseq):
        xc[s].wait_send()
        there = dx.at[(1 - mi) * nseq + s]
        rdma(there, there, xs_.at[s], xr_.at[s], 'z').wait_recv()


def run_reduce(grad, dx):
    g = grad.reshape(2 * NCOL * 8, BR, GL)
    nb = NCOL * 8
    V = pltpu.VMEM
    S = pltpu.SemaphoreType.DMA
    anyspec = pl.BlockSpec(memory_space=pl.ANY)
    return pl.pallas_call(
        reduce_kernel,
        in_specs=[anyspec, anyspec],
        out_specs=[pl.BlockSpec(memory_space=pltpu.VMEM), anyspec],
        out_shape=[jax.ShapeDtypeStruct((nb, BR, GL), F32), jax.ShapeDtypeStruct(dx.shape, dx.dtype)],
        scratch_shapes=[V((nb, BR, GL), F32), V((nb, BR, GL), F32), V((4 * NCOL, BR, GL), F32), V((2 * NCOL, BR, GL), F32), V((NCOL, BR, GL), F32),
                        S((nb,)), S((nb,)), S((nb,)), S((7 * NCOL,)), S((7 * NCOL,)), S((3 * NCOL,)), S((3 * NCOL,)), S((4 * NCOL,)), S((4 * NCOL,)),
                        S((6,)), S((6,))],
        input_output_aliases={1: 1},
        compiler_params=pltpu.CompilerParams(vmem_limit_bytes=60_000_000, collective_id=1, has_side_effects=True),
    )(g, dx)


def solution(mesh):
    spec_col, spec_row, spec_act, spec_rep = P(None, 'model'), P('model', None), P('data', None, None), P(None, None)

    def device_step(x_in, cot_out, step_emb, w_q, w_k, w_v, w_o, w_1, w_2):
        wqkv, wo, w1, w2 = run_gather((w_q, w_k, w_v, w_o, w_1, w_2))
        dx, grad = run_kernel(x_in, cot_out, step_emb, wqkv, wo, w1, w2)
        g, dx = run_reduce(grad, dx)
        g = g.reshape(GROWS, GL)

        def join(r0, n, k):
            return jnp.concatenate([g[r0 + n * i:r0 + n * (i + 1)] for i in range(k)], axis=1)

        return g[:512], g[512:1024], g[1024:1536], join(5632, 256, 2), join(1536, 512, 4), join(3584, 1024, 2), dx

    return jax.shard_map(device_step, mesh=mesh,
                         in_specs=(spec_act, spec_act, spec_rep, spec_col, spec_col, spec_col, spec_row, spec_col, spec_row),
                         out_specs=(spec_col, spec_col, spec_col, spec_row, spec_col, spec_row, spec_act),
                         check_vma=False)
```

time: 1190 us -> 682 us (0.57)
  waiting for transfers between devices: 454 us -> 0 us
  blocking collectives: 24.5 us -> 0 us
  local copies, waits for them, and re-layouts: 23.5 us -> 8.9 us
  between operations: 13.9 us -> 0.69 us
    reduce_scatter x4 -> x0, waiting for transfers between devices: 241 us -> none  [device_step(): lax.psum_scatter(g, both, scatter_dimension=0, tiled=True)]
    all_gather x7 -> x0, waiting for transfers between devices: 210 us -> none  [the longest x3 71.9 us: device_step(): lax.all_gather(lax.psum_scatter(g, both, scatter_dimension=0, tiled=True)...]
    pallas_call x1, Pallas kernels: 672 us -> 524 us  [run_kernel(): pl.pallas_call(functools.partial(kernel, nseq), grid=(nseq,), in_specs=[b...]
    pallas_call x0 -> x2, Pallas kernels: none -> 143 us  [the longest x1 103 us: run_reduce(): pl.pallas_call(reduce_kernel, in_specs=[anyspec, anyspec], out_specs=[pl....]
    all_gather x2 -> x0, blocking collectives: 24.5 us -> none  [the longest x1 15.3 us: device_step(): gat = lambda w: lax.all_gather(w, both, axis=0, tiled=True)]
  transfers between devices with their start and end apart: 11 -> 0, of which waited for: 11 -> 0; matrix products, arithmetic and copies ran while one was open for 1% -> 0% of each run, Pallas kernels for 0% -> 0%
where the time goes in v2:
time: 682 us; the launch traced here: 681 us
  Pallas kernels  668 us (98%)
  local copies, waits for them, and re-layouts  8.9 us (1%)
    pallas_call x1, Pallas kernels, run_kernel(): pl.pallas_call(functools.partial(kernel, nseq), grid=(nseq,), in_specs=[b...  524 us
    pallas_call x1, Pallas kernels, run_reduce(): pl.pallas_call(reduce_kernel, in_specs=[anyspec, anyspec], out_specs=[pl....  103 us
    pallas_call x1, Pallas kernels, run_gather(): pl.pallas_call(gather_kernel, in_specs=[anyspec] * NW, out_specs=[anyspec...  40.2 us

profile of v2, /device:TPU:0, one launch (start us, length us, event | category | flops | bytes accessed | tf_op | source)
XLA Modules:
  0.0 681.3 jit_solution(3927215388960180102)
XLA Ops:
  0.6 1.8 broadcast_in_dim.2.emb_ref
  2.4 40.2 %shard_map.144 = (bf16[2,512,768]{2,1,0:T(8,128)(2,1)}, bf16[512,512]{1,0:T(8,128)(2,1)}, bf16[2,512,1024]{2,1,0:T(8,128)(2,1)}, bf16[2048,512]{1,0:T(8,128)(2,1)}) custom-call(bf16[512,256]{1,0:T(8,128)(2,1)} %refs_0_.1, bf16[512,256]{1,0:T(8,128)(2,1)} %refs_1_.1, bf16[512,256]{1,0:T(8,128)(2,1)} %refs_2_.1, bf16[256,512]{1,0:T(8,128)(2,1)} %refs_3_.1, ...), custom_call_target="tpu_custom_call" | custom-call | tf_op jit(solution)/shard_map/pallas_call | solution.py:487
  42.7 524.2 %shard_map.145 = (bf16[12,512,512]{2,1,0:T(8,128)(2,1)}, f32[2,6144,256]{2,1,0:T(8,128)}) custom-call(bf16[12,512,512]{2,1,0:T(8,128)(2,1)} %x_ref.1, bf16[12,512,512]{2,1,0:T(8,128)(2,1)} %cot_ref.1, bf16[4,512,128]{2,1,0:T(8,128)(2,1)} %broadcast_in_dim.2.emb_ref, bf16[2,512,768]{2,1,0:T(8,128)(2,1)} %get-tuple-element.15.wqkv_h, ...), custom_call_target="tpu_custom_call" | custom-call | tf_op jit(solution)/shard_map/pallas_call | solution.py:402
  566.9 103.2 %shard_map.146 = (f32[16,384,256]{2,1,0:T(8,128)}, bf16[12,512,512]{2,1,0:T(8,128)(2,1)}) custom-call(f32[32,384,256]{2,1,0:T(8,128)} %bitcast.4, bf16[12,512,512]{2,1,0:T(8,128)(2,1)} %get-tuple-element.20.dx_in), custom_call_target="tpu_custom_call", output_to_operand_aliasing={{1}: (1, {})} | custom-call | tf_op jit(solution)/shard_map/pallas_call | solution.py:648
  670.2 0.0 copy-start
  670.2 1.2 fusion.2
  671.4 0.9 pad_maximum_fusion.2
  672.3 1.8 fusion
  674.0 0.0 copy-done
  674.0 0.0 slice-start
  674.0 1.2 fusion.1
  675.3 0.0 slice-start.1
  675.3 1.6 pad_maximum_fusion
  676.9 1.6 pad_maximum_fusion.1
  678.4 0.0 slice-done
  678.4 0.2 slice-done.1
  678.6 2.7 copy.19
  (1 shorter events, 0.0 us)
Async XLA Ops:
  670.2 3.8 copy-start
  674.0 4.4 slice-start
  675.3 3.3 slice-start.1

commit v3 on v2

--- a/solution.py
+++ b/solution.py
@@ -14,7 +14,7 @@
 SCALE = E ** -0.5
 GK0 = 0.7978845608028654
 GK1 = 0.044715
-R = 16
+R = 8
 LN = 128
 
 
@@ -32,16 +32,12 @@
 
 def wide(e):
     return jnp.concatenate([e] * (T // LN), axis=1)
-
-
-def fold8(v):
-    return v[:8] + v[8:]
 
 
 def col_sum(tile_fn):
     accs = [None, None]
     for i, r in enumerate(range(0, D, R)):
-        v = fold8(tile_fn(r))
+        v = tile_fn(r)
         accs[i % 2] = v if accs[i % 2] is None else accs[i % 2] + v
     return jnp.sum(accs[0] + accs[1], axis=0, keepdims=True)
 
@@ -65,17 +61,14 @@
 
 
 def gelu_fwd(z):
-    t = jnp.tanh(z * (GK0 + (GK0 * GK1) * (z * z)))
-    return (0.5 * z) * (1.0 + t)
+    return z * jax.nn.sigmoid(z * (2 * GK0 + (2 * GK0 * GK1) * (z * z)))
 
 
 def gelu_both(z):
     z2 = z * z
-    t = jnp.tanh(z * (GK0 + (GK0 * GK1) * z2))
-    up = 1.0 + t
-    hz = 0.5 * z
-    w = z * (GK0 + (3.0 * GK0 * GK1) * z2)
-    return hz * up, (0.5 * up) * (1.0 + w * (1.0 - t))
+    s = jax.nn.sigmoid(z * (2 * GK0 + (2 * GK0 * GK1) * z2))
+    w = z * (2 * GK0 + (6 * GK0 * GK1) * z2)
+    return z * s, s * (1.0 + w * (1.0 - s))
 
 
 def qrow(hd):
@@ -85,6 +78,10 @@
 def pad_head(block, hh):
     zero = jnp.zeros_like(block)
     return jnp.concatenate([block, zero] if hh == 0 else [zero, block], axis=0)
+
+
+def zip_pad(a, b):
+    return [(a[i:i + 1], b[i:i + 1]) for i in range(max(len(a), len(b)))]
 
 
 def max_cols(ref, cols):
@@ -100,7 +97,7 @@
 def kernel(nseq, x_ref, cot_ref, emb_ref, wqkv_h, wo_h, w1_h, w2_h,
            dx_ref, grad_h,
            wqkv, wo, w1, w2, wqkvt, wot, w1t, w2t, gqkv, go, g1, g2,
-           xs, qkv, ctx, ctxl, hs, zs, lse, u, m, act, dz, dn, dmid, dctx, dqkv, tmp, sbuf, sem):
+           xs, qkv, ctx, ctxl, hs, zs, lse, rsc, u, m, act, dz, dn, dmid, dctx, dqkv, tmp, sbuf, lcol, dcol, sem):
     step = pl.program_id(0)
     halves = range(2)
     pairs_in = ([(wqkv_h.at[k], wqkv.at[:, pl.ds(768 * k, 768)]) for k in halves] + [(wo_h, wo)]
@@ -127,35 +124,37 @@
     half = [pl.ds(0, 256), pl.ds(256, 256)]
 
     def s_tile(l):
-        return lambda r: xs[l, rows(r), :].astype(F32) + wide(emb_ref[l, rows(r), :].astype(F32))
-
-    def norm_into(dst, tile_fn):
+        return lambda r: xs[l, rows(r), :].astype(F32) + wide(emb_ref[l, rows(r), :])
+
+    def norm_into(dst, tile_fn, l, k, fresh):
         box = {}
 
         def stat():
-            box['r'] = rms_of(tile_fn)
+            if fresh:
+                box['r'] = rms_of(tile_fn)
+                rsc[l, pl.ds(k, 1), :] = box['r']
+            else:
+                box['r'] = rsc[l, pl.ds(k, 1), :]
 
         def put(r):
             dst[rows(r), :] = (tile_fn(r) * box['r']).astype(BF16)
 
         return [stat] + [functools.partial(put, r) for r in range(0, D, R)]
 
-    def pull_into(dst, base, tile_fn, dy):
+    def pull_into(dst, base, tile_fn, dy, l, k):
         box = {}
 
         def stat():
-            box['r'] = rms_of(tile_fn)
-
-        def stat2():
             a = col_sum(lambda r: dy[rows(r), :].astype(F32) * tile_fn(r)) * (1.0 / D)
-            rr = box['r']
+            rr = rsc[l, pl.ds(k, 1), :]
+            box['r'] = rr
             box['a'] = rr * rr * rr * a
 
         def put(r):
             g = dy[rows(r), :].astype(F32)
             dst[rows(r), :] = (base[rows(r), :].astype(F32) + (box['r'] * g - tile_fn(r) * box['a'])).astype(BF16)
 
-        return [stat, stat2] + [functools.partial(put, r) for r in range(0, D, R)]
+        return [stat] + [functools.partial(put, r) for r in range(0, D, R)]
 
     def run(stream):
         for f in stream:
@@ -165,7 +164,7 @@
         return lambda r: hs[l, rows(r), :].astype(F32)
 
     def fwd(l, carry):
-        run(norm_into(u, s_tile(l)))
+        run(norm_into(u, s_tile(l), l, 0, True))
         for j in range(3):
             qkv[l, pl.ds(512 * j, 512), :] = dot_nn(wqkvt[pl.ds(512 * j, 512), :], u[...]).astype(BF16)
 
@@ -214,17 +213,18 @@
 
         run(stage_a(0))
         for hd in range(H + 1):
-            mx = (stage_a(hd + 1) if hd + 1 < H else []) + (stage_c(hd - 1) if hd >= 1 else [])
+            mx = []
+            for x_, y_ in zip_pad(stage_a(hd + 1) if hd + 1 < H else [], stage_c(hd - 1) if hd >= 1 else []):
+                mx += x_ + y_
             va = stage_b(hd) if hd < H else []
             weave(mx, va)
 
-        st = s_tile(l)
         for c in range(2):
             o = dot_nn(wot[...], ctx[l, :, half[c]])
             for r in range(0, D, R):
-                sx = xs[l, rows(r), half[c]].astype(F32) + jnp.concatenate([emb_ref[l, rows(r), :].astype(F32)] * 2, axis=1)
+                sx = xs[l, rows(r), half[c]].astype(F32) + jnp.concatenate([emb_ref[l, rows(r), :]] * 2, axis=1)
                 hs[l, rows(r), half[c]] = (sx + o[r:r + R]).astype(BF16)
-        run(norm_into(m, h_tile(l)))
+        run(norm_into(m, h_tile(l), l, 1, True))
 
         def z_dot(j):
             def f(c):
@@ -233,9 +233,9 @@
             return [lambda: f(0), lambda: f(1)]
 
         def gelu_stream(j):
-            def f(r):
-                act[rows(r), :] = gelu_fwd(zs[l, rows(r), :].astype(F32)).astype(BF16)
-            return [functools.partial(f, r) for r in range(512 * j, 512 * j + 512, R)]
+            def f(r, c):
+                act[rows(r), half[c]] = gelu_fwd(zs[l, rows(r), half[c]].astype(F32)).astype(BF16)
+            return [functools.partial(f, r, c) for r in range(512 * j, 512 * j + 512, R) for c in range(2)]
 
         @pl.when(l < L - 1)
         def _():
@@ -267,11 +267,11 @@
             return [lambda: f(0), lambda: f(1)]
 
         def gelu_stream(j):
-            def f(r):
-                g, gp = gelu_both(zs[l, rows(r), :].astype(F32))
-                act[rows(r), :] = g.astype(BF16)
-                dz[rows(r), :] = (dz[rows(r), :].astype(F32) * gp).astype(BF16)
-            return [functools.partial(f, r) for r in range(512 * j, 512 * j + 512, R)]
+            def f(r, c):
+                g, gp = gelu_both(zs[l, rows(r), half[c]].astype(F32))
+                act[rows(r), half[c]] = g.astype(BF16)
+                dz[rows(r), half[c]] = (dz[rows(r), half[c]].astype(F32) * gp).astype(BF16)
+            return [functools.partial(f, r, c) for r in range(512 * j, 512 * j + 512, R) for c in range(2)]
 
         def wgrad(j):
             js = pl.ds(512 * j, 512)
@@ -284,18 +284,31 @@
                 g1[:, jc] += dot_nt(m[...], dz[jc, :])
             return [lambda: a(0), lambda: a(1), lambda: b(0), lambda: b(1)]
 
-        weave(dg_dot(0), norm_into(m, h_tile(l)))
-        weave(dg_dot(1) + dg_dot(2), gelu_stream(0))
-        weave(wgrad(0) + dg_dot(3), gelu_stream(1))
-        weave(wgrad(1), gelu_stream(2))
+        weave(dg_dot(0), norm_into(m, h_tile(l), l, 1, False))
+        def dm_part(k0, k1, last):
+            def f(c):
+                p = dot_nn(w1[:, 512 * k0:512 * k1], dz[pl.ds(512 * k0, 512 * (k1 - k0)), half[c]])
+                if k0 > 0:
+                    p = sbuf[0, :, half[c]] + p
+                if last:
+                    tmp[:, half[c]] = p.astype(BF16)
+                else:
+                    sbuf[0, :, half[c]] = p
+            return [lambda: f(0), lambda: f(1)]
+
+        weave(dg_dot(1) + dg_dot(2) + dg_dot(3), gelu_stream(0))
+        weave(wgrad(0), gelu_stream(1))
+        weave(wgrad(1) + dm_part(0, 2, False), gelu_stream(2))
         weave(wgrad(2), gelu_stream(3))
-        for c in range(2):
-            tmp[:, half[c]] = dot_nn(w1[...], dz[:, half[c]]).astype(BF16)
-        weave(wgrad(3), pull_into(dmid, dn, h_tile(l), tmp))
+        run(dm_part(2, 4, True))
+        weave(wgrad(3), pull_into(dmid, dn, h_tile(l), tmp, l, 1))
         for c in range(2):
             dctx[:, half[c]] = dot_nn(wo[...], dmid[:, half[c]]).astype(BF16)
 
-        kps, vps, delta = {}, {}, {}
+        qps, dcs = {}, {}
+
+        def column(row):
+            return jnp.broadcast_to(row, (LN, T)).T
 
         def stage_a(hd):
             p, hh = divmod(hd, 2)
@@ -303,35 +316,42 @@
 
             def first():
                 if hh == 0:
-                    kps[p] = qkv[l, pl.ds(qrow(hd) + 256, 128), :].T
-                    vps[p] = qkv[l, pl.ds(qrow(hd) + 512, 128), :].T
+                    qps[p] = qkv[l, pl.ds(qrow(hd), 128), :].T
+                    dcs[p] = dctx[pl.ds(64 * hd, 128), :].T
                 c = ctx[l, hsl, :].astype(F32) + ctxl[l, hsl, :].astype(F32)
-                delta[hd] = jnp.sum(dctx[hsl, :].astype(F32) * c, axis=0, keepdims=True)
+                dcol[hd % 2] = column(jnp.sum(dctx[hsl, :].astype(F32) * c, axis=0, keepdims=True))
+                lcol[hd % 2] = column(lse[l, pl.ds(hd, 1), :])
 
             def s_part(c):
-                qp = pad_head(qkv[l, pl.ds(qrow(hd), 64), half[c]], hh)
-                sbuf[hd % 2, :, half[c]] = dot_nn(kps[p], qp)
+                kp = pad_head(qkv[l, pl.ds(qrow(hd) + 256, 64), half[c]], hh)
+                sbuf[hd % 2, :, half[c]] = dot_nn(qps[p], kp)
 
             def p_part(c):
-                dcp = pad_head(dctx[hsl, half[c]], hh)
-                dz[pl.ds(512 * (hd % 2), 512), half[c]] = dot_nn(vps[p], dcp).astype(BF16)
-
-            return [first, lambda: s_part(0), lambda: s_part(1), lambda: p_part(0), lambda: p_part(1)]
+                vp = pad_head(qkv[l, pl.ds(qrow(hd) + 512, 64), half[c]], hh)
+                dz[pl.ds(512 * (hd % 2), 512), half[c]] = dot_nn(dcs[p], vp).astype(BF16)
+
+            return [first] + [functools.partial(f, c) for f in (s_part, p_part) for c in range(2)]
+
+        def merge(xs_, ys_):
+            out = []
+            for i in range(max(len(xs_), len(ys_))):
+                out += xs_[i:i + 1] + ys_[i:i + 1]
+            return out
 
         def stage_b(hd):
             sl = 512 * (hd % 2)
 
             def group(g, r0):
                 cols = half[g]
-                ls = lse[l, pl.ds(hd, 1), cols]
-                de = delta[hd][:, 256 * g:256 * g + 256]
-                for r in range(r0, r0 + 128, 8):
-                    pr = jnp.exp2(sbuf[hd % 2, rows(r, 8), cols] * CEXP - ls)
+                for r in range(r0, r0 + 64, 8):
+                    lc = lcol[hd % 2, rows(r, 8), :]
+                    dc = dcol[hd % 2, rows(r, 8), :]
+                    pr = jnp.exp2(sbuf[hd % 2, rows(r, 8), cols] * CEXP - jnp.concatenate([lc, lc], axis=1))
                     act[rows(sl + r, 8), cols] = pr.astype(BF16)
                     dp = dz[rows(sl + r, 8), cols].astype(F32)
-                    act[rows(1024 + sl + r, 8), cols] = (pr * (dp - de)).astype(BF16)
-
-            return [functools.partial(group, g, r0) for g in range(2) for r0 in range(0, T, 128)]
+                    act[rows(1024 + sl + r, 8), cols] = (pr * (dp - jnp.concatenate([dc, dc], axis=1))).astype(BF16)
+
+            return [functools.partial(group, g, r0) for r0 in range(0, T, 64) for g in range(2)]
 
         def stage_c(hd):
             sl = 512 * (hd % 2)
@@ -339,35 +359,43 @@
             db = act.at[pl.ds(1024 + sl, 512), :]
             hsl = pl.ds(64 * hd, 64)
 
-            def f_v():
-                dqkv[pl.ds(qrow(hd) + 512, 64), :] = dot_nt(dctx[hsl, :], pb[...]).astype(BF16)
-
-            def f_k():
-                dqkv[pl.ds(qrow(hd) + 256, 64), :] = (dot_nt(qkv[l, pl.ds(qrow(hd), 64), :], db[...]) * SCALE).astype(BF16)
-
-            def f_q():
-                dqkv[pl.ds(qrow(hd), 64), :] = (dot_nn(qkv[l, pl.ds(qrow(hd) + 256, 64), :], db[...]) * SCALE).astype(BF16)
-
-            return [f_v, f_k, f_q]
-
-        def wo_grad():
-            go[...] += dot_nt(ctx[l], dmid[...])
-
-        run(stage_a(0))
-        for hd in range(H + 1):
-            mx = (stage_a(hd + 1) if hd + 1 < H else []) + (stage_c(hd - 1) if hd >= 1 else [wo_grad])
-            va = stage_b(hd) if hd < H else []
-            weave(mx, va)
-
-        for c in range(2):
-            tmp[:, half[c]] = dot_nn(wqkv[...], dqkv[:, half[c]]).astype(BF16)
+            def f_v(c):
+                dqkv[pl.ds(qrow(hd) + 512, 64), half[c]] = dot_nn(dctx[hsl, :], pb[:, half[c]]).astype(BF16)
+
+            def f_k(c):
+                dk = dot_nn(qkv[l, pl.ds(qrow(hd), 64), :], db[:, half[c]]) * SCALE
+                dqkv[pl.ds(qrow(hd) + 256, 64), half[c]] = dk.astype(BF16)
+
+            def f_q(c):
+                dq = dot_nt(qkv[l, pl.ds(qrow(hd) + 256, 64), :], db[half[c], :]) * SCALE
+                dqkv[pl.ds(qrow(hd), 64), half[c]] = dq.astype(BF16)
+
+            return [functools.partial(f, c) for f in (f_v, f_k, f_q) for c in range(2)]
+
+        def wo_grad(c):
+            go[:, half[c]] += dot_nt(ctx[l], dmid[half[c], :])
 
         def qkv_grad(j):
             js = pl.ds(256 * j, 256)
             gqkv[:, js] += dot_nt(u[...], dqkv[js, :])
 
-        run(norm_into(u, s_tile(l)))
-        weave([functools.partial(qkv_grad, j) for j in range(6)], pull_into(dn, dmid, s_tile(l), tmp))
+        wo_parts = [functools.partial(wo_grad, c) for c in range(2)]
+        qkv_parts = [functools.partial(qkv_grad, j) for j in range(6)]
+        u_norm = norm_into(u, s_tile(l), l, 0, False)
+        run(stage_a(0))
+        for hd in range(H + 1):
+            ma = stage_a(hd + 1) if hd + 1 < H else []
+            mc = stage_c(hd - 1) if hd >= 1 else wo_parts
+            if hd == H:
+                ma = qkv_parts[:3]
+            va = stage_b(hd) if hd < H else []
+            if hd == H - 1:
+                va = va + u_norm
+            weave(merge(mc, ma), va)
+
+        for c in range(2):
+            tmp[:, half[c]] = dot_nn(wqkv[...], dqkv[:, half[c]]).astype(BF16)
+        weave(qkv_parts[3:], pull_into(dn, dmid, s_tile(l), tmp, l, 0))
         return carry
 
     lax.fori_loop(0, L, bwd, 0)
@@ -409,9 +437,9 @@
                         V((1536, D), BF16), V((D, D), BF16), V((FF, D), BF16), V((D, FF), BF16),
                         V((D, 1536), F32), V((D, D), F32), V((D, FF), F32), V((FF, D), F32),
                         V((L, D, T), BF16), V((L, 1536, T), BF16), V((L, D, T), BF16), V((L, D, T), BF16), V((L, D, T), BF16),
-                        V((L, FF, T), BF16), V((L, H, T), F32), V((D, T), BF16), V((D, T), BF16), V((FF, T), BF16),
+                        V((L, FF, T), BF16), V((L, H, T), F32), V((L, 2, T), F32), V((D, T), BF16), V((D, T), BF16), V((FF, T), BF16),
                         V((FF, T), BF16), V((D, T), BF16), V((D, T), BF16), V((D, T), BF16), V((1536, T), BF16), V((D, T), BF16),
-                        V((2, T, T), F32), pltpu.SemaphoreType.DMA((22,))],
+                        V((2, T, T), F32), V((2, T, LN), F32), V((2, T, LN), F32), pltpu.SemaphoreType.DMA((22,))],
         compiler_params=pltpu.CompilerParams(dimension_semantics=("arbitrary",), vmem_limit_bytes=67_000_000),
     )(x, cot, embb, wqkv, wo, w1, w2)
 

time: 682 us -> 620 us (0.909)
  Pallas kernels: 668 us -> 606 us
    pallas_call x1, Pallas kernels: 524 us -> 463 us  [run_kernel(): pl.pallas_call(functools.partial(kernel, nseq), grid=(nseq,), in_specs=[b...]
where the time goes in v3:
time: 620 us
  Pallas kernels  606 us (98%)
  local copies, waits for them, and re-layouts  8.9 us (1%)
    pallas_call x1, Pallas kernels, run_kernel(): pl.pallas_call(functools.partial(kernel, nseq), grid=(nseq,), in_specs=[b...  463 us
    pallas_call x1, Pallas kernels, run_reduce(): pl.pallas_call(reduce_kernel, in_specs=[anyspec, anyspec], out_specs=[pl....  103 us
    pallas_call x1, Pallas kernels, run_gather(): pl.pallas_call(gather_kernel, in_specs=[anyspec] * NW, out_specs=[anyspec...  40.2 us

profile of v3, /device:TPU:0, one launch (start us, length us, event | category | flops | bytes accessed | tf_op | source)
XLA Modules:
  0.0 619.9 jit_solution(11330371931629742932)
XLA Ops:
  0.6 1.8 broadcast_in_dim.2.emb_ref
  2.4 40.2 %shard_map.144 = (bf16[2,512,768]{2,1,0:T(8,128)(2,1)}, bf16[512,512]{1,0:T(8,128)(2,1)}, bf16[2,512,1024]{2,1,0:T(8,128)(2,1)}, bf16[2048,512]{1,0:T(8,128)(2,1)}) custom-call(bf16[512,256]{1,0:T(8,128)(2,1)} %refs_0_.1, bf16[512,256]{1,0:T(8,128)(2,1)} %refs_1_.1, bf16[512,256]{1,0:T(8,128)(2,1)} %refs_2_.1, bf16[256,512]{1,0:T(8,128)(2,1)} %refs_3_.1, ...), custom_call_target="tpu_custom_call" | custom-call | tf_op jit(solution)/shard_map/pallas_call | solution.py:515
  42.7 462.8 %shard_map.145 = (bf16[12,512,512]{2,1,0:T(8,128)(2,1)}, f32[2,6144,256]{2,1,0:T(8,128)}) custom-call(bf16[12,512,512]{2,1,0:T(8,128)(2,1)} %x_ref.1, bf16[12,512,512]{2,1,0:T(8,128)(2,1)} %cot_ref.1, bf16[4,512,128]{2,1,0:T(8,128)(2,1)} %broadcast_in_dim.2.emb_ref, bf16[2,512,768]{2,1,0:T(8,128)(2,1)} %get-tuple-element.15.wqkv_h, ...), custom_call_target="tpu_custom_call" | custom-call | tf_op jit(solution)/shard_map/pallas_call | solution.py:430
  505.5 103.2 %shard_map.146 = (f32[16,384,256]{2,1,0:T(8,128)}, bf16[12,512,512]{2,1,0:T(8,128)(2,1)}) custom-call(f32[32,384,256]{2,1,0:T(8,128)} %bitcast.4, bf16[12,512,512]{2,1,0:T(8,128)(2,1)} %get-tuple-element.20.dx_in), custom_call_target="tpu_custom_call", output_to_operand_aliasing={{1}: (1, {})} | custom-call | tf_op jit(solution)/shard_map/pallas_call | solution.py:676
  608.8 0.0 copy-start
  608.8 1.2 fusion.2
  610.0 0.9 pad_maximum_fusion.2
  610.9 1.8 fusion
  612.6 0.0 copy-done
  612.7 0.0 slice-start
  612.7 1.2 fusion.1
  613.9 0.0 slice-start.1
  613.9 1.6 pad_maximum_fusion
  615.5 1.6 pad_maximum_fusion.1
  617.1 0.0 slice-done
  617.1 0.2 slice-done.1
  617.2 2.7 copy.19
  (1 shorter events, 0.0 us)
Async XLA Ops:
  608.8 3.8 copy-start
  612.7 4.4 slice-start
  613.9 3.3 slice-start.1

commit v4 on v3

--- a/solution.py
+++ b/solution.py
@@ -14,7 +14,7 @@
 SCALE = E ** -0.5
 GK0 = 0.7978845608028654
 GK1 = 0.044715
-R = 8
+R = 32
 LN = 128
 
 
@@ -86,29 +86,77 @@
 
 def max_cols(ref, cols):
     accs = [None] * 4
-    for i, r in enumerate(range(0, T, 8)):
-        v = ref[rows(r, 8), cols]
+    for i, r in enumerate(range(0, T, 64)):
+        v = ref[rows(r, 64), cols]
         accs[i % 4] = v if accs[i % 4] is None else jnp.maximum(accs[i % 4], v)
     m = jnp.maximum(jnp.maximum(accs[0], accs[1]), jnp.maximum(accs[2], accs[3]))
     return jnp.max(m, axis=0, keepdims=True)
 
 GL, GROWS = 256, 6144
 
-def kernel(nseq, x_ref, cot_ref, emb_ref, wqkv_h, wo_h, w1_h, w2_h,
-           dx_ref, grad_h,
+
+MESH_ID = pl.DeviceIdType.MESH
+NW = 6
+
+
+def other(i):
+    return 1 - i
+
+
+def kernel(nseq, x_ref, cot_ref, emb_ref, wq_h, wk_h, wv_h, wo_h, w1_h, w2_h,
+           dx_h, grad_h,
            wqkv, wo, w1, w2, wqkvt, wot, w1t, w2t, gqkv, go, g1, g2,
-           xs, qkv, ctx, ctxl, hs, zs, lse, rsc, u, m, act, dz, dn, dmid, dctx, dqkv, tmp, sbuf, lcol, dcol, sem):
+           xs, qkv, ctx, ctxl, hs, zs, lse, rsc, u, m, act, dz, dn, dmid, dctx, dqkv, tmp, sbuf, lcol, dcol, dxs,
+           sem, zsend, zrecv, csend, crecv, xloc, xsend, xrecv):
     step = pl.program_id(0)
-    halves = range(2)
-    pairs_in = ([(wqkv_h.at[k], wqkv.at[:, pl.ds(768 * k, 768)]) for k in halves] + [(wo_h, wo)]
-                + [(w1_h.at[k], w1.at[:, pl.ds(1024 * k, 1024)]) for k in halves] + [(w2_h, w2)])
+    mi = lax.axis_index('model')
+    di = lax.axis_index('data')
+    core = di % 2
+    zdev = {'model': 1 - mi, 'data': di}
+    cdev = {'model': mi, 'data': di + 1 - 2 * core}
+
+    def place(k, m, r0, n):
+        if k < 3:
+            return wqkv.at[pl.ds(r0, n), pl.ds(768 * m + 256 * k, 256)]
+        if k == 3:
+            return wo.at[pl.ds(256 * m + r0, n), :]
+        if k == 4:
+            return w1.at[pl.ds(r0, n), pl.ds(1024 * m, 1024)]
+        return w2.at[pl.ds(1024 * m + r0, n), :]
+
+    w_hbm = (wq_h, wk_h, wv_h, wo_h, w1_h, w2_h)
+    w_rows = (512, 512, 512, 256, 512, 1024)
+
+    def load_weights():
+        barrier = pltpu.get_barrier_semaphore()
+        for dev in (zdev, cdev):
+            pl.semaphore_signal(barrier, inc=1, device_id=dev, device_id_type=MESH_ID)
+        pl.semaphore_wait(barrier, 2)
+        local, zs_, cs_ = [], [], []
+        for k in range(NW):
+            n = w_rows[k] // 2
+            zs_.append(pltpu.make_async_remote_copy(
+                w_hbm[k].at[pl.ds(n * core, n), :], place(k, mi, n * core, n),
+                zsend.at[k], zrecv.at[k], device_id=zdev, device_id_type=MESH_ID))
+            zs_[-1].start()
+        for k in range(NW):
+            local.append(pltpu.make_async_copy(w_hbm[k], place(k, mi, 0, w_rows[k]), sem.at[k]))
+            local[-1].start()
+        for k in range(NW):
+            n = w_rows[k] // 2
+            zs_[k].wait_recv()
+            mine = place(k, 1 - mi, n * core, n)
+            cs_.append(pltpu.make_async_remote_copy(
+                mine, mine, csend.at[k], crecv.at[k], device_id=cdev, device_id_type=MESH_ID))
+            cs_[-1].start()
+        for k in range(NW):
+            local[k].wait()
+            zs_[k].wait_send()
+            cs_[k].wait()
+
     @pl.when(step == 0)
     def _():
-        cps = [pltpu.make_async_copy(s, d, sem.at[i]) for i, (s, d) in enumerate(pairs_in)]
-        for c in cps:
-            c.start()
-        for c in cps:
-            c.wait()
+        load_weights()
         for j in range(3):
             wqkvt[pl.ds(512 * j, 512), :] = wqkv[:, pl.ds(512 * j, 512)].T
         wot[...] = wo[...].T
@@ -191,10 +239,10 @@
                 cols = half[g]
                 mx = max_cols(sref, cols) * CEXP
                 accs = [None, None]
-                for i, r in enumerate(range(0, T, 8)):
-                    e = jnp.exp2(sref[rows(r, 8), cols] * CEXP - mx)
+                for i, r in enumerate(range(0, T, 64)):
+                    e = jnp.exp2(sref[rows(r, 64), cols] * CEXP - mx)
                     accs[i % 2] = e if accs[i % 2] is None else accs[i % 2] + e
-                    eref[rows(r, 8), cols] = e.astype(BF16)
+                    eref[rows(r, 64), cols] = e.astype(BF16)
                 sm = jnp.sum(accs[0] + accs[1], axis=0, keepdims=True)
                 lse[l, pl.ds(hd, 1), cols] = mx + jnp.log2(sm)
                 inv[hd, g] = 1.0 / sm
@@ -234,8 +282,8 @@
 
         def gelu_stream(j):
             def f(r, c):
-                act[rows(r), half[c]] = gelu_fwd(zs[l, rows(r), half[c]].astype(F32)).astype(BF16)
-            return [functools.partial(f, r, c) for r in range(512 * j, 512 * j + 512, R) for c in range(2)]
+                act[rows(r, 64), half[c]] = gelu_fwd(zs[l, rows(r, 64), half[c]].astype(F32)).astype(BF16)
+            return [functools.partial(f, r, c) for r in range(512 * j, 512 * j + 512, 64) for c in range(2)]
 
         @pl.when(l < L - 1)
         def _():
@@ -268,10 +316,10 @@
 
         def gelu_stream(j):
             def f(r, c):
-                g, gp = gelu_both(zs[l, rows(r), half[c]].astype(F32))
-                act[rows(r), half[c]] = g.astype(BF16)
-                dz[rows(r), half[c]] = (dz[rows(r), half[c]].astype(F32) * gp).astype(BF16)
-            return [functools.partial(f, r, c) for r in range(512 * j, 512 * j + 512, R) for c in range(2)]
+                g, gp = gelu_both(zs[l, rows(r, 64), half[c]].astype(F32))
+                act[rows(r, 64), half[c]] = g.astype(BF16)
+                dz[rows(r, 64), half[c]] = (dz[rows(r, 64), half[c]].astype(F32) * gp).astype(BF16)
+            return [functools.partial(f, r, c) for r in range(512 * j, 512 * j + 512, 64) for c in range(2)]
 
         def wgrad(j):
             js = pl.ds(512 * j, 512)
@@ -343,13 +391,13 @@
 
             def group(g, r0):
                 cols = half[g]
-                for r in range(r0, r0 + 64, 8):
-                    lc = lcol[hd % 2, rows(r, 8), :]
-                    dc = dcol[hd % 2, rows(r, 8), :]
-                    pr = jnp.exp2(sbuf[hd % 2, rows(r, 8), cols] * CEXP - jnp.concatenate([lc, lc], axis=1))
-                    act[rows(sl + r, 8), cols] = pr.astype(BF16)
-                    dp = dz[rows(sl + r, 8), cols].astype(F32)
-                    act[rows(1024 + sl + r, 8), cols] = (pr * (dp - jnp.concatenate([dc, dc], axis=1))).astype(BF16)
+                for r in range(r0, r0 + 64, 64):
+                    lc = lcol[hd % 2, rows(r, 64), :]
+                    dc = dcol[hd % 2, rows(r, 64), :]
+                    pr = jnp.exp2(sbuf[hd % 2, rows(r, 64), cols] * CEXP - jnp.concatenate([lc, lc], axis=1))
+                    act[rows(sl + r, 64), cols] = pr.astype(BF16)
+                    dp = dz[rows(sl + r, 64), cols].astype(F32)
+                    act[rows(1024 + sl + r, 64), cols] = (pr * (dp - jnp.concatenate([dc, dc], axis=1))).astype(BF16)
 
             return [functools.partial(group, g, r0) for r0 in range(0, T, 64) for g in range(2)]
 
@@ -399,7 +447,26 @@
         return carry
 
     lax.fori_loop(0, L, bwd, 0)
-    dx_ref[0] = dn[...].T
+    slot = step % 2
+
+    def dx_copies(s, at):
+        here = dx_h.at[mi * nseq + s]
+        loc = pltpu.make_async_copy(dxs.at[at], here, xloc.at[at])
+        rem = pltpu.make_async_remote_copy(dxs.at[at], here, xsend.at[at], xrecv.at[s], device_id=zdev, device_id_type=MESH_ID)
+        return loc, rem
+
+    def dx_drain(s, at):
+        loc, rem = dx_copies(s, at)
+        loc.wait()
+        rem.wait_send()
+
+    @pl.when(step >= 2)
+    def _():
+        dx_drain(step - 2, slot)
+
+    dxs[slot] = dn[...].T
+    for c in dx_copies(step, slot):
+        c.start()
 
     @pl.when(step == nseq - 1)
     def _():
@@ -417,21 +484,27 @@
         cps = [pltpu.make_async_copy(s, d, sem.at[i]) for i, (s, d) in enumerate(cps)]
         for c in cps:
             c.start()
+        dx_drain(nseq - 2, (nseq - 2) % 2)
+        dx_drain(nseq - 1, (nseq - 1) % 2)
+        for s in range(nseq):
+            theirs = dx_h.at[(1 - mi) * nseq + s]
+            pltpu.make_async_remote_copy(dxs.at[s % 2], theirs, xsend.at[s % 2], xrecv.at[s],
+                                         device_id=zdev, device_id_type=MESH_ID).wait_recv()
         for c in cps:
             c.wait()
 
 
-def run_kernel(x, cot, emb, wqkv, wo, w1, w2):
-    nseq = x.shape[0] // 2
-    embb = jnp.broadcast_to(emb[:, :, None], (L, D, LN))
+def run_kernel(x, cot, emb, ws, nseq):
+    embb = jnp.broadcast_to(emb.astype(F32)[:, :, None], (L, D, LN))
     blk = pl.BlockSpec((1, T, D), lambda i: (lax.axis_index('model') * nseq + i, 0, 0))
     anyspec = pl.BlockSpec(memory_space=pl.ANY)
     V = pltpu.VMEM
+    S = pltpu.SemaphoreType.DMA
     return pl.pallas_call(
         functools.partial(kernel, nseq),
         grid=(nseq,),
-        in_specs=[blk, blk, pl.BlockSpec(memory_space=pltpu.VMEM)] + [anyspec] * 4,
-        out_specs=[blk, anyspec],
+        in_specs=[blk, blk, pl.BlockSpec(memory_space=pltpu.VMEM)] + [anyspec] * NW,
+        out_specs=[anyspec] * 2,
         out_shape=[jax.ShapeDtypeStruct((2 * nseq, T, D), BF16), jax.ShapeDtypeStruct((2, GROWS, GL), F32)],
         scratch_shapes=[V((D, 1536), BF16), V((D, D), BF16), V((D, FF), BF16), V((FF, D), BF16),
                         V((1536, D), BF16), V((D, D), BF16), V((FF, D), BF16), V((D, FF), BF16),
@@ -439,128 +512,54 @@
                         V((L, D, T), BF16), V((L, 1536, T), BF16), V((L, D, T), BF16), V((L, D, T), BF16), V((L, D, T), BF16),
                         V((L, FF, T), BF16), V((L, H, T), F32), V((L, 2, T), F32), V((D, T), BF16), V((D, T), BF16), V((FF, T), BF16),
                         V((FF, T), BF16), V((D, T), BF16), V((D, T), BF16), V((D, T), BF16), V((1536, T), BF16), V((D, T), BF16),
-                        V((2, T, T), F32), V((2, T, LN), F32), V((2, T, LN), F32), pltpu.SemaphoreType.DMA((22,))],
-        compiler_params=pltpu.CompilerParams(dimension_semantics=("arbitrary",), vmem_limit_bytes=67_000_000),
-    )(x, cot, embb, wqkv, wo, w1, w2)
-
-
-MESH_ID = pl.DeviceIdType.MESH
-NCOL = 2
-BR, GL = 384, 256
+                        V((2, T, T), F32), V((2, T, LN), F32), V((2, T, LN), F32), V((2, T, D), BF16),
+                        S((22,)), S((NW,)), S((NW,)), S((NW,)), S((NW,)), S((2,)), S((2,)), S((nseq,))],
+        compiler_params=pltpu.CompilerParams(dimension_semantics=("arbitrary",), vmem_limit_bytes=67_000_000,
+                                             collective_id=0, has_side_effects=True),
+    )(x, cot, embb, *ws)
+
+
+NCOL = 3
+BR = 256
 GROWS = NCOL * 8 * BR
-ORDERS = ('xyz', 'yxz')
-NW = 6
-
-
-def neighbours():
+ORDERS = ('xyz', 'yzx', 'zxy')
+SPREAD = ((0, 0, BR, 'xy'), (1, 0, BR, 'yx'), (2, 0, BR // 2, 'xy'), (2, BR // 2, BR // 2, 'yx'))
+
+
+def reduce_kernel(g_h, out, acc, rd, r1, r2, r3, locsem, ds, dr, ps, pr, gs, gr, cs, cr):
     mi = lax.axis_index('model')
     di = lax.axis_index('data')
     core, x, y = di % 2, (di // 2) % 2, di // 4
+    me = {'x': x, 'y': y, 'z': mi}
     dev = {'x': {'model': mi, 'data': di + 2 - 4 * x}, 'y': {'model': mi, 'data': di + 4 - 8 * y},
            'z': {'model': 1 - mi, 'data': di}, 'c': {'model': mi, 'data': di + 1 - 2 * core}}
-    return {'x': x, 'y': y, 'z': mi}, core, dev
-
-
-def greet(dev, names):
-    barrier = pltpu.get_barrier_semaphore()
-    for d in names:
-        pl.semaphore_signal(barrier, inc=1, device_id=dev[d], device_id_type=MESH_ID)
-    pl.semaphore_wait(barrier, len(names))
-
-
-def gather_kernel(*refs):
-    w_in, (wqkv, wo, w1, w2), (stage, lsem, ssem, zsend, zrecv, csend, crecv) = refs[:NW], refs[NW:NW + 4], refs[NW + 4:]
-    me, core, dev = neighbours()
-    mi = me['z']
-    greet(dev, 'zc')
-
-    def place(k, m, r0, n):
-        if k < 3:
-            return wqkv.at[m, pl.ds(r0, n), pl.ds(256 * k, 256)]
-        if k == 3:
-            return wo.at[pl.ds(256 * m + r0, n), :]
-        if k == 4:
-            return w1.at[m, pl.ds(r0, n), :]
-        return w2.at[pl.ds(1024 * m + r0, n), :]
-
-    n_rows = (512, 512, 512, 256, 512, 1024)
-    zc, cc, loc, put = [], [], [], []
-    for k in range(NW):
-        n = n_rows[k] // 2
-        zc.append(pltpu.make_async_remote_copy(w_in[k].at[pl.ds(n * core, n), :], place(k, mi, n * core, n), zsend.at[k], zrecv.at[k],
-                                               device_id=dev['z'], device_id_type=MESH_ID))
-        zc[k].start()
-    for k in range(NW):
-        loc.append(pltpu.make_async_copy(w_in[k], stage.at[k, pl.ds(0, n_rows[k]), pl.ds(0, w_in[k].shape[1])], lsem.at[k]))
-        loc[k].start()
-    for k in range(NW):
-        loc[k].wait()
-        put.append(pltpu.make_async_copy(stage.at[k, pl.ds(0, n_rows[k]), pl.ds(0, w_in[k].shape[1])], place(k, mi, 0, n_rows[k]), ssem.at[k]))
-        put[k].start()
-    for k in range(NW):
-        n = n_rows[k] // 2
-        zc[k].wait_recv()
-        got = place(k, 1 - mi, n * core, n)
-        cc.append(pltpu.make_async_remote_copy(got, got, csend.at[k], crecv.at[k], device_id=dev['c'], device_id_type=MESH_ID))
-        cc[k].start()
-    for k in range(NW):
-        put[k].wait()
-        zc[k].wait_send()
-        cc[k].wait()
-
-
-def run_gather(ws):
-    anyspec = pl.BlockSpec(memory_space=pl.ANY)
-    S = pltpu.SemaphoreType.DMA
-    return pl.pallas_call(
-        gather_kernel,
-        in_specs=[anyspec] * NW,
-        out_specs=[anyspec] * 4,
-        out_shape=[jax.ShapeDtypeStruct((2, D, 768), BF16), jax.ShapeDtypeStruct((D, D), BF16),
-                   jax.ShapeDtypeStruct((2, D, 1024), BF16), jax.ShapeDtypeStruct((FF, D), BF16)],
-        scratch_shapes=[pltpu.VMEM((NW, 1024, 1024), BF16)] + [S((NW,))] * 6,
-        compiler_params=pltpu.CompilerParams(vmem_limit_bytes=60_000_000, collective_id=0, has_side_effects=True),
-    )(*ws)
-
-
-def reduce_kernel(g_h, dx_in, out, dx, acc, rd, r1, r2, r3, locsem, ds, dr, ps, pr, gs, gr, cs, cr, xs_, xr_):
-    me, core, dev = neighbours()
-    x, y, mi = me['x'], me['y'], me['z']
-    nseq = dx.shape[0] // 2
 
     def rdma(src, dst, s, r, d):
         return pltpu.make_async_remote_copy(src, dst, s, r, device_id=dev[d], device_id_type=MESH_ID)
 
-    greet(dev, 'xyzc')
-
-    xc = []
-    for s in range(nseq):
-        here = dx.at[mi * nseq + s]
-        xc.append(rdma(here, here, xs_.at[s], xr_.at[s], 'z'))
-
-    def blk(color, pos):
+    barrier = pltpu.get_barrier_semaphore()
+    for d in 'xyzc':
+        pl.semaphore_signal(barrier, inc=1, device_id=dev[d], device_id_type=MESH_ID)
+    pl.semaphore_wait(barrier, 4)
+
+    def blk(color, far):
+        pos = {ax: (1 - me[ax] if ax in far else me[ax]) for ax in 'xyz'}
         return (pos['z'] * NCOL + color) * 4 + pos['y'] * 2 + pos['x']
-
-    def all_pos(fixed):
-        out_ = [dict(fixed)]
-        for ax in 'zyx':
-            if ax not in fixed:
-                out_ = [dict(p, **{ax: v}) for p in out_ for v in (0, 1)]
-        return out_
 
     def add(dst, src):
         def body(i, c):
-            r = pl.multiple_of(i * 32, 32)
-            acc[dst, pl.ds(r, 32), :] += src[pl.ds(r, 32), :]
+            r = pl.multiple_of(i * 64, 64)
+            acc[dst, pl.ds(r, 64), :] += src[pl.ds(r, 64), :]
             return c
-        lax.fori_loop(0, BR // 32, body, 0)
-
-    first, rest = [], []
-    for color in range(NCOL):
-        a = ORDERS[color][0]
-        first += [blk(color, p) for p in all_pos({a: 1 - me[a]})]
-        rest += [blk(color, p) for p in all_pos({a: me[a]})]
-    seq = first + rest
+        lax.fori_loop(0, BR // 64, body, 0)
+
+    def places(color):
+        a, b, c = ORDERS[color]
+        keep = [b + c, b, c, '']
+        return [a + k for k in keep], keep
+
+    seq = ([blk(color, places(color)[0][j]) for j in range(4) for color in range(NCOL)]
+           + [blk(color, places(color)[1][j]) for j in range(4) for color in range(NCOL)])
     nb = len(seq)
     dcp, lcp = [], []
     for i, b in enumerate(seq):
@@ -569,131 +568,120 @@
     for i in range(nb):
         dcp[i].start()
         lcp[i].start()
-    for s in range(4):
-        xc[s].start()
 
     def fold_core(i):
         dcp[i].wait_recv()
         lcp[i].wait()
         add(seq[i], rd.at[seq[i]])
 
-    p1, p2, p3 = [], [], []
+    p1, p2, p3 = {}, {}, {}
     for j in range(4):
         for color in range(NCOL):
-            a = ORDERS[color][0]
-            i = 4 * color + j
+            i = j * NCOL + color
             fold_core(i)
-            cp = rdma(acc.at[blk(color, all_pos({a: 1 - me[a]})[j])], r1.at[i], ps.at[i], pr.at[i], a)
-            cp.start()
-            p1.append(cp)
-    p1 = [p1[(i % 4) * NCOL + i // 4] for i in range(4 * NCOL)]
-    for i in range(4 * NCOL, nb):
-        fold_core(i)
+            p1[j, color] = rdma(acc.at[seq[i]], r1.at[i], ps.at[i], pr.at[i], ORDERS[color][0])
+            p1[j, color].start()
+    base2, base3 = 4 * NCOL, 6 * NCOL
+
+    def fold_kept(j, color):
+        i = j * NCOL + color
+        fold_core(4 * NCOL + i)
+        p1[j, color].wait_recv()
+        add(seq[4 * NCOL + i], r1.at[i])
+        return seq[4 * NCOL + i]
+
+    for j in range(2):
+        for color in range(NCOL):
+            b = fold_kept(j, color)
+            i = j * NCOL + color
+            p2[j, color] = rdma(acc.at[b], r2.at[i], ps.at[base2 + i], pr.at[base2 + i], ORDERS[color][1])
+            p2[j, color].start()
     for color in range(NCOL):
-        a, b = ORDERS[color][0], ORDERS[color][1]
-        for j, p in enumerate(all_pos({a: me[a]})):
-            p1[4 * color + j].wait_recv()
-            add(blk(color, p), r1.at[4 * color + j])
-        for j, p in enumerate(all_pos({a: me[a], b: 1 - me[b]})):
-            i = 2 * color + j
-            cp = rdma(acc.at[blk(color, p)], r2.at[i], ps.at[4 * NCOL + i], pr.at[4 * NCOL + i], b)
-            cp.start()
-            p2.append(cp)
+        b = fold_kept(2, color)
+        p2[0, color].wait_recv()
+        add(b, r2.at[color])
+        p3[color] = rdma(acc.at[b], r3.at[color], ps.at[base3 + color], pr.at[base3 + color], ORDERS[color][2])
+        p3[color].start()
+    last = {}
     for color in range(NCOL):
-        a, b, c = ORDERS[color]
-        for j, p in enumerate(all_pos({a: me[a], b: me[b]})):
-            p2[2 * color + j].wait_recv()
-            add(blk(color, p), r2.at[2 * color + j])
-        cp = rdma(acc.at[blk(color, dict(me, **{c: 1 - me[c]}))], r3.at[color], ps.at[6 * NCOL + color], pr.at[6 * NCOL + color], c)
-        cp.start()
-        p3.append(cp)
-    for s in range(4, nseq):
-        xc[s].start()
-
-    cps, g1_, g2_ = [], [], []
-
-    def out_at(color, yy, xx):
-        return out.at[(color * 4 + yy * 2 + xx) * 2 + core]
-
-    def to_sibling(color, yy, xx, i):
-        o = out_at(color, yy, xx)
+        last[color] = fold_kept(3, color)
+        p2[1, color].wait_recv()
+        add(last[color], r2.at[NCOL + color])
+
+    def out_at(color, far, r0, n):
+        yy = 1 - y if 'y' in far else y
+        xx = 1 - x if 'x' in far else x
+        return out.at[(color * 4 + yy * 2 + xx) * 2 + core, pl.ds(r0, n), :]
+
+    ns_ = len(SPREAD)
+    cps, g1, g2, g3 = [], {}, {}, {}
+
+    def to_sibling(k, far, i):
+        color, r0, n, _ = SPREAD[k]
+        o = out_at(color, far, r0, n)
         cp = rdma(o, o, cs.at[i], cr.at[i], 'c')
         cp.start()
         cps.append(cp)
 
     for color in range(NCOL):
         p3[color].wait_recv()
-        b = blk(color, me)
+        b = last[color]
         o_blk = (color * 4 + y * 2 + x) * 2 + core
 
         def body(i, c, b=b, o_blk=o_blk, color=color):
-            r = pl.multiple_of(i * 32, 32)
-            out[o_blk, pl.ds(r, 32), :] = acc[b, pl.ds(r, 32), :] + r3[color, pl.ds(r, 32), :]
+            r = pl.multiple_of(i * 64, 64)
+            out[o_blk, pl.ds(r, 64), :] = acc[b, pl.ds(r, 64), :] + r3[color, pl.ds(r, 64), :]
             return c
-        lax.fori_loop(0, BR // 32, body, 0)
-        o = out_at(color, y, x)
-        cp = rdma(o, o, gs.at[color], gr.at[color], ORDERS[color][0])
-        cp.start()
-        g1_.append(cp)
-        c2 = rdma(o, o, gs.at[NCOL + 2 * color], gr.at[NCOL + 2 * color], ORDERS[color][1])
-        c2.start()
-        g2_.append(c2)
-        to_sibling(color, y, x, color)
-    for color in range(NCOL):
-        g1_[color].wait_recv()
-        a, b = ORDERS[color][0], ORDERS[color][1]
-        yy, xx = (y, 1 - x) if a == 'x' else (1 - y, x)
-        o = out_at(color, yy, xx)
-        c2 = rdma(o, o, gs.at[NCOL + 2 * color + 1], gr.at[NCOL + 2 * color + 1], b)
-        c2.start()
-        g2_.append(c2)
-        to_sibling(color, yy, xx, NCOL + color)
-    for k in range(2 * NCOL):
-        color = k % NCOL
-        b = ORDERS[color][1]
-        g2_[k].wait_recv()
-        if k < NCOL:
-            ty, tx = (y, 1 - x) if b == 'x' else (1 - y, x)
-        else:
-            ty, tx = 1 - y, 1 - x
-        to_sibling(color, ty, tx, 2 * NCOL + k)
+        lax.fori_loop(0, BR // 64, body, 0)
+        for k, (col, r0, n, ab) in enumerate(SPREAD):
+            if col != color:
+                continue
+            o = out_at(color, '', r0, n)
+            g1[k] = rdma(o, o, gs.at[k], gr.at[k], ab[0])
+            g2[k] = rdma(o, o, gs.at[ns_ + k], gr.at[ns_ + k], ab[1])
+            g1[k].start()
+            g2[k].start()
+    for k in range(ns_):
+        to_sibling(k, '', k)
+    for k, (color, r0, n, ab) in enumerate(SPREAD):
+        g1[k].wait_recv()
+        o = out_at(color, ab[0], r0, n)
+        g3[k] = rdma(o, o, gs.at[2 * ns_ + k], gr.at[2 * ns_ + k], ab[1])
+        g3[k].start()
+        to_sibling(k, ab[0], ns_ + k)
+    for k, (color, r0, n, ab) in enumerate(SPREAD):
+        g2[k].wait_recv()
+        to_sibling(k, ab[1], 2 * ns_ + k)
+    for k, (color, r0, n, ab) in enumerate(SPREAD):
+        g3[k].wait_recv()
+        to_sibling(k, 'xy', 3 * ns_ + k)
     for cp in cps:
         cp.wait()
-    for cp in dcp + p1 + p2 + p3 + g1_ + g2_:
+    for cp in dcp + list(p1.values()) + list(p2.values()) + list(p3.values()) + list(g1.values()) + list(g2.values()) + list(g3.values()):
         cp.wait_send()
-    for s in range(nseq):
-        xc[s].wait_send()
-        there = dx.at[(1 - mi) * nseq + s]
-        rdma(there, there, xs_.at[s], xr_.at[s], 'z').wait_recv()
-
-
-def run_reduce(grad, dx):
-    g = grad.reshape(2 * NCOL * 8, BR, GL)
+
+
+def run_reduce(grad):
     nb = NCOL * 8
     V = pltpu.VMEM
     S = pltpu.SemaphoreType.DMA
-    anyspec = pl.BlockSpec(memory_space=pl.ANY)
     return pl.pallas_call(
         reduce_kernel,
-        in_specs=[anyspec, anyspec],
-        out_specs=[pl.BlockSpec(memory_space=pltpu.VMEM), anyspec],
-        out_shape=[jax.ShapeDtypeStruct((nb, BR, GL), F32), jax.ShapeDtypeStruct(dx.shape, dx.dtype)],
+        in_specs=[pl.BlockSpec(memory_space=pl.ANY)],
+        out_specs=pl.BlockSpec(memory_space=pltpu.VMEM),
+        out_shape=jax.ShapeDtypeStruct((nb, BR, GL), F32),
         scratch_shapes=[V((nb, BR, GL), F32), V((nb, BR, GL), F32), V((4 * NCOL, BR, GL), F32), V((2 * NCOL, BR, GL), F32), V((NCOL, BR, GL), F32),
-                        S((nb,)), S((nb,)), S((nb,)), S((7 * NCOL,)), S((7 * NCOL,)), S((3 * NCOL,)), S((3 * NCOL,)), S((4 * NCOL,)), S((4 * NCOL,)),
-                        S((6,)), S((6,))],
-        input_output_aliases={1: 1},
+                        S((nb,)), S((nb,)), S((nb,)), S((7 * NCOL,)), S((7 * NCOL,)), S((12,)), S((12,)), S((16,)), S((16,))],
         compiler_params=pltpu.CompilerParams(vmem_limit_bytes=60_000_000, collective_id=1, has_side_effects=True),
-    )(g, dx)
+    )(grad.reshape(2 * nb, BR, GL))
 
 
 def solution(mesh):
     spec_col, spec_row, spec_act, spec_rep = P(None, 'model'), P('model', None), P('data', None, None), P(None, None)
 
     def device_step(x_in, cot_out, step_emb, w_q, w_k, w_v, w_o, w_1, w_2):
-        wqkv, wo, w1, w2 = run_gather((w_q, w_k, w_v, w_o, w_1, w_2))
-        dx, grad = run_kernel(x_in, cot_out, step_emb, wqkv, wo, w1, w2)
-        g, dx = run_reduce(grad, dx)
-        g = g.reshape(GROWS, GL)
+        dx, grad = run_kernel(x_in, cot_out, step_emb, (w_q, w_k, w_v, w_o, w_1, w_2), x_in.shape[0] // 2)
+        g = run_reduce(grad).reshape(GROWS, GL)
 
         def join(r0, n, k):
             return jnp.concatenate([g[r0 + n * i:r0 + n * (i + 1)] for i in range(k)], axis=1)

time: 620 us -> 603 us (0.973)
  Pallas kernels: 606 us -> 589 us
    pallas_call x2 -> x1, Pallas kernels: 143 us -> 77.7 us  [run_reduce(): pl.pallas_call(reduce_kernel, in_specs=[pl.BlockSpec(memory_space=pl.ANY)...]
    pallas_call x1, Pallas kernels: 463 us -> 511 us  [run_kernel(): pl.pallas_call(functools.partial(kernel, nseq), grid=(nseq,), in_specs=[b...]
where the time goes in v4:
time: 603 us; the launch traced here: 602 us
  Pallas kernels  589 us (98%)
  local copies, waits for them, and re-layouts  9.12 us (2%)
    pallas_call x1, Pallas kernels, run_kernel(): pl.pallas_call(functools.partial(kernel, nseq), grid=(nseq,), in_specs=[b...  511 us
    pallas_call x1, Pallas kernels, run_reduce(): pl.pallas_call(reduce_kernel, in_specs=[pl.BlockSpec(memory_space=pl.ANY)...  77.7 us

profile of v4, /device:TPU:0, one launch (start us, length us, event | category | flops | bytes accessed | tf_op | source)
XLA Modules:
  0.0 602.4 jit_solution(10962782453024903237)
XLA Ops:
  0.6 2.0 broadcast_in_dim.2.emb_ref
  2.6 510.9 %shard_map.144 = (bf16[12,512,512]{2,1,0:T(8,128)(2,1)}, f32[2,6144,256]{2,1,0:T(8,128)}) custom-call(bf16[12,512,512]{2,1,0:T(8,128)(2,1)} %x_ref.1, bf16[12,512,512]{2,1,0:T(8,128)(2,1)} %cot_ref.1, f32[4,512,128]{2,1,0:T(8,128)} %broadcast_in_dim.2.emb_ref, bf16[512,256]{1,0:T(8,128)(2,1)} %wq_h.1, bf16[512,256]{1,0:T(8,128)(2,1)} %wk_h.1, ...), custom_call_target="tpu_custom_call" | custom-call | tf_op jit(solution)/shard_map/pallas_call | solution.py:503
  513.5 77.7 %shard_map.145 = f32[24,256,256]{2,1,0:T(8,128)} custom-call(f32[48,256,256]{2,1,0:T(8,128)} %bitcast.14), custom_call_target="tpu_custom_call" | custom-call | tf_op jit(solution)/shard_map/pallas_call | solution.py:668
  591.2 0.0 copy-start
  591.3 1.2 slice_bitcast_fusion.1
  592.5 0.9 pad_maximum_fusion.2
  593.3 1.8 fusion
  595.1 0.0 copy-done
  595.1 0.0 slice-start
  595.1 1.2 fusion.1
  596.3 0.0 slice-start.1
  596.3 1.6 pad_maximum_fusion
  597.9 1.6 pad_maximum_fusion.1
  599.5 0.0 slice-done
  599.5 0.2 slice-done.1
  599.7 2.7 copy.17
  (1 shorter events, 0.0 us)
Async XLA Ops:
  591.2 3.8 copy-start
  595.1 4.4 slice-start
  596.3 3.4 slice-start.1

commit v5 on v4

--- a/solution.py
+++ b/solution.py
@@ -107,7 +107,7 @@
            dx_h, grad_h,
            wqkv, wo, w1, w2, wqkvt, wot, w1t, w2t, gqkv, go, g1, g2,
            xs, qkv, ctx, ctxl, hs, zs, lse, rsc, u, m, act, dz, dn, dmid, dctx, dqkv, tmp, sbuf, lcol, dcol, dxs,
-           sem, zsend, zrecv, csend, crecv, xloc, xsend, xrecv):
+           embv, sem, zsend, zrecv, gsend, grecv, xloc, xsend, xrecv):
     step = pl.program_id(0)
     mi = lax.axis_index('model')
     di = lax.axis_index('data')
@@ -124,39 +124,94 @@
             return w1.at[pl.ds(r0, n), pl.ds(1024 * m, 1024)]
         return w2.at[pl.ds(1024 * m + r0, n), :]
 
+    xx, yy = (di // 2) % 2, di // 4
+    dev = {'x': {'model': mi, 'data': di + 2 - 4 * xx}, 'y': {'model': mi, 'data': di + 4 - 8 * yy}, 'z': zdev, 'c': cdev}
+
     w_hbm = (wq_h, wk_h, wv_h, wo_h, w1_h, w2_h)
     w_rows = (512, 512, 512, 256, 512, 1024)
+    groups = ((0, 1, 2), (3,), (4,), (5,))
+
+    def region(g, far, color):
+        k = groups[g][0]
+        pr = w_rows[k] // 8
+        py = 1 - yy if 'y' in far else yy
+        px = 1 - xx if 'x' in far else xx
+        r0, n = (py * 4 + px * 2 + core) * pr, pr
+        if color is not None:
+            r0, n = r0 + color * (pr // 2), pr // 2
+        if g == 0:
+            return wqkv.at[pl.ds(r0, n), pl.ds(768 * (1 - mi), 768)]
+        return place(k, 1 - mi, r0, n)
 
     def load_weights():
         barrier = pltpu.get_barrier_semaphore()
-        for dev in (zdev, cdev):
-            pl.semaphore_signal(barrier, inc=1, device_id=dev, device_id_type=MESH_ID)
-        pl.semaphore_wait(barrier, 2)
-        local, zs_, cs_ = [], [], []
+        for d in 'xyzc':
+            pl.semaphore_signal(barrier, inc=1, device_id=dev[d], device_id_type=MESH_ID)
+        pl.semaphore_wait(barrier, 4)
+        zc, local, plane, sib = {}, [], {}, []
+
+        def hand(g, far, color, d, i):
+            o = region(g, far, color)
+            cp = pltpu.make_async_remote_copy(o, o, gsend.at[g, i], grecv.at[g, i], device_id=dev[d], device_id_type=MESH_ID)
+            cp.start()
+            return cp
+
         for k in range(NW):
-            n = w_rows[k] // 2
-            zs_.append(pltpu.make_async_remote_copy(
-                w_hbm[k].at[pl.ds(n * core, n), :], place(k, mi, n * core, n),
-                zsend.at[k], zrecv.at[k], device_id=zdev, device_id_type=MESH_ID))
-            zs_[-1].start()
+            pr = w_rows[k] // 8
+            zc[k] = pltpu.make_async_remote_copy(w_hbm[k].at[pl.ds(di * pr, pr), :], place(k, mi, di * pr, pr),
+                                                 zsend.at[k], zrecv.at[k], device_id=zdev, device_id_type=MESH_ID)
+            zc[k].start()
         for k in range(NW):
             local.append(pltpu.make_async_copy(w_hbm[k], place(k, mi, 0, w_rows[k]), sem.at[k]))
             local[-1].start()
-        for k in range(NW):
-            n = w_rows[k] // 2
-            zs_[k].wait_recv()
-            mine = place(k, 1 - mi, n * core, n)
-            cs_.append(pltpu.make_async_remote_copy(
-                mine, mine, csend.at[k], crecv.at[k], device_id=cdev, device_id_type=MESH_ID))
-            cs_[-1].start()
+
+        def own(g):
+            for k in groups[g]:
+                zc[k].wait_recv()
+            for color, ab in enumerate(('xy', 'yx')):
+                plane[g, color, 0] = hand(g, '', color, ab[0], 3 * color)
+                plane[g, color, 1] = hand(g, '', color, ab[1], 3 * color + 1)
+            sib.append(hand(g, '', None, 'c', 6))
+
+        def forward(g):
+            for color, ab in enumerate(('xy', 'yx')):
+                plane[g, color, 0].wait_recv()
+                plane[g, color, 2] = hand(g, ab[0], color, ab[1], 3 * color + 2)
+                sib.append(hand(g, ab[0], color, 'c', 7 + 3 * color))
+
+        def finish(g):
+            for color, ab in enumerate(('xy', 'yx')):
+                plane[g, color, 1].wait_recv()
+                sib.append(hand(g, ab[1], color, 'c', 8 + 3 * color))
+            for color in range(2):
+                plane[g, color, 2].wait_recv()
+                sib.append(hand(g, 'xy', color, 'c', 9 + 3 * color))
+
+        own(0)
+        own(1)
+        own(2)
+        forward(0)
+        forward(1)
+        own(3)
+        forward(2)
+        finish(0)
+        finish(1)
+        forward(3)
+        finish(2)
+        finish(3)
         for k in range(NW):
             local[k].wait()
-            zs_[k].wait_send()
-            cs_[k].wait()
+            zc[k].wait_send()
+        for cp in plane.values():
+            cp.wait_send()
+        for cp in sib:
+            cp.wait()
 
     @pl.when(step == 0)
     def _():
         load_weights()
+        for l_ in range(L):
+            embv[l_] = jnp.broadcast_to(emb_ref[l_:l_ + 1, :].astype(F32), (LN, D)).T
         for j in range(3):
             wqkvt[pl.ds(512 * j, 512), :] = wqkv[:, pl.ds(512 * j, 512)].T
         wot[...] = wo[...].T
@@ -172,7 +227,7 @@
     half = [pl.ds(0, 256), pl.ds(256, 256)]
 
     def s_tile(l):
-        return lambda r: xs[l, rows(r), :].astype(F32) + wide(emb_ref[l, rows(r), :])
+        return lambda r: xs[l, rows(r), :].astype(F32) + wide(embv[l, rows(r), :])
 
     def norm_into(dst, tile_fn, l, k, fresh):
         box = {}
@@ -270,7 +325,7 @@
         for c in range(2):
             o = dot_nn(wot[...], ctx[l, :, half[c]])
             for r in range(0, D, R):
-                sx = xs[l, rows(r), half[c]].astype(F32) + jnp.concatenate([emb_ref[l, rows(r), :]] * 2, axis=1)
+                sx = xs[l, rows(r), half[c]].astype(F32) + jnp.concatenate([embv[l, rows(r), :]] * 2, axis=1)
                 hs[l, rows(r), half[c]] = (sx + o[r:r + R]).astype(BF16)
         run(norm_into(m, h_tile(l), l, 1, True))
 
@@ -465,8 +520,11 @@
         dx_drain(step - 2, slot)
 
     dxs[slot] = dn[...].T
-    for c in dx_copies(step, slot):
-        c.start()
+    dx_copies(step, slot)[0].start()
+
+    @pl.when(step < nseq - 1)
+    def _():
+        dx_copies(step, slot)[1].start()
 
     @pl.when(step == nseq - 1)
     def _():
@@ -485,8 +543,8 @@
         for c in cps:
             c.start()
         dx_drain(nseq - 2, (nseq - 2) % 2)
-        dx_drain(nseq - 1, (nseq - 1) % 2)
-        for s in range(nseq):
+        dx_copies(nseq - 1, (nseq - 1) % 2)[0].wait()
+        for s in range(nseq - 1):
             theirs = dx_h.at[(1 - mi) * nseq + s]
             pltpu.make_async_remote_copy(dxs.at[s % 2], theirs, xsend.at[s % 2], xrecv.at[s],
                                          device_id=zdev, device_id_type=MESH_ID).wait_recv()
@@ -495,7 +553,6 @@
 
 
 def run_kernel(x, cot, emb, ws, nseq):
-    embb = jnp.broadcast_to(emb.astype(F32)[:, :, None], (L, D, LN))
     blk = pl.BlockSpec((1, T, D), lambda i: (lax.axis_index('model') * nseq + i, 0, 0))
     anyspec = pl.BlockSpec(memory_space=pl.ANY)
     V = pltpu.VMEM
@@ -513,10 +570,10 @@
                         V((L, FF, T), BF16), V((L, H, T), F32), V((L, 2, T), F32), V((D, T), BF16), V((D, T), BF16), V((FF, T), BF16),
                         V((FF, T), BF16), V((D, T), BF16), V((D, T), BF16), V((D, T), BF16), V((1536, T), BF16), V((D, T), BF16),
                         V((2, T, T), F32), V((2, T, LN), F32), V((2, T, LN), F32), V((2, T, D), BF16),
-                        S((22,)), S((NW,)), S((NW,)), S((NW,)), S((NW,)), S((2,)), S((2,)), S((nseq,))],
+                        V((L, D, LN), F32), S((22,)), S((NW,)), S((NW,)), S((4, 13)), S((4, 13)), S((2,)), S((2,)), S((nseq,))],
         compiler_params=pltpu.CompilerParams(dimension_semantics=("arbitrary",), vmem_limit_bytes=67_000_000,
                                              collective_id=0, has_side_effects=True),
-    )(x, cot, embb, *ws)
+    )(x, cot, emb, *ws)
 
 
 NCOL = 3
@@ -526,7 +583,7 @@
 SPREAD = ((0, 0, BR, 'xy'), (1, 0, BR, 'yx'), (2, 0, BR // 2, 'xy'), (2, BR // 2, BR // 2, 'yx'))
 
 
-def reduce_kernel(g_h, out, acc, rd, r1, r2, r3, locsem, ds, dr, ps, pr, gs, gr, cs, cr):
+def reduce_kernel(g_h, dx_in, out, dx, acc, rd, r1, r2, r3, locsem, ds, dr, ps, pr, gs, gr, cs, cr, xs_, xr_):
     mi = lax.axis_index('model')
     di = lax.axis_index('data')
     core, x, y = di % 2, (di // 2) % 2, di // 4
@@ -602,6 +659,10 @@
         add(b, r2.at[color])
         p3[color] = rdma(acc.at[b], r3.at[color], ps.at[base3 + color], pr.at[base3 + color], ORDERS[color][2])
         p3[color].start()
+    nseq = dx.shape[0] // 2
+    mine, theirs = dx.at[mi * nseq + nseq - 1], dx.at[(1 - mi) * nseq + nseq - 1]
+    dx_out = rdma(mine, mine, xs_.at[0], xr_.at[0], 'z')
+    dx_out.start()
     last = {}
     for color in range(NCOL):
         last[color] = fold_kept(3, color)
@@ -657,23 +718,26 @@
         to_sibling(k, 'xy', 3 * ns_ + k)
     for cp in cps:
         cp.wait()
+    dx_out.wait_send()
+    rdma(theirs, theirs, xs_.at[0], xr_.at[0], 'z').wait_recv()
     for cp in dcp + list(p1.values()) + list(p2.values()) + list(p3.values()) + list(g1.values()) + list(g2.values()) + list(g3.values()):
         cp.wait_send()
 
 
-def run_reduce(grad):
+def run_reduce(grad, dx):
     nb = NCOL * 8
     V = pltpu.VMEM
     S = pltpu.SemaphoreType.DMA
     return pl.pallas_call(
         reduce_kernel,
-        in_specs=[pl.BlockSpec(memory_space=pl.ANY)],
-        out_specs=pl.BlockSpec(memory_space=pltpu.VMEM),
-        out_shape=jax.ShapeDtypeStruct((nb, BR, GL), F32),
+        in_specs=[pl.BlockSpec(memory_space=pl.ANY)] * 2,
+        out_specs=[pl.BlockSpec(memory_space=pltpu.VMEM), pl.BlockSpec(memory_space=pl.ANY)],
+        out_shape=[jax.ShapeDtypeStruct((nb, BR, GL), F32), jax.ShapeDtypeStruct(dx.shape, dx.dtype)],
         scratch_shapes=[V((nb, BR, GL), F32), V((nb, BR, GL), F32), V((4 * NCOL, BR, GL), F32), V((2 * NCOL, BR, GL), F32), V((NCOL, BR, GL), F32),
-                        S((nb,)), S((nb,)), S((nb,)), S((7 * NCOL,)), S((7 * NCOL,)), S((12,)), S((12,)), S((16,)), S((16,))],
+                        S((nb,)), S((nb,)), S((nb,)), S((7 * NCOL,)), S((7 * NCOL,)), S((12,)), S((12,)), S((16,)), S((16,)), S((1,)), S((1,))],
+        input_output_aliases={1: 1},
         compiler_params=pltpu.CompilerParams(vmem_limit_bytes=60_000_000, collective_id=1, has_side_effects=True),
-    )(grad.reshape(2 * nb, BR, GL))
+    )(grad.reshape(2 * nb, BR, GL), dx)
 
 
 def solution(mesh):
@@ -681,7 +745,8 @@
 
     def device_step(x_in, cot_out, step_emb, w_q, w_k, w_v, w_o, w_1, w_2):
         dx, grad = run_kernel(x_in, cot_out, step_emb, (w_q, w_k, w_v, w_o, w_1, w_2), x_in.shape[0] // 2)
-        g = run_reduce(grad).reshape(GROWS, GL)
+        g, dx = run_reduce(grad, dx)
+        g = g.reshape(GROWS, GL)
 
         def join(r0, n, k):
             return jnp.concatenate([g[r0 + n * i:r0 + n * (i + 1)] for i in range(k)], axis=1)

time: 603 us -> 577 us (0.957)
  Pallas kernels: 589 us -> 565 us
    pallas_call x1, Pallas kernels: 511 us -> 488 us  [run_kernel(): pl.pallas_call(functools.partial(kernel, nseq), grid=(nseq,), in_specs=[b...]
where the time goes in v5:
time: 577 us
  Pallas kernels  565 us (98%)
  local copies, waits for them, and re-layouts  7.13 us (1%)
    pallas_call x1, Pallas kernels, run_kernel(): pl.pallas_call(functools.partial(kernel, nseq), grid=(nseq,), in_specs=[b...  488 us
    pallas_call x1, Pallas kernels, run_reduce(): pl.pallas_call(reduce_kernel, in_specs=[pl.BlockSpec(memory_space=pl.ANY)...  77.4 us

profile of v5, /device:TPU:0, one launch (start us, length us, event | category | flops | bytes accessed | tf_op | source)
XLA Modules:
  0.0 576.9 jit_solution(4769507833000681075)
XLA Ops:
  0.6 487.7 %shard_map.144 = (bf16[12,512,512]{2,1,0:T(8,128)(2,1)}, f32[2,6144,256]{2,1,0:T(8,128)}) custom-call(bf16[12,512,512]{2,1,0:T(8,128)(2,1)} %x_ref.1, bf16[12,512,512]{2,1,0:T(8,128)(2,1)} %cot_ref.1, bf16[4,512]{1,0:T(4,128)(2,1)} %emb_ref.1, bf16[512,256]{1,0:T(8,128)(2,1)} %wq_h.1, bf16[512,256]{1,0:T(8,128)(2,1)} %wk_h.1, bf16[512,256]{1,0:T(8,128)(2,1)} %wv_h.1, ...), custom_call_target="tpu_custom_call" | custom-call | tf_op jit(solution)/shard_map/pallas_call | solution.py:560
  488.3 77.4 %shard_map.145 = (f32[24,256,256]{2,1,0:T(8,128)}, bf16[12,512,512]{2,1,0:T(8,128)(2,1)}) custom-call(f32[48,256,256]{2,1,0:T(8,128)} %bitcast.16, bf16[12,512,512]{2,1,0:T(8,128)(2,1)} %get-tuple-element.12.dx_in), custom_call_target="tpu_custom_call", output_to_operand_aliasing={{1}: (1, {})} | custom-call | tf_op jit(solution)/shard_map/pallas_call | solution.py:731
  565.7 0.0 copy-start
  565.7 1.2 slice_bitcast_fusion.1
  566.9 0.9 pad_maximum_fusion.2
  567.8 1.8 fusion
  569.5 0.0 copy-done
  569.6 0.0 slice-start
  569.6 1.2 fusion.1
  570.8 0.0 slice-start.1
  570.8 1.6 pad_maximum_fusion
  572.4 1.6 pad_maximum_fusion.1
  573.9 0.0 slice-done
  573.9 0.2 slice-done.1
  574.2 2.7 copy.19
  (1 shorter events, 0.0 us)
Async XLA Ops:
  565.7 3.8 copy-start
  569.6 4.4 slice-start
  570.8 3.4 slice-start.1

commit v6 on v5

--- a/solution.py
+++ b/solution.py
@@ -226,48 +226,54 @@
     xs[0] = x_ref[0].T
     half = [pl.ds(0, 256), pl.ds(256, 256)]
 
-    def s_tile(l):
-        return lambda r: xs[l, rows(r), :].astype(F32) + wide(embv[l, rows(r), :])
-
-    def norm_into(dst, tile_fn, l, k, fresh):
+    def s_tile(l, cols=slice(None)):
+        w = 4 if cols == slice(None) else 2
+        return lambda r: xs[l, rows(r), cols].astype(F32) + jnp.concatenate([embv[l, rows(r), :]] * w, axis=1)
+
+    def norm_into(dst, tile_fn, l, k, fresh, cols=slice(None)):
         box = {}
 
         def stat():
             if fresh:
                 box['r'] = rms_of(tile_fn)
-                rsc[l, pl.ds(k, 1), :] = box['r']
+                rsc[l, pl.ds(k, 1), cols] = box['r']
             else:
-                box['r'] = rsc[l, pl.ds(k, 1), :]
+                box['r'] = rsc[l, pl.ds(k, 1), cols]
 
         def put(r):
-            dst[rows(r), :] = (tile_fn(r) * box['r']).astype(BF16)
+            dst[rows(r), cols] = (tile_fn(r) * box['r']).astype(BF16)
 
         return [stat] + [functools.partial(put, r) for r in range(0, D, R)]
 
-    def pull_into(dst, base, tile_fn, dy, l, k):
-        box = {}
-
-        def stat():
-            a = col_sum(lambda r: dy[rows(r), :].astype(F32) * tile_fn(r)) * (1.0 / D)
-            rr = rsc[l, pl.ds(k, 1), :]
-            box['r'] = rr
-            box['a'] = rr * rr * rr * a
-
-        def put(r):
-            g = dy[rows(r), :].astype(F32)
-            dst[rows(r), :] = (base[rows(r), :].astype(F32) + (box['r'] * g - tile_fn(r) * box['a'])).astype(BF16)
-
-        return [stat] + [functools.partial(put, r) for r in range(0, D, R)]
+    def pull_into(dst, base, tile_of, dy, l, k):
+        out = []
+        for cols in half:
+            tile_fn = tile_of(l, cols)
+            box = {}
+
+            def stat(cols=cols, tile_fn=tile_fn, box=box):
+                a = col_sum(lambda r: dy[rows(r), cols].astype(F32) * tile_fn(r)) * (1.0 / D)
+                rr = rsc[l, pl.ds(k, 1), cols]
+                box['r'] = rr
+                box['a'] = rr * rr * rr * a
+
+            def put(r, cols=cols, tile_fn=tile_fn, box=box):
+                g = dy[rows(r), cols].astype(F32)
+                dst[rows(r), cols] = (base[rows(r), cols].astype(F32) + (box['r'] * g - tile_fn(r) * box['a'])).astype(BF16)
+
+            out += [stat] + [functools.partial(put, r) for r in range(0, D, R)]
+        return out
 
     def run(stream):
         for f in stream:
             f()
 
-    def h_tile(l):
-        return lambda r: hs[l, rows(r), :].astype(F32)
+    def h_tile(l, cols=slice(None)):
+        return lambda r: hs[l, rows(r), cols].astype(F32)
 
     def fwd(l, carry):
-        run(norm_into(u, s_tile(l), l, 0, True))
+        for c in range(2):
+            run(norm_into(u, s_tile(l, half[c]), l, 0, True, half[c]))
         for j in range(3):
             qkv[l, pl.ds(512 * j, 512), :] = dot_nn(wqkvt[pl.ds(512 * j, 512), :], u[...]).astype(BF16)
 
@@ -327,7 +333,8 @@
             for r in range(0, D, R):
                 sx = xs[l, rows(r), half[c]].astype(F32) + jnp.concatenate([embv[l, rows(r), :]] * 2, axis=1)
                 hs[l, rows(r), half[c]] = (sx + o[r:r + R]).astype(BF16)
-        run(norm_into(m, h_tile(l), l, 1, True))
+        for c in range(2):
+            run(norm_into(m, h_tile(l, half[c]), l, 1, True, half[c]))
 
         def z_dot(j):
             def f(c):
@@ -387,7 +394,7 @@
                 g1[:, jc] += dot_nt(m[...], dz[jc, :])
             return [lambda: a(0), lambda: a(1), lambda: b(0), lambda: b(1)]
 
-        weave(dg_dot(0), norm_into(m, h_tile(l), l, 1, False))
+        weave(dg_dot(0), norm_into(m, h_tile(l, half[0]), l, 1, False, half[0]) + norm_into(m, h_tile(l, half[1]), l, 1, False, half[1]))
         def dm_part(k0, k1, last):
             def f(c):
                 p = dot_nn(w1[:, 512 * k0:512 * k1], dz[pl.ds(512 * k0, 512 * (k1 - k0)), half[c]])
@@ -404,7 +411,7 @@
         weave(wgrad(1) + dm_part(0, 2, False), gelu_stream(2))
         weave(wgrad(2), gelu_stream(3))
         run(dm_part(2, 4, True))
-        weave(wgrad(3), pull_into(dmid, dn, h_tile(l), tmp, l, 1))
+        weave(wgrad(3), pull_into(dmid, dn, h_tile, tmp, l, 1))
         for c in range(2):
             dctx[:, half[c]] = dot_nn(wo[...], dmid[:, half[c]]).astype(BF16)
 
@@ -484,7 +491,7 @@
 
         wo_parts = [functools.partial(wo_grad, c) for c in range(2)]
         qkv_parts = [functools.partial(qkv_grad, j) for j in range(6)]
-        u_norm = norm_into(u, s_tile(l), l, 0, False)
+        u_norm = sum([norm_into(u, s_tile(l, cc), l, 0, False, cc) for cc in half], [])
         run(stage_a(0))
         for hd in range(H + 1):
             ma = stage_a(hd + 1) if hd + 1 < H else []
@@ -498,7 +505,7 @@
 
         for c in range(2):
             tmp[:, half[c]] = dot_nn(wqkv[...], dqkv[:, half[c]]).astype(BF16)
-        weave(qkv_parts[3:], pull_into(dn, dmid, s_tile(l), tmp, l, 0))
+        weave(qkv_parts[3:], pull_into(dn, dmid, s_tile, tmp, l, 0))
         return carry
 
     lax.fori_loop(0, L, bwd, 0)
@@ -740,18 +747,47 @@
     )(grad.reshape(2 * nb, BR, GL), dx)
 
 
+def place_kernel(g, o_q, o_k, o_v, o_o, o_1, o_2, sem):
+    cps = []
+
+    def move(b, dst):
+        cps.append(pltpu.make_async_copy(g.at[b], dst, sem.at[b]))
+        cps[-1].start()
+
+    for j, o in enumerate((o_q, o_k, o_v)):
+        for i in range(2):
+            move(2 * j + i, o.at[pl.ds(256 * i, 256), :])
+    for k in range(4):
+        for i in range(2):
+            move(6 + 2 * k + i, o_1.at[pl.ds(256 * i, 256), pl.ds(256 * k, 256)])
+    for k in range(2):
+        for i in range(4):
+            move(14 + 4 * k + i, o_2.at[pl.ds(256 * i, 256), pl.ds(256 * k, 256)])
+    for k in range(2):
+        move(22 + k, o_o.at[:, pl.ds(256 * k, 256)])
+    for c in cps:
+        c.wait()
+
+
+def run_place(g):
+    shapes = [(512, 256)] * 3 + [(256, 512), (512, 1024), (1024, 512)]
+    return pl.pallas_call(
+        place_kernel,
+        in_specs=[pl.BlockSpec(memory_space=pltpu.VMEM)],
+        out_specs=[pl.BlockSpec(memory_space=pl.ANY)] * 6,
+        out_shape=[jax.ShapeDtypeStruct(s, F32) for s in shapes],
+        scratch_shapes=[pltpu.SemaphoreType.DMA((24,))],
+        compiler_params=pltpu.CompilerParams(vmem_limit_bytes=20_000_000),
+    )(g)
+
+
 def solution(mesh):
     spec_col, spec_row, spec_act, spec_rep = P(None, 'model'), P('model', None), P('data', None, None), P(None, None)
 
     def device_step(x_in, cot_out, step_emb, w_q, w_k, w_v, w_o, w_1, w_2):
         dx, grad = run_kernel(x_in, cot_out, step_emb, (w_q, w_k, w_v, w_o, w_1, w_2), x_in.shape[0] // 2)
         g, dx = run_reduce(grad, dx)
-        g = g.reshape(GROWS, GL)
-
-        def join(r0, n, k):
-            return jnp.concatenate([g[r0 + n * i:r0 + n * (i + 1)] for i in range(k)], axis=1)
-
-        return g[:512], g[512:1024], g[1024:1536], join(5632, 256, 2), join(1536, 512, 4), join(3584, 1024, 2), dx
+        return (*run_place(g), dx)
 
     return jax.shard_map(device_step, mesh=mesh,
                          in_specs=(spec_act, spec_act, spec_rep, spec_col, spec_col, spec_col, spec_row, spec_col, spec_row),

time: 577 us -> 573 us (level)
  no operation moved by 1% of the time
where the time goes in v6:
time: 573 us; the launch traced here: 572 us
  Pallas kernels  565 us (99%)
  local copies, waits for them, and re-layouts  7.13 us (1%)
    pallas_call x1, Pallas kernels, run_kernel(): pl.pallas_call(functools.partial(kernel, nseq), grid=(nseq,), in_specs=[b...  484 us
    pallas_call x1, Pallas kernels, run_reduce(): pl.pallas_call(reduce_kernel, in_specs=[pl.BlockSpec(memory_space=pl.ANY)...  77.4 us

profile of v6, /device:TPU:0, one launch (start us, length us, event | category | flops | bytes accessed | tf_op | source)
XLA Modules:
  0.0 572.4 jit_solution(9698194164983582483)
XLA Ops:
  0.6 483.9 %shard_map.144 = (bf16[12,512,512]{2,1,0:T(8,128)(2,1)}, f32[2,6144,256]{2,1,0:T(8,128)}) custom-call(bf16[12,512,512]{2,1,0:T(8,128)(2,1)} %x_ref.1, bf16[12,512,512]{2,1,0:T(8,128)(2,1)} %cot_ref.1, bf16[4,512]{1,0:T(4,128)(2,1)} %emb_ref.1, bf16[512,256]{1,0:T(8,128)(2,1)} %wq_h.1, bf16[512,256]{1,0:T(8,128)(2,1)} %wk_h.1, bf16[512,256]{1,0:T(8,128)(2,1)} %wv_h.1, ...), custom_call_target="tpu_custom_call" | custom-call | tf_op jit(solution)/shard_map/pallas_call | solution.py:567
  484.6 77.4 %shard_map.145 = (f32[24,256,256]{2,1,0:T(8,128)}, bf16[12,512,512]{2,1,0:T(8,128)(2,1)}) custom-call(f32[48,256,256]{2,1,0:T(8,128)} %bitcast.1, bf16[12,512,512]{2,1,0:T(8,128)(2,1)} %get-tuple-element.18.dx_in), custom_call_target="tpu_custom_call", output_to_operand_aliasing={{1}: (1, {})} | custom-call | tf_op jit(solution)/shard_map/pallas_call | solution.py:738
  561.9 0.0 copy-start
  561.9 2.8 copy-done
  564.7 0.0 copy-start.1
  564.7 3.3 shard_map.146
  568.1 1.6 copy-done.1
  569.7 2.7 copy.19
Async XLA Ops:
  561.9 2.8 copy-start
  564.7 5.0 copy-start.1

commit v7 on v6

--- a/solution.py
+++ b/solution.py
@@ -92,7 +92,7 @@
     m = jnp.maximum(jnp.maximum(accs[0], accs[1]), jnp.maximum(accs[2], accs[3]))
     return jnp.max(m, axis=0, keepdims=True)
 
-GL, GROWS = 256, 6144
+GL, PR1, PR2 = 256, 512, 256
 
 
 MESH_ID = pl.DeviceIdType.MESH
@@ -104,10 +104,10 @@
 
 
 def kernel(nseq, x_ref, cot_ref, emb_ref, wq_h, wk_h, wv_h, wo_h, w1_h, w2_h,
-           dx_h, grad_h,
-           wqkv, wo, w1, w2, wqkvt, wot, w1t, w2t, gqkv, go, g1, g2,
+           dx_h, grad_h, u_h, dmid_h, ctx_h, dqkv_h,
+           wqkv, wo, w1, w2, wqkvt, wot, w1t, w2t, g1, g2,
            xs, qkv, ctx, ctxl, hs, zs, lse, rsc, u, m, act, dz, dn, dmid, dctx, dqkv, tmp, sbuf, lcol, dcol, dxs,
-           embv, sem, zsend, zrecv, gsend, grecv, xloc, xsend, xrecv):
+           embv, ssem, sem, zsend, zrecv, gsend, grecv, xloc, xsend, xrecv):
     step = pl.program_id(0)
     mi = lax.axis_index('model')
     di = lax.axis_index('data')
@@ -218,10 +218,24 @@
         for j in range(4):
             w1t[pl.ds(512 * j, 512), :] = w1[:, pl.ds(512 * j, 512)].T
             w2t[:, pl.ds(512 * j, 512)] = w2[pl.ds(512 * j, 512), :].T
-        gqkv[...] = jnp.zeros_like(gqkv)
-        go[...] = jnp.zeros_like(go)
         g1[...] = jnp.zeros_like(g1)
         g2[...] = jnp.zeros_like(g2)
+
+    def stash(k, names):
+        pairs = dict(ctx=(ctx.at[k % L], ctx_h), u=(u, u_h), dmid=(dmid, dmid_h), dqkv=(dqkv, dqkv_h))
+        return [pltpu.make_async_copy(pairs[n][0], pairs[n][1].at[k], ssem.at[list(pairs).index(n)]) for n in names]
+
+    def start_all(cs):
+        for c in cs:
+            c.start()
+
+    def wait_all(cs):
+        for c in cs:
+            c.wait()
+
+    @pl.when(step == 0)
+    def _():
+        start_all(stash(L - 1, ('u', 'dmid', 'dqkv')))
 
     xs[0] = x_ref[0].T
     half = [pl.ds(0, 256), pl.ds(256, 256)]
@@ -273,9 +287,9 @@
 
     def fwd(l, carry):
         for c in range(2):
-            run(norm_into(u, s_tile(l, half[c]), l, 0, True, half[c]))
+            run(norm_into(tmp, s_tile(l, half[c]), l, 0, True, half[c]))
         for j in range(3):
-            qkv[l, pl.ds(512 * j, 512), :] = dot_nn(wqkvt[pl.ds(512 * j, 512), :], u[...]).astype(BF16)
+            qkv[l, pl.ds(512 * j, 512), :] = dot_nn(wqkvt[pl.ds(512 * j, 512), :], tmp[...]).astype(BF16)
 
         kps = {}
         inv = {}
@@ -369,6 +383,8 @@
 
     def bwd(i, carry):
         l = L - 1 - i
+        k = step * L + l
+        start_all(stash(k, ('ctx',)))
 
         def dg_dot(j):
             def f(c):
@@ -411,6 +427,7 @@
         weave(wgrad(1) + dm_part(0, 2, False), gelu_stream(2))
         weave(wgrad(2), gelu_stream(3))
         run(dm_part(2, 4, True))
+        wait_all(stash(k, ('ctx', 'u', 'dmid', 'dqkv')))
         weave(wgrad(3), pull_into(dmid, dn, h_tile, tmp, l, 1))
         for c in range(2):
             dctx[:, half[c]] = dot_nn(wo[...], dmid[:, half[c]]).astype(BF16)
@@ -482,22 +499,11 @@
 
             return [functools.partial(f, c) for f in (f_v, f_k, f_q) for c in range(2)]
 
-        def wo_grad(c):
-            go[:, half[c]] += dot_nt(ctx[l], dmid[half[c], :])
-
-        def qkv_grad(j):
-            js = pl.ds(256 * j, 256)
-            gqkv[:, js] += dot_nt(u[...], dqkv[js, :])
-
-        wo_parts = [functools.partial(wo_grad, c) for c in range(2)]
-        qkv_parts = [functools.partial(qkv_grad, j) for j in range(6)]
         u_norm = sum([norm_into(u, s_tile(l, cc), l, 0, False, cc) for cc in half], [])
         run(stage_a(0))
         for hd in range(H + 1):
             ma = stage_a(hd + 1) if hd + 1 < H else []
-            mc = stage_c(hd - 1) if hd >= 1 else wo_parts
-            if hd == H:
-                ma = qkv_parts[:3]
+            mc = stage_c(hd - 1) if hd >= 1 else []
             va = stage_b(hd) if hd < H else []
             if hd == H - 1:
                 va = va + u_norm
@@ -505,7 +511,8 @@
 
         for c in range(2):
             tmp[:, half[c]] = dot_nn(wqkv[...], dqkv[:, half[c]]).astype(BF16)
-        weave(qkv_parts[3:], pull_into(dn, dmid, s_tile, tmp, l, 0))
+        weave([], pull_into(dn, dmid, s_tile, tmp, l, 0))
+        start_all(stash(k, ('u', 'dmid', 'dqkv')))
         return carry
 
     lax.fori_loop(0, L, bwd, 0)
@@ -535,17 +542,12 @@
 
     @pl.when(step == nseq - 1)
     def _():
+        wait_all(stash(0, ('u', 'dmid', 'dqkv')))
         cps = []
         for m_ in range(2):
-            g = grad_h.at[m_]
-            for k in range(3):
-                cps.append((gqkv.at[:, pl.ds(768 * m_ + 256 * k, 256)], g.at[pl.ds(512 * k, 512), :]))
             for k in range(4):
-                cps.append((g1.at[:, pl.ds(1024 * m_ + 256 * k, 256)], g.at[pl.ds(1536 + 512 * k, 512), :]))
-            for k in range(2):
-                cps.append((g2.at[pl.ds(1024 * m_, 1024), pl.ds(256 * k, 256)], g.at[pl.ds(3584 + 1024 * k, 1024), :]))
-            for k in range(2):
-                cps.append((go.at[pl.ds(256 * m_, 256), pl.ds(256 * k, 256)], g.at[pl.ds(5632 + 256 * k, 256), :]))
+                cps.append((g1.at[:, pl.ds(1024 * m_ + 256 * k, 256)], grad_h.at[m_, k]))
+                cps.append((g2.at[pl.ds(1024 * m_ + 512 * (k % 2), 512), pl.ds(256 * (k // 2), 256)], grad_h.at[m_, 4 + k]))
         cps = [pltpu.make_async_copy(s, d, sem.at[i]) for i, (s, d) in enumerate(cps)]
         for c in cps:
             c.start()
@@ -568,29 +570,204 @@
         functools.partial(kernel, nseq),
         grid=(nseq,),
         in_specs=[blk, blk, pl.BlockSpec(memory_space=pltpu.VMEM)] + [anyspec] * NW,
-        out_specs=[anyspec] * 2,
-        out_shape=[jax.ShapeDtypeStruct((2 * nseq, T, D), BF16), jax.ShapeDtypeStruct((2, GROWS, GL), F32)],
+        out_specs=[anyspec] * 6,
+        out_shape=[jax.ShapeDtypeStruct((2 * nseq, T, D), BF16), jax.ShapeDtypeStruct((2, 8, PR1, GL), F32)]
+                  + [jax.ShapeDtypeStruct((nseq * L, n, T), BF16) for n in (D, D, D, 1536)],
         scratch_shapes=[V((D, 1536), BF16), V((D, D), BF16), V((D, FF), BF16), V((FF, D), BF16),
                         V((1536, D), BF16), V((D, D), BF16), V((FF, D), BF16), V((D, FF), BF16),
-                        V((D, 1536), F32), V((D, D), F32), V((D, FF), F32), V((FF, D), F32),
+                        V((D, FF), F32), V((FF, D), F32),
                         V((L, D, T), BF16), V((L, 1536, T), BF16), V((L, D, T), BF16), V((L, D, T), BF16), V((L, D, T), BF16),
                         V((L, FF, T), BF16), V((L, H, T), F32), V((L, 2, T), F32), V((D, T), BF16), V((D, T), BF16), V((FF, T), BF16),
                         V((FF, T), BF16), V((D, T), BF16), V((D, T), BF16), V((D, T), BF16), V((1536, T), BF16), V((D, T), BF16),
                         V((2, T, T), F32), V((2, T, LN), F32), V((2, T, LN), F32), V((2, T, D), BF16),
-                        V((L, D, LN), F32), S((22,)), S((NW,)), S((NW,)), S((4, 13)), S((4, 13)), S((2,)), S((2,)), S((nseq,))],
+                        V((L, D, LN), F32), S((4,)), S((16,)), S((NW,)), S((NW,)), S((4, 13)), S((4, 13)), S((2,)), S((2,)), S((nseq,))],
         compiler_params=pltpu.CompilerParams(dimension_semantics=("arbitrary",), vmem_limit_bytes=67_000_000,
                                              collective_id=0, has_side_effects=True),
     )(x, cot, emb, *ws)
 
 
-NCOL = 3
-BR = 256
-GROWS = NCOL * 8 * BR
 ORDERS = ('xyz', 'yzx', 'zxy')
-SPREAD = ((0, 0, BR, 'xy'), (1, 0, BR, 'yx'), (2, 0, BR // 2, 'xy'), (2, BR // 2, BR // 2, 'yx'))
-
-
-def reduce_kernel(g_h, dx_in, out, dx, acc, rd, r1, r2, r3, locsem, ds, dr, ps, pr, gs, gr, cs, cr, xs_, xr_):
+SPREAD = ('xy', 'yx', None)
+CUTS = {PR1: ((0, 176), (176, 168), (344, 168)), PR2: ((0, 88), (88, 88), (176, 80))}
+NB = 12
+
+
+class Later:
+    def __init__(self, make):
+        self.make = make
+
+    def start(self):
+        self.make().start()
+
+    def wait(self):
+        self.make().wait()
+
+    def wait_recv(self):
+        self.make().wait_recv()
+
+    def wait_send(self):
+        self.make().wait_send()
+
+
+class Summed:
+    def __init__(self, pr, mine, other, load, out, rd, r1, r2, r3, sems, me, core, rdma):
+        self.pr, self.mine, self.other, self.load, self.out = pr, mine, other, load, out
+        self.rd, self.r1, self.r2, self.r3, self.me, self.core, self.rdma = rd, r1, r2, r3, me, core, rdma
+        self.ds, self.dr, self.ls, self.ps, self.prv, self.gs, self.gr, self.cs, self.cr = sems
+        self.sends, self.sib = [], []
+
+    def piece(self, far):
+        pos = {ax: (1 - v if ax in far else v) for ax, v in self.me.items()}
+        return (pos['z'] * 2 + pos['y']) * 2 + pos['x']
+
+    def kept(self, color):
+        a, b, c = ORDERS[color]
+        return [b + c, b, c, '']
+
+    def go(self, ends, d):
+        cp = self.rdma(ends, d)
+        cp.start()
+        self.sends.append(cp)
+        return cp
+
+    def rows(self, color):
+        return pl.ds(*CUTS[self.pr][color])
+
+    def add(self, dst, src, color):
+        r0, n = CUTS[self.pr][color]
+
+        def body(i, c):
+            r = pl.multiple_of(r0 + i * 8, 8)
+            dst[pl.ds(r, 8), :] += src[pl.ds(r, 8), :]
+            return c
+        lax.fori_loop(0, n // 8, body, 0, unroll=2)
+
+    def start(self):
+        self.d, self.l = {}, {}
+        i = 0
+        for first in (True, False):
+            for j in range(4):
+                for color in range(3):
+                    k = self.kept(color)[j]
+                    e = self.piece(ORDERS[color][0] + k if first else k)
+                    r = self.rows(color)
+                    self.d[first, j, color] = (e, self.go(
+                        lambda e=e, r=r, i=i: (self.other(e).at[r, :], self.rd.at[e, r, :], self.ds.at[i], self.dr.at[i]), 'c'))
+                    if self.load is not None:
+                        cp = Later(lambda e=e, r=r, i=i: pltpu.make_async_copy(self.load(e).at[r, :], self.mine(e).at[r, :], self.ls.at[i]))
+                        cp.start()
+                        self.l[first, j, color] = cp
+                    i += 1
+
+    def fold(self, first, j, color):
+        e, cp = self.d[first, j, color]
+        cp.wait_recv()
+        if self.load is not None:
+            self.l[first, j, color].wait()
+        self.add(self.mine(e), self.rd.at[e], color)
+        return e
+
+    def phase1(self):
+        self.p1, self.p2, self.p3 = {}, {}, {}
+        for j in range(4):
+            for color in range(3):
+                e, r, i = self.fold(True, j, color), self.rows(color), 3 * j + color
+                self.p1[j, color] = self.go(
+                    lambda e=e, r=r, i=i, j=j: (self.mine(e).at[r, :], self.r1.at[j, r, :], self.ps.at[i], self.prv.at[i]), ORDERS[color][0])
+
+    def fold_kept(self):
+        self.e = {(j, color): self.fold(False, j, color) for j in range(4) for color in range(3)}
+
+    def take1(self, j, color):
+        self.p1[j, color].wait_recv()
+        e = self.e[j, color]
+        self.add(self.mine(e), self.r1.at[j], color)
+        return e
+
+    def phase2(self):
+        for j in range(2):
+            for color in range(3):
+                e, r, i = self.take1(j, color), self.rows(color), 12 + 3 * j + color
+                self.p2[j, color] = self.go(
+                    lambda e=e, r=r, i=i, j=j: (self.mine(e).at[r, :], self.r2.at[j, r, :], self.ps.at[i], self.prv.at[i]), ORDERS[color][1])
+
+    def phase3(self):
+        for color in range(3):
+            e, r, i = self.take1(2, color), self.rows(color), 18 + color
+            self.p2[0, color].wait_recv()
+            self.add(self.mine(e), self.r2.at[0], color)
+            self.p3[color] = self.go(
+                lambda e=e, r=r, i=i: (self.mine(e).at[r, :], self.r3.at[r, :], self.ps.at[i], self.prv.at[i]), ORDERS[color][2])
+        for color in range(3):
+            e = self.take1(3, color)
+            self.p2[1, color].wait_recv()
+            self.add(self.mine(e), self.r2.at[1], color)
+
+    def at(self, far, r0, n):
+        y = 1 - self.me['y'] if 'y' in far else self.me['y']
+        x = 1 - self.me['x'] if 'x' in far else self.me['x']
+        return self.out.at[(y * 2 + x) * 2 + self.core, pl.ds(r0, n), :]
+
+    def parts(self):
+        out = []
+        for color, (r0, n) in enumerate(CUTS[self.pr]):
+            if SPREAD[color]:
+                out.append((color, r0, n, SPREAD[color]))
+            else:
+                h = n // 16 * 8
+                out += [(color, r0, h, 'xy'), (color, r0 + h, n - h, 'yx')]
+        return out
+
+    def sibling(self, far, r0, n, i):
+        cp = self.rdma(lambda: (self.at(far, r0, n), self.at(far, r0, n), self.cs.at[i], self.cr.at[i]), 'c')
+        cp.start()
+        self.sib.append(cp)
+
+    def hand(self, far, r0, n, i, d):
+        return self.go(lambda: (self.at(far, r0, n), self.at(far, r0, n), self.gs.at[i], self.gr.at[i]), d)
+
+    def spread(self):
+        self.g1, self.g2, self.g3 = {}, {}, {}
+        for color, (r0, n) in enumerate(CUTS[self.pr]):
+            self.p3[color].wait_recv()
+            m = self.mine(self.e[3, color])
+            o = self.out.at[(self.me['y'] * 2 + self.me['x']) * 2 + self.core]
+
+            def body(i, c, r0=r0, m=m, o=o):
+                r = pl.multiple_of(r0 + i * 8, 8)
+                o[pl.ds(r, 8), :] = m[pl.ds(r, 8), :] + self.r3[pl.ds(r, 8), :]
+                return c
+            lax.fori_loop(0, n // 8, body, 0, unroll=2)
+            for k, (col, q0, qn, ab) in enumerate(self.parts()):
+                if col == color:
+                    self.g1[k] = self.hand('', q0, qn, k, ab[0])
+                    self.g2[k] = self.hand('', q0, qn, 4 + k, ab[1])
+        for k, (col, r0, n, ab) in enumerate(self.parts()):
+            self.sibling('', r0, n, k)
+
+    def forward(self):
+        for k, (col, r0, n, ab) in enumerate(self.parts()):
+            self.g1[k].wait_recv()
+            self.g3[k] = self.hand(ab[0], r0, n, 8 + k, ab[1])
+            self.sibling(ab[0], r0, n, 4 + k)
+
+    def collect(self):
+        for k, (col, r0, n, ab) in enumerate(self.parts()):
+            self.g2[k].wait_recv()
+            self.sibling(ab[1], r0, n, 8 + k)
+        for k, (col, r0, n, ab) in enumerate(self.parts()):
+            self.g3[k].wait_recv()
+            self.sibling('xy', r0, n, 12 + k)
+
+    def finish(self):
+        for cp in self.sib:
+            cp.wait()
+        for cp in self.sends:
+            cp.wait_send()
+
+
+def reduce_kernel(g_h, dx_in, u_h, dmid_h, ctx_h, dqkv_h, out1, out2, dx, acc, full, ub, qb, cb, mb, ra, r1, r2, r3, rb, s1, s2, s3, bsem,
+                  ds1, dr1, ls1, ps1, pr1, gs1, gr1, cs1, cr1, ds2, dr2, ls2, ps2, pr2, gs2, gr2, cs2, cr2, xs_, xr_):
     mi = lax.axis_index('model')
     di = lax.axis_index('data')
     core, x, y = di % 2, (di // 2) % 2, di // 4
@@ -598,196 +775,161 @@
     dev = {'x': {'model': mi, 'data': di + 2 - 4 * x}, 'y': {'model': mi, 'data': di + 4 - 8 * y},
            'z': {'model': 1 - mi, 'data': di}, 'c': {'model': mi, 'data': di + 1 - 2 * core}}
 
-    def rdma(src, dst, s, r, d):
-        return pltpu.make_async_remote_copy(src, dst, s, r, device_id=dev[d], device_id_type=MESH_ID)
+    def rdma(ends, d):
+        return Later(lambda: pltpu.make_async_remote_copy(*ends(), device_id=dev[d], device_id_type=MESH_ID))
 
     barrier = pltpu.get_barrier_semaphore()
     for d in 'xyzc':
         pl.semaphore_signal(barrier, inc=1, device_id=dev[d], device_id_type=MESH_ID)
     pl.semaphore_wait(barrier, 4)
 
-    def blk(color, far):
-        pos = {ax: (1 - me[ax] if ax in far else me[ax]) for ax in 'xyz'}
-        return (pos['z'] * NCOL + color) * 4 + pos['y'] * 2 + pos['x']
-
-    def add(dst, src):
-        def body(i, c):
-            r = pl.multiple_of(i * 64, 64)
-            acc[dst, pl.ds(r, 64), :] += src[pl.ds(r, 64), :]
-            return c
-        lax.fori_loop(0, BR // 64, body, 0)
-
-    def places(color):
-        a, b, c = ORDERS[color]
-        keep = [b + c, b, c, '']
-        return [a + k for k in keep], keep
-
-    seq = ([blk(color, places(color)[0][j]) for j in range(4) for color in range(NCOL)]
-           + [blk(color, places(color)[1][j]) for j in range(4) for color in range(NCOL)])
-    nb = len(seq)
-    dcp, lcp = [], []
-    for i, b in enumerate(seq):
-        dcp.append(rdma(g_h.at[b * 2 + (1 - core)], rd.at[b], ds.at[i], dr.at[i], 'c'))
-        lcp.append(pltpu.make_async_copy(g_h.at[b * 2 + core], acc.at[b], locsem.at[i]))
-    for i in range(nb):
-        dcp[i].start()
-        lcp[i].start()
-
-    def fold_core(i):
-        dcp[i].wait_recv()
-        lcp[i].wait()
-        add(seq[i], rd.at[seq[i]])
-
-    p1, p2, p3 = {}, {}, {}
-    for j in range(4):
-        for color in range(NCOL):
-            i = j * NCOL + color
-            fold_core(i)
-            p1[j, color] = rdma(acc.at[seq[i]], r1.at[i], ps.at[i], pr.at[i], ORDERS[color][0])
-            p1[j, color].start()
-    base2, base3 = 4 * NCOL, 6 * NCOL
-
-    def fold_kept(j, color):
-        i = j * NCOL + color
-        fold_core(4 * NCOL + i)
-        p1[j, color].wait_recv()
-        add(seq[4 * NCOL + i], r1.at[i])
-        return seq[4 * NCOL + i]
-
-    for j in range(2):
-        for color in range(NCOL):
-            b = fold_kept(j, color)
-            i = j * NCOL + color
-            p2[j, color] = rdma(acc.at[b], r2.at[i], ps.at[base2 + i], pr.at[base2 + i], ORDERS[color][1])
-            p2[j, color].start()
-    for color in range(NCOL):
-        b = fold_kept(2, color)
-        p2[0, color].wait_recv()
-        add(b, r2.at[color])
-        p3[color] = rdma(acc.at[b], r3.at[color], ps.at[base3 + color], pr.at[base3 + color], ORDERS[color][2])
-        p3[color].start()
+    def g_at(e, c):
+        return g_h.at[e // 4, (e % 4) * 2 + c]
+
+    mlp = Summed(PR1, lambda e: acc.at[e], lambda e: g_at(e, 1 - core), lambda e: g_at(e, core), out1, ra, r1, r2, r3,
+                 (ds1, dr1, ls1, ps1, pr1, gs1, gr1, cs1, cr1), me, core, rdma)
+    att = Summed(PR2, lambda e: full.at[e * 2 + core], lambda e: full.at[e * 2 + 1 - core], None, out2, rb, s1, s2, s3,
+                 (ds2, dr2, ls2, ps2, pr2, gs2, gr2, cs2, cr2), me, core, rdma)
+
+    def fetch(i, slot):
+        two = pl.ds(2 * i, 2)
+        return [pltpu.make_async_copy(u_h.at[two], ub.at[slot], bsem.at[slot, 0]),
+                pltpu.make_async_copy(dqkv_h.at[two], qb.at[slot], bsem.at[slot, 1])]
+
+    def fetch_o(i, slot):
+        two = pl.ds(2 * i, 2)
+        return [pltpu.make_async_copy(ctx_h.at[two], cb.at[slot], bsem.at[2 + slot, 0]),
+                pltpu.make_async_copy(dmid_h.at[two], mb.at[slot], bsem.at[2 + slot, 1])]
+
+    def begin(cs):
+        for c in cs:
+            c.start()
+
+    def end(cs):
+        for c in cs:
+            c.wait()
+
+    mlp.start()
+    begin(fetch(0, 0))
+    begin(fetch_o(0, 0))
+    full[...] = jnp.zeros_like(full)
+
+    def loop(fetch_fn, products, hooks):
+        def body(i, carry):
+            slot = i % 2
+            end(fetch_fn(i, slot))
+
+            @pl.when(i < NB - 1)
+            def _():
+                begin(fetch_fn(i + 1, 1 - slot))
+
+            products(slot)
+            for at, hook in hooks.items():
+                pl.when(i == at)(hook)
+            return carry
+        lax.fori_loop(0, NB, body, 0)
+
+    def qkv_products(slot):
+        for j in range(6):
+            p = None
+            for k in range(2):
+                d = dot_nt(ub[slot, k], qb[slot, k, pl.ds(256 * j, 256), :])
+                p = d if p is None else p + d
+            t = (j // 3) * 8 + 2 * (j % 3)
+            full[t] += p[:256]
+            full[t + 1] += p[256:]
+
+    def o_products(slot):
+        for z in range(2):
+            for c in range(2):
+                p = None
+                for k in range(2):
+                    d = dot_nt(cb[slot, k, pl.ds(256 * z, 256), :], mb[slot, k, pl.ds(256 * c, 256), :])
+                    p = d if p is None else p + d
+                full[z * 8 + 6 + c] += p
+
     nseq = dx.shape[0] // 2
-    mine, theirs = dx.at[mi * nseq + nseq - 1], dx.at[(1 - mi) * nseq + nseq - 1]
-    dx_out = rdma(mine, mine, xs_.at[0], xr_.at[0], 'z')
+    mine_x, theirs_x = dx.at[mi * nseq + nseq - 1], dx.at[(1 - mi) * nseq + nseq - 1]
+    dx_out = rdma(lambda: (mine_x, mine_x, xs_.at[0], xr_.at[0]), 'z')
+
+    loop(fetch, qkv_products, {2: mlp.phase1, 4: mlp.fold_kept, 8: mlp.phase2})
+    loop(fetch_o, o_products, {6: mlp.phase3})
+    att.start()
     dx_out.start()
-    last = {}
-    for color in range(NCOL):
-        last[color] = fold_kept(3, color)
-        p2[1, color].wait_recv()
-        add(last[color], r2.at[NCOL + color])
-
-    def out_at(color, far, r0, n):
-        yy = 1 - y if 'y' in far else y
-        xx = 1 - x if 'x' in far else x
-        return out.at[(color * 4 + yy * 2 + xx) * 2 + core, pl.ds(r0, n), :]
-
-    ns_ = len(SPREAD)
-    cps, g1, g2, g3 = [], {}, {}, {}
-
-    def to_sibling(k, far, i):
-        color, r0, n, _ = SPREAD[k]
-        o = out_at(color, far, r0, n)
-        cp = rdma(o, o, cs.at[i], cr.at[i], 'c')
-        cp.start()
-        cps.append(cp)
-
-    for color in range(NCOL):
-        p3[color].wait_recv()
-        b = last[color]
-        o_blk = (color * 4 + y * 2 + x) * 2 + core
-
-        def body(i, c, b=b, o_blk=o_blk, color=color):
-            r = pl.multiple_of(i * 64, 64)
-            out[o_blk, pl.ds(r, 64), :] = acc[b, pl.ds(r, 64), :] + r3[color, pl.ds(r, 64), :]
-            return c
-        lax.fori_loop(0, BR // 64, body, 0)
-        for k, (col, r0, n, ab) in enumerate(SPREAD):
-            if col != color:
-                continue
-            o = out_at(color, '', r0, n)
-            g1[k] = rdma(o, o, gs.at[k], gr.at[k], ab[0])
-            g2[k] = rdma(o, o, gs.at[ns_ + k], gr.at[ns_ + k], ab[1])
-            g1[k].start()
-            g2[k].start()
-    for k in range(ns_):
-        to_sibling(k, '', k)
-    for k, (color, r0, n, ab) in enumerate(SPREAD):
-        g1[k].wait_recv()
-        o = out_at(color, ab[0], r0, n)
-        g3[k] = rdma(o, o, gs.at[2 * ns_ + k], gr.at[2 * ns_ + k], ab[1])
-        g3[k].start()
-        to_sibling(k, ab[0], ns_ + k)
-    for k, (color, r0, n, ab) in enumerate(SPREAD):
-        g2[k].wait_recv()
-        to_sibling(k, ab[1], 2 * ns_ + k)
-    for k, (color, r0, n, ab) in enumerate(SPREAD):
-        g3[k].wait_recv()
-        to_sibling(k, 'xy', 3 * ns_ + k)
-    for cp in cps:
-        cp.wait()
+    mlp.spread()
+    att.phase1()
+    att.fold_kept()
+    mlp.forward()
+    att.phase2()
+    mlp.collect()
+    att.phase3()
+    att.spread()
+    att.forward()
+    att.collect()
+    mlp.finish()
+    att.finish()
     dx_out.wait_send()
-    rdma(theirs, theirs, xs_.at[0], xr_.at[0], 'z').wait_recv()
-    for cp in dcp + list(p1.values()) + list(p2.values()) + list(p3.values()) + list(g1.values()) + list(g2.values()) + list(g3.values()):
-        cp.wait_send()
-
-
-def run_reduce(grad, dx):
-    nb = NCOL * 8
+    rdma(lambda: (theirs_x, theirs_x, xs_.at[0], xr_.at[0]), 'z').wait_recv()
+
+
+def run_reduce(grad, dx, u, dmid, ctx, dqkv):
     V = pltpu.VMEM
     S = pltpu.SemaphoreType.DMA
+    anyspec = pl.BlockSpec(memory_space=pl.ANY)
+    sems = [S((24,)), S((24,)), S((24,)), S((21,)), S((21,)), S((12,)), S((12,)), S((16,)), S((16,))]
     return pl.pallas_call(
         reduce_kernel,
-        in_specs=[pl.BlockSpec(memory_space=pl.ANY)] * 2,
-        out_specs=[pl.BlockSpec(memory_space=pltpu.VMEM), pl.BlockSpec(memory_space=pl.ANY)],
-        out_shape=[jax.ShapeDtypeStruct((nb, BR, GL), F32), jax.ShapeDtypeStruct(dx.shape, dx.dtype)],
-        scratch_shapes=[V((nb, BR, GL), F32), V((nb, BR, GL), F32), V((4 * NCOL, BR, GL), F32), V((2 * NCOL, BR, GL), F32), V((NCOL, BR, GL), F32),
-                        S((nb,)), S((nb,)), S((nb,)), S((7 * NCOL,)), S((7 * NCOL,)), S((12,)), S((12,)), S((16,)), S((16,)), S((1,)), S((1,))],
-        input_output_aliases={1: 1},
-        compiler_params=pltpu.CompilerParams(vmem_limit_bytes=60_000_000, collective_id=1, has_side_effects=True),
-    )(grad.reshape(2 * nb, BR, GL), dx)
-
-
-def place_kernel(g, o_q, o_k, o_v, o_o, o_1, o_2, sem):
+        in_specs=[anyspec] * 6,
+        out_specs=[pl.BlockSpec(memory_space=pltpu.VMEM)] * 2 + [anyspec],
+        out_shape=[jax.ShapeDtypeStruct((8, PR1, GL), F32), jax.ShapeDtypeStruct((8, PR2, GL), F32), jax.ShapeDtypeStruct(dx.shape, dx.dtype)],
+        scratch_shapes=[V((8, PR1, GL), F32), V((16, PR2, GL), F32),
+                        V((2, 2, D, T), BF16), V((2, 2, 1536, T), BF16), V((2, 2, D, T), BF16), V((2, 2, D, T), BF16),
+                        V((8, PR1, GL), F32), V((4, PR1, GL), F32), V((2, PR1, GL), F32), V((PR1, GL), F32),
+                        V((8, PR2, GL), F32), V((4, PR2, GL), F32), V((2, PR2, GL), F32), V((PR2, GL), F32), S((4, 2))]
+                       + sems + sems + [S((1,)), S((1,))],
+        input_output_aliases={1: 2},
+        compiler_params=pltpu.CompilerParams(vmem_limit_bytes=47_000_000, collective_id=1, has_side_effects=True),
+    )(grad, dx, u, dmid, ctx, dqkv)
+
+
+def place_kernel(a, b, o_q, o_k, o_v, o_o, o_1, o_2, sem):
     cps = []
 
-    def move(b, dst):
-        cps.append(pltpu.make_async_copy(g.at[b], dst, sem.at[b]))
+    def move(src, dst):
+        cps.append(pltpu.make_async_copy(src, dst, sem.at[len(cps)]))
         cps[-1].start()
 
+    for k in range(4):
+        move(a.at[k], o_1.at[:, pl.ds(256 * k, 256)])
+        move(a.at[4 + k], o_2.at[pl.ds(512 * (k % 2), 512), pl.ds(256 * (k // 2), 256)])
     for j, o in enumerate((o_q, o_k, o_v)):
         for i in range(2):
-            move(2 * j + i, o.at[pl.ds(256 * i, 256), :])
-    for k in range(4):
-        for i in range(2):
-            move(6 + 2 * k + i, o_1.at[pl.ds(256 * i, 256), pl.ds(256 * k, 256)])
+            move(b.at[2 * j + i], o.at[pl.ds(256 * i, 256), :])
     for k in range(2):
-        for i in range(4):
-            move(14 + 4 * k + i, o_2.at[pl.ds(256 * i, 256), pl.ds(256 * k, 256)])
-    for k in range(2):
-        move(22 + k, o_o.at[:, pl.ds(256 * k, 256)])
+        move(b.at[6 + k], o_o.at[:, pl.ds(256 * k, 256)])
     for c in cps:
         c.wait()
 
 
-def run_place(g):
+def run_place(a, b):
     shapes = [(512, 256)] * 3 + [(256, 512), (512, 1024), (1024, 512)]
     return pl.pallas_call(
         place_kernel,
-        in_specs=[pl.BlockSpec(memory_space=pltpu.VMEM)],
-        out_specs=[pl.BlockSpec(memory_space=pl.ANY)] * 6,
+        in_specs=[pl.BlockSpec(memory_space=pltpu.VMEM)] * 2,
+        out_specs=[pl.BlockSpec(memory_space=pltpu.HBM)] * 6,
         out_shape=[jax.ShapeDtypeStruct(s, F32) for s in shapes],
-        scratch_shapes=[pltpu.SemaphoreType.DMA((24,))],
-        compiler_params=pltpu.CompilerParams(vmem_limit_bytes=20_000_000),
-    )(g)
+        scratch_shapes=[pltpu.SemaphoreType.DMA((16,))],
+        compiler_params=pltpu.CompilerParams(vmem_limit_bytes=2_000_000),
+    )(a, b)
 
 
 def solution(mesh):
     spec_col, spec_row, spec_act, spec_rep = P(None, 'model'), P('model', None), P('data', None, None), P(None, None)
 
     def device_step(x_in, cot_out, step_emb, w_q, w_k, w_v, w_o, w_1, w_2):
-        dx, grad = run_kernel(x_in, cot_out, step_emb, (w_q, w_k, w_v, w_o, w_1, w_2), x_in.shape[0] // 2)
-        g, dx = run_reduce(grad, dx)
-        return (*run_place(g), dx)
+        dx, grad, *rest = run_kernel(x_in, cot_out, step_emb, (w_q, w_k, w_v, w_o, w_1, w_2), x_in.shape[0] // 2)
+        a, b, dx = run_reduce(grad, dx, *rest)
+        return (*run_place(a, b), dx)
 
     return jax.shard_map(device_step, mesh=mesh,
                          in_specs=(spec_act, spec_act, spec_rep, spec_col, spec_col, spec_col, spec_row, spec_col, spec_row),

time: 573 us -> 578 us (level)
  Pallas kernels: 565 us -> 573 us
    pallas_call x1, Pallas kernels: 77.4 us -> 98.2 us  [run_reduce(): pl.pallas_call(reduce_kernel, in_specs=[anyspec] * 6, out_specs=[pl.Block...]
    pallas_call x1, Pallas kernels: 484 us -> 471 us  [run_kernel(): pl.pallas_call(functools.partial(kernel, nseq), grid=(nseq,), in_specs=[b...]
where the time goes in v7:
time: 578 us
  Pallas kernels  573 us (99%)
    pallas_call x1, Pallas kernels, run_kernel(): pl.pallas_call(functools.partial(kernel, nseq), grid=(nseq,), in_specs=[b...  471 us
    pallas_call x1, Pallas kernels, run_reduce(): pl.pallas_call(reduce_kernel, in_specs=[anyspec] * 6, out_specs=[pl.Block...  98.2 us

profile of v7, /device:TPU:0, one launch (start us, length us, event | category | flops | bytes accessed | tf_op | source)
XLA Modules:
  0.0 577.8 jit_solution(17252570534867097759)
XLA Ops:
  0.6 471.3 %shard_map.144 = (bf16[12,512,512]{2,1,0:T(8,128)(2,1)}, f32[2,8,512,256]{3,2,1,0:T(8,128)}, bf16[24,512,512]{2,1,0:T(8,128)(2,1)}, bf16[24,512,512]{2,1,0:T(8,1...) custom-call(bf16[12,512,512]{2,1,0:T(8,128)(2,1)} %x_ref.1, bf16[12,512,512]{2,1,0:T(8,128)(2,1)} %cot_ref.1, ...), custom_call_target="tpu_custom_call" | custom-call | tf_op jit(solution)/shard_map/pallas_call | solution.py:569
  471.9 98.2 %shard_map.145 = (f32[8,512,256]{2,1,0:T(8,128)S(1)}, f32[8,256,256]{2,1,0:T(8,128)S(1)}, bf16[12,512,512]{2,1,0:T(8,128)(2,1)}) custom-call(f32[2,8,512,256]{3,2,1,0:T(8,128)} %get-tuple-element.22.g_h, bf16[12,512,512]{2,1,0:T(8,128)(2,1)} %get-tuple-element.23.dx_in, ...), custom_call_target="tpu_custom_call", output_to_operand_aliasing={{2}: (1, {})} | custom-call | tf_op jit(solution)/shard_map/pallas_call | solution.py:880
  570.1 0.0 copy-start
  570.1 3.3 shard_map.146
  573.4 1.7 copy-done
  575.1 2.7 copy.19
Async XLA Ops:
  570.1 5.0 copy-start

commit v8 on v7

--- a/solution.py
+++ b/solution.py
@@ -634,13 +634,8 @@
         return pl.ds(*CUTS[self.pr][color])
 
     def add(self, dst, src, color):
-        r0, n = CUTS[self.pr][color]
-
-        def body(i, c):
-            r = pl.multiple_of(r0 + i * 8, 8)
-            dst[pl.ds(r, 8), :] += src[pl.ds(r, 8), :]
-            return c
-        lax.fori_loop(0, n // 8, body, 0, unroll=2)
+        r = self.rows(color)
+        dst[r, :] += src[r, :]
 
     def start(self):
         self.d, self.l = {}, {}
@@ -730,14 +725,7 @@
         self.g1, self.g2, self.g3 = {}, {}, {}
         for color, (r0, n) in enumerate(CUTS[self.pr]):
             self.p3[color].wait_recv()
-            m = self.mine(self.e[3, color])
-            o = self.out.at[(self.me['y'] * 2 + self.me['x']) * 2 + self.core]
-
-            def body(i, c, r0=r0, m=m, o=o):
-                r = pl.multiple_of(r0 + i * 8, 8)
-                o[pl.ds(r, 8), :] = m[pl.ds(r, 8), :] + self.r3[pl.ds(r, 8), :]
-                return c
-            lax.fori_loop(0, n // 8, body, 0, unroll=2)
+            self.at('', r0, n)[...] = self.mine(self.e[3, color])[pl.ds(r0, n), :] + self.r3[pl.ds(r0, n), :]
             for k, (col, q0, qn, ab) in enumerate(self.parts()):
                 if col == color:
                     self.g1[k] = self.hand('', q0, qn, k, ab[0])
@@ -798,8 +786,8 @@
 
     def fetch_o(i, slot):
         two = pl.ds(2 * i, 2)
-        return [pltpu.make_async_copy(ctx_h.at[two], cb.at[slot], bsem.at[2 + slot, 0]),
-                pltpu.make_async_copy(dmid_h.at[two], mb.at[slot], bsem.at[2 + slot, 1])]
+        return [pltpu.make_async_copy(ctx_h.at[two], cb.at[slot], bsem.at[3 + slot, 0]),
+                pltpu.make_async_copy(dmid_h.at[two], mb.at[slot], bsem.at[3 + slot, 1])]
 
     def begin(cs):
         for c in cs:
@@ -810,18 +798,20 @@
             c.wait()
 
     mlp.start()
-    begin(fetch(0, 0))
-    begin(fetch_o(0, 0))
+    for i in range(2):
+        begin(fetch(i, i))
+    for i in range(2):
+        begin(fetch_o(i, i))
     full[...] = jnp.zeros_like(full)
 
     def loop(fetch_fn, products, hooks):
         def body(i, carry):
-            slot = i % 2
+            slot = i % 3
             end(fetch_fn(i, slot))
 
-            @pl.when(i < NB - 1)
+            @pl.when(i < NB - 2)
             def _():
-                begin(fetch_fn(i + 1, 1 - slot))
+                begin(fetch_fn(i + 2, (i + 2) % 3))
 
             products(slot)
             for at, hook in hooks.items():
@@ -883,9 +873,9 @@
         out_specs=[pl.BlockSpec(memory_space=pltpu.VMEM)] * 2 + [anyspec],
         out_shape=[jax.ShapeDtypeStruct((8, PR1, GL), F32), jax.ShapeDtypeStruct((8, PR2, GL), F32), jax.ShapeDtypeStruct(dx.shape, dx.dtype)],
         scratch_shapes=[V((8, PR1, GL), F32), V((16, PR2, GL), F32),
-                        V((2, 2, D, T), BF16), V((2, 2, 1536, T), BF16), V((2, 2, D, T), BF16), V((2, 2, D, T), BF16),
+                        V((3, 2, D, T), BF16), V((3, 2, 1536, T), BF16), V((3, 2, D, T), BF16), V((3, 2, D, T), BF16),
                         V((8, PR1, GL), F32), V((4, PR1, GL), F32), V((2, PR1, GL), F32), V((PR1, GL), F32),
-                        V((8, PR2, GL), F32), V((4, PR2, GL), F32), V((2, PR2, GL), F32), V((PR2, GL), F32), S((4, 2))]
+                        V((8, PR2, GL), F32), V((4, PR2, GL), F32), V((2, PR2, GL), F32), V((PR2, GL), F32), S((6, 2))]
                        + sems + sems + [S((1,)), S((1,))],
         input_output_aliases={1: 2},
         compiler_params=pltpu.CompilerParams(vmem_limit_bytes=47_000_000, collective_id=1, has_side_effects=True),

time: 578 us -> 566 us (0.979)
  Pallas kernels: 573 us -> 560 us
    pallas_call x1, Pallas kernels: 98.2 us -> 85.8 us  [run_reduce(): pl.pallas_call(reduce_kernel, in_specs=[anyspec] * 6, out_specs=[pl.Block...]
where the time goes in v8:
time: 566 us; the launch traced here: 565 us
  Pallas kernels  560 us (99%)
    pallas_call x1, Pallas kernels, run_kernel(): pl.pallas_call(functools.partial(kernel, nseq), grid=(nseq,), in_specs=[b...  471 us
    pallas_call x1, Pallas kernels, run_reduce(): pl.pallas_call(reduce_kernel, in_specs=[anyspec] * 6, out_specs=[pl.Block...  85.8 us

profile of v8, /device:TPU:0, one launch (start us, length us, event | category | flops | bytes accessed | tf_op | source)
XLA Modules:
  0.0 565.4 jit_solution(8689351021964606018)
XLA Ops:
  0.6 471.3 %shard_map.144 = (bf16[12,512,512]{2,1,0:T(8,128)(2,1)}, f32[2,8,512,256]{3,2,1,0:T(8,128)}, bf16[24,512,512]{2,1,0:T(8,128)(2,1)}, bf16[24,512,512]{2,1,0:T(8,1...) custom-call(bf16[12,512,512]{2,1,0:T(8,128)(2,1)} %x_ref.1, bf16[12,512,512]{2,1,0:T(8,128)(2,1)} %cot_ref.1, ...), custom_call_target="tpu_custom_call" | custom-call | tf_op jit(solution)/shard_map/pallas_call | solution.py:569
  471.9 85.8 %shard_map.145 = (f32[8,512,256]{2,1,0:T(8,128)S(1)}, f32[8,256,256]{2,1,0:T(8,128)S(1)}, bf16[12,512,512]{2,1,0:T(8,128)(2,1)}) custom-call(f32[2,8,512,256]{3,2,1,0:T(8,128)} %get-tuple-element.22.g_h, bf16[12,512,512]{2,1,0:T(8,128)(2,1)} %get-tuple-element.23.dx_in, ...), custom_call_target="tpu_custom_call", output_to_operand_aliasing={{2}: (1, {})} | custom-call | tf_op jit(solution)/shard_map/pallas_call | solution.py:870
  557.7 0.0 copy-start
  557.8 3.3 shard_map.146
  561.0 1.7 copy-done
  562.7 2.7 copy.19
Async XLA Ops:
  557.7 5.0 copy-start

commit v9 on v8

--- a/solution.py
+++ b/solution.py
@@ -106,7 +106,7 @@
 def kernel(nseq, x_ref, cot_ref, emb_ref, wq_h, wk_h, wv_h, wo_h, w1_h, w2_h,
            dx_h, grad_h, u_h, dmid_h, ctx_h, dqkv_h,
            wqkv, wo, w1, w2, wqkvt, wot, w1t, w2t, g1, g2,
-           xs, qkv, ctx, ctxl, hs, zs, lse, rsc, u, m, act, dz, dn, dmid, dctx, dqkv, tmp, sbuf, lcol, dcol, dxs,
+           xs, qkv, ctx, ctxl, hs, zs, lse, rsc, us, ms, act, dz, dn, dmid2, dctx, dqkv2, tmp, sbuf, lcol, dcol, dxs,
            embv, ssem, sem, zsend, zrecv, gsend, grecv, xloc, xsend, xrecv):
     step = pl.program_id(0)
     mi = lax.axis_index('model')
@@ -143,6 +143,17 @@
             return wqkv.at[pl.ds(r0, n), pl.ds(768 * (1 - mi), 768)]
         return place(k, 1 - mi, r0, n)
 
+    def turn(m_):
+        for j in range(3):
+            c = pl.ds(pl.multiple_of(768 * m_ + 256 * j, 256), 256)
+            wqkvt[c, :] = wqkv[:, c].T
+        c = pl.ds(pl.multiple_of(256 * m_, 256), 256)
+        wot[:, c] = wo[c, :].T
+        for j in range(2):
+            c = pl.ds(pl.multiple_of(1024 * m_ + 512 * j, 512), 512)
+            w1t[c, :] = w1[:, c].T
+            w2t[:, c] = w2[c, :].T
+
     def load_weights():
         barrier = pltpu.get_barrier_semaphore()
         for d in 'xyzc':
@@ -187,6 +198,11 @@
                 plane[g, color, 2].wait_recv()
                 sib.append(hand(g, 'xy', color, 'c', 9 + 3 * color))
 
+        for cp in local:
+            cp.wait()
+        turn(mi)
+        for l_ in range(L):
+            embv[l_] = jnp.broadcast_to(emb_ref[l_:l_ + 1, :].astype(F32), (LN, D)).T
         own(0)
         own(1)
         own(2)
@@ -200,7 +216,6 @@
         finish(2)
         finish(3)
         for k in range(NW):
-            local[k].wait()
             zc[k].wait_send()
         for cp in plane.values():
             cp.wait_send()
@@ -210,20 +225,13 @@
     @pl.when(step == 0)
     def _():
         load_weights()
-        for l_ in range(L):
-            embv[l_] = jnp.broadcast_to(emb_ref[l_:l_ + 1, :].astype(F32), (LN, D)).T
-        for j in range(3):
-            wqkvt[pl.ds(512 * j, 512), :] = wqkv[:, pl.ds(512 * j, 512)].T
-        wot[...] = wo[...].T
-        for j in range(4):
-            w1t[pl.ds(512 * j, 512), :] = w1[:, pl.ds(512 * j, 512)].T
-            w2t[:, pl.ds(512 * j, 512)] = w2[pl.ds(512 * j, 512), :].T
+        turn(1 - mi)
         g1[...] = jnp.zeros_like(g1)
         g2[...] = jnp.zeros_like(g2)
 
-    def stash(k, names):
-        pairs = dict(ctx=(ctx.at[k % L], ctx_h), u=(u, u_h), dmid=(dmid, dmid_h), dqkv=(dqkv, dqkv_h))
-        return [pltpu.make_async_copy(pairs[n][0], pairs[n][1].at[k], ssem.at[list(pairs).index(n)]) for n in names]
+    def stash(k, names, at=0):
+        pairs = dict(ctx=(ctx.at[k % L], ctx_h), u=(us.at[k % L], u_h), dmid=(dmid2.at[at], dmid_h), dqkv=(dqkv2.at[at], dqkv_h))
+        return [pltpu.make_async_copy(pairs[n][0], pairs[n][1].at[k], ssem.at[at, list(pairs).index(n)]) for n in names]
 
     def start_all(cs):
         for c in cs:
@@ -235,7 +243,8 @@
 
     @pl.when(step == 0)
     def _():
-        start_all(stash(L - 1, ('u', 'dmid', 'dqkv')))
+        start_all(stash(L - 1, ('dmid', 'dqkv'), 0))
+        start_all(stash(L - 2, ('dmid', 'dqkv'), 1))
 
     xs[0] = x_ref[0].T
     half = [pl.ds(0, 256), pl.ds(256, 256)]
@@ -287,9 +296,9 @@
 
     def fwd(l, carry):
         for c in range(2):
-            run(norm_into(tmp, s_tile(l, half[c]), l, 0, True, half[c]))
+            run(norm_into(us.at[l], s_tile(l, half[c]), l, 0, True, half[c]))
         for j in range(3):
-            qkv[l, pl.ds(512 * j, 512), :] = dot_nn(wqkvt[pl.ds(512 * j, 512), :], tmp[...]).astype(BF16)
+            qkv[l, pl.ds(512 * j, 512), :] = dot_nn(wqkvt[pl.ds(512 * j, 512), :], us[l]).astype(BF16)
 
         kps = {}
         inv = {}
@@ -348,12 +357,12 @@
                 sx = xs[l, rows(r), half[c]].astype(F32) + jnp.concatenate([embv[l, rows(r), :]] * 2, axis=1)
                 hs[l, rows(r), half[c]] = (sx + o[r:r + R]).astype(BF16)
         for c in range(2):
-            run(norm_into(m, h_tile(l, half[c]), l, 1, True, half[c]))
+            run(norm_into(ms.at[l], h_tile(l, half[c]), l, 1, True, half[c]))
 
         def z_dot(j):
             def f(c):
                 js = pl.ds(512 * j, 512)
-                zs[l, js, half[c]] = dot_nn(w1t[js, :], m[:, half[c]]).astype(BF16)
+                zs[l, js, half[c]] = dot_nn(w1t[js, :], ms[l, :, half[c]]).astype(BF16)
             return [lambda: f(0), lambda: f(1)]
 
         def gelu_stream(j):
@@ -375,16 +384,18 @@
         def _():
             for j in range(4):
                 run(z_dot(j))
+                dn[:, pl.ds(128 * j, 128)] = cot_ref[0, pl.ds(128 * j, 128), :].T
         return carry
 
     lax.fori_loop(0, L, fwd, 0)
 
-    dn[...] = cot_ref[0].T
 
     def bwd(i, carry):
         l = L - 1 - i
         k = step * L + l
-        start_all(stash(k, ('ctx',)))
+        dmid, dqkv = dmid2.at[i % 2], dqkv2.at[i % 2]
+        wait_all(stash(k, ('dmid', 'dqkv'), i % 2))
+        start_all(stash(k, ('ctx', 'u')))
 
         def dg_dot(j):
             def f(c):
@@ -407,10 +418,10 @@
 
             def b(c):
                 jc = pl.ds(512 * j + 256 * c, 256)
-                g1[:, jc] += dot_nt(m[...], dz[jc, :])
+                g1[:, jc] += dot_nt(ms[l], dz[jc, :])
             return [lambda: a(0), lambda: a(1), lambda: b(0), lambda: b(1)]
 
-        weave(dg_dot(0), norm_into(m, h_tile(l, half[0]), l, 1, False, half[0]) + norm_into(m, h_tile(l, half[1]), l, 1, False, half[1]))
+        run(dg_dot(0))
         def dm_part(k0, k1, last):
             def f(c):
                 p = dot_nn(w1[:, 512 * k0:512 * k1], dz[pl.ds(512 * k0, 512 * (k1 - k0)), half[c]])
@@ -427,7 +438,6 @@
         weave(wgrad(1) + dm_part(0, 2, False), gelu_stream(2))
         weave(wgrad(2), gelu_stream(3))
         run(dm_part(2, 4, True))
-        wait_all(stash(k, ('ctx', 'u', 'dmid', 'dqkv')))
         weave(wgrad(3), pull_into(dmid, dn, h_tile, tmp, l, 1))
         for c in range(2):
             dctx[:, half[c]] = dot_nn(wo[...], dmid[:, half[c]]).astype(BF16)
@@ -499,20 +509,18 @@
 
             return [functools.partial(f, c) for f in (f_v, f_k, f_q) for c in range(2)]
 
-        u_norm = sum([norm_into(u, s_tile(l, cc), l, 0, False, cc) for cc in half], [])
         run(stage_a(0))
         for hd in range(H + 1):
             ma = stage_a(hd + 1) if hd + 1 < H else []
             mc = stage_c(hd - 1) if hd >= 1 else []
             va = stage_b(hd) if hd < H else []
-            if hd == H - 1:
-                va = va + u_norm
             weave(merge(mc, ma), va)
 
         for c in range(2):
             tmp[:, half[c]] = dot_nn(wqkv[...], dqkv[:, half[c]]).astype(BF16)
         weave([], pull_into(dn, dmid, s_tile, tmp, l, 0))
-        start_all(stash(k, ('u', 'dmid', 'dqkv')))
+        wait_all(stash(k, ('ctx', 'u')))
+        start_all(stash(k, ('dmid', 'dqkv'), i % 2))
         return carry
 
     lax.fori_loop(0, L, bwd, 0)
@@ -542,7 +550,8 @@
 
     @pl.when(step == nseq - 1)
     def _():
-        wait_all(stash(0, ('u', 'dmid', 'dqkv')))
+        for at in range(2):
+            wait_all(stash(0, ('dmid', 'dqkv'), at))
         cps = []
         for m_ in range(2):
             for k in range(4):
@@ -577,10 +586,10 @@
                         V((1536, D), BF16), V((D, D), BF16), V((FF, D), BF16), V((D, FF), BF16),
                         V((D, FF), F32), V((FF, D), F32),
                         V((L, D, T), BF16), V((L, 1536, T), BF16), V((L, D, T), BF16), V((L, D, T), BF16), V((L, D, T), BF16),
-                        V((L, FF, T), BF16), V((L, H, T), F32), V((L, 2, T), F32), V((D, T), BF16), V((D, T), BF16), V((FF, T), BF16),
-                        V((FF, T), BF16), V((D, T), BF16), V((D, T), BF16), V((D, T), BF16), V((1536, T), BF16), V((D, T), BF16),
+                        V((L, FF, T), BF16), V((L, H, T), F32), V((L, 2, T), F32), V((L, D, T), BF16), V((L, D, T), BF16), V((FF, T), BF16),
+                        V((FF, T), BF16), V((D, T), BF16), V((2, D, T), BF16), V((D, T), BF16), V((2, 1536, T), BF16), V((D, T), BF16),
                         V((2, T, T), F32), V((2, T, LN), F32), V((2, T, LN), F32), V((2, T, D), BF16),
-                        V((L, D, LN), F32), S((4,)), S((16,)), S((NW,)), S((NW,)), S((4, 13)), S((4, 13)), S((2,)), S((2,)), S((nseq,))],
+                        V((L, D, LN), F32), S((2, 4)), S((16,)), S((NW,)), S((NW,)), S((4, 13)), S((4, 13)), S((2,)), S((2,)), S((nseq,))],
         compiler_params=pltpu.CompilerParams(dimension_semantics=("arbitrary",), vmem_limit_bytes=67_000_000,
                                              collective_id=0, has_side_effects=True),
     )(x, cot, emb, *ws)

time: 566 us -> 559 us (0.988)
  Pallas kernels: 560 us -> 554 us
    pallas_call x1, Pallas kernels: 471 us -> 465 us  [run_kernel(): pl.pallas_call(functools.partial(kernel, nseq), grid=(nseq,), in_specs=[b...]
where the time goes in v9:
time: 559 us
  Pallas kernels  554 us (99%)
    pallas_call x1, Pallas kernels, run_kernel(): pl.pallas_call(functools.partial(kernel, nseq), grid=(nseq,), in_specs=[b...  465 us
    pallas_call x1, Pallas kernels, run_reduce(): pl.pallas_call(reduce_kernel, in_specs=[anyspec] * 6, out_specs=[pl.Block...  85.9 us

profile of v9, /device:TPU:0, one launch (start us, length us, event | category | flops | bytes accessed | tf_op | source)
XLA Modules:
  0.0 559.2 jit_solution(9969421425238429071)
XLA Ops:
  0.6 465.0 %shard_map.144 = (bf16[12,512,512]{2,1,0:T(8,128)(2,1)}, f32[2,8,512,256]{3,2,1,0:T(8,128)}, bf16[24,512,512]{2,1,0:T(8,128)(2,1)}, bf16[24,512,512]{2,1,0:T(8,1...) custom-call(bf16[12,512,512]{2,1,0:T(8,128)(2,1)} %x_ref.1, bf16[12,512,512]{2,1,0:T(8,128)(2,1)} %cot_ref.1, ...), custom_call_target="tpu_custom_call" | custom-call | tf_op jit(solution)/shard_map/pallas_call | solution.py:578
  465.6 85.9 %shard_map.145 = (f32[8,512,256]{2,1,0:T(8,128)S(1)}, f32[8,256,256]{2,1,0:T(8,128)S(1)}, bf16[12,512,512]{2,1,0:T(8,128)(2,1)}) custom-call(f32[2,8,512,256]{3,2,1,0:T(8,128)} %get-tuple-element.22.g_h, bf16[12,512,512]{2,1,0:T(8,128)(2,1)} %get-tuple-element.23.dx_in, ...), custom_call_target="tpu_custom_call", output_to_operand_aliasing={{2}: (1, {})} | custom-call | tf_op jit(solution)/shard_map/pallas_call | solution.py:879
  551.5 0.0 copy-start
  551.5 3.3 shard_map.146
  554.8 1.7 copy-done
  556.5 2.7 copy.19
Async XLA Ops:
  551.5 5.0 copy-start

commit v10 on v9

--- a/solution.py
+++ b/solution.py
@@ -67,8 +67,8 @@
 def gelu_both(z):
     z2 = z * z
     s = jax.nn.sigmoid(z * (2 * GK0 + (2 * GK0 * GK1) * z2))
-    w = z * (2 * GK0 + (6 * GK0 * GK1) * z2)
-    return z * s, s * (1.0 + w * (1.0 - s))
+    g = z * s
+    return g, s + (g * (1.0 - s)) * (2 * GK0 + (6 * GK0 * GK1) * z2)
 
 
 def qrow(hd):
@@ -321,14 +321,14 @@
 
             def group(g):
                 cols = half[g]
-                mx = max_cols(sref, cols) * CEXP
+                mx = max_cols(sref, cols)
                 accs = [None, None]
                 for i, r in enumerate(range(0, T, 64)):
-                    e = jnp.exp2(sref[rows(r, 64), cols] * CEXP - mx)
+                    e = jnp.exp2((sref[rows(r, 64), cols] - mx) * CEXP)
                     accs[i % 2] = e if accs[i % 2] is None else accs[i % 2] + e
                     eref[rows(r, 64), cols] = e.astype(BF16)
                 sm = jnp.sum(accs[0] + accs[1], axis=0, keepdims=True)
-                lse[l, pl.ds(hd, 1), cols] = mx + jnp.log2(sm)
+                lse[l, pl.ds(hd, 1), cols] = mx + jnp.log2(sm) * (1.0 / CEXP)
                 inv[hd, g] = 1.0 / sm
 
             return [functools.partial(group, g) for g in range(2)]
@@ -483,7 +483,7 @@
                 for r in range(r0, r0 + 64, 64):
                     lc = lcol[hd % 2, rows(r, 64), :]
                     dc = dcol[hd % 2, rows(r, 64), :]
-                    pr = jnp.exp2(sbuf[hd % 2, rows(r, 64), cols] * CEXP - jnp.concatenate([lc, lc], axis=1))
+                    pr = jnp.exp2((sbuf[hd % 2, rows(r, 64), cols] - jnp.concatenate([lc, lc], axis=1)) * CEXP)
                     act[rows(sl + r, 64), cols] = pr.astype(BF16)
                     dp = dz[rows(sl + r, 64), cols].astype(F32)
                     act[rows(1024 + sl + r, 64), cols] = (pr * (dp - jnp.concatenate([dc, dc], axis=1))).astype(BF16)

time: 559 us -> 552 us (0.987)
  Pallas kernels: 554 us -> 547 us
    pallas_call x1, Pallas kernels: 465 us -> 457 us  [run_kernel(): pl.pallas_call(functools.partial(kernel, nseq), grid=(nseq,), in_specs=[b...]
where the time goes in v10:
time: 552 us
  Pallas kernels  547 us (99%)
    pallas_call x1, Pallas kernels, run_kernel(): pl.pallas_call(functools.partial(kernel, nseq), grid=(nseq,), in_specs=[b...  457 us
    pallas_call x1, Pallas kernels, run_reduce(): pl.pallas_call(reduce_kernel, in_specs=[anyspec] * 6, out_specs=[pl.Block...  85.9 us

profile of v10, /device:TPU:0, one launch (start us, length us, event | category | flops | bytes accessed | tf_op | source)
XLA Modules:
  0.0 551.7 jit_solution(7605048124069606372)
XLA Ops:
  0.6 457.5 %shard_map.144 = (bf16[12,512,512]{2,1,0:T(8,128)(2,1)}, f32[2,8,512,256]{3,2,1,0:T(8,128)}, bf16[24,512,512]{2,1,0:T(8,128)(2,1)}, bf16[24,512,512]{2,1,0:T(8,1...) custom-call(bf16[12,512,512]{2,1,0:T(8,128)(2,1)} %x_ref.1, bf16[12,512,512]{2,1,0:T(8,128)(2,1)} %cot_ref.1, ...), custom_call_target="tpu_custom_call" | custom-call | tf_op jit(solution)/shard_map/pallas_call | solution.py:578
  458.1 85.9 %shard_map.145 = (f32[8,512,256]{2,1,0:T(8,128)S(1)}, f32[8,256,256]{2,1,0:T(8,128)S(1)}, bf16[12,512,512]{2,1,0:T(8,128)(2,1)}) custom-call(f32[2,8,512,256]{3,2,1,0:T(8,128)} %get-tuple-element.22.g_h, bf16[12,512,512]{2,1,0:T(8,128)(2,1)} %get-tuple-element.23.dx_in, ...), custom_call_target="tpu_custom_call", output_to_operand_aliasing={{2}: (1, {})} | custom-call | tf_op jit(solution)/shard_map/pallas_call | solution.py:879
  544.0 0.0 copy-start
  544.0 3.3 shard_map.146
  547.3 1.7 copy-done
  549.0 2.7 copy.19
Async XLA Ops:
  544.0 5.0 copy-start
